TPU v7x, 256 devices: a whole 4x4x8 slice. The times are simulated.
256 devices in a mesh: dp: 8 (over x, y_lo), tp: 32 (over y_hi, z, core).
Axes of the slice: x: 4, y: 4 (y_hi: 2, y_lo: 2; y = y_hi * 2 + y_lo), z: 8, core: 2. Of those that a mesh axis runs over, the one named last changes fastest.
Arguments:
- proj_in: bfloat16 [1, 32768, 8192], P(None, 'dp', 'tp'), may hold values from -6 to 6
- kv_grad: bfloat16 [1, 32768, 2048], P(None, ('dp', 'tp')), may hold values from -0.75 to 0.75
- normed: bfloat16 [1, 32768, 8192], P(None, ('dp', 'tp')), may hold values from -6 to 6
- norm_grad: bfloat16 [1, 32768, 8192], P(None, ('dp', 'tp')), may hold values from -0.6 to 0.6
- first_moment: float32 [1, 8192, 2048], P(None, 'tp', 'dp'), may hold values from -0.6 to 0.6
- second_moment: float32 [1, 8192, 2048], P(None, 'tp', 'dp'), may hold values from 0.002 to 0.02
Outputs:
- new_first: float32 [1, 8192, 2048], P(None, 'tp', 'dp')
- new_second: float32 [1, 8192, 2048], P(None, 'tp', 'dp')
- adam_step: float32 [1, 8192, 2048], P(None, 'tp', 'dp')
- gain_grad: float32 [1, 8192], replicated
All inputs are finite; a program needn't handle non-finite values.
Results may differ from a plain program's by a relative error of at most 0.0003.
Values may be sent and summed in bfloat16 or wider, within the bound.
No kernel may reach another device: no remote copies, remote signals or barrier semaphores. Data moves between devices by JAX's collectives and lax.ppermute only.
A program may use at most 128 MiB of HBM per device.

v0:
```python
import functools

import jax
import jax.numpy as jnp
from jax import lax
from jax.sharding import Mesh
from jax.sharding import PartitionSpec as P

DP = ("dp_0", "dp_1")
DP_TP = ("dp_0", "dp_1", "tp_0", "tp_1", "tp_2")
TP = ("tp_0", "tp_1", "tp_2")


beta_one = 0.9
beta_two = 0.95
correct_one = 0.19
correct_two = 0.0975
epsilon = 1e-08


def over_axes(array, axes):
    return functools.reduce(lax.psum, axes, array)


def in_blocks(array, dim, size):
    lengths = array.shape
    pieces = array.reshape(*lengths[:dim], size, lengths[dim] // size, *lengths[dim + 1 :])
    return jnp.moveaxis(pieces, dim, 0)


def sent_and_summed(array, axis, dim):
    pieces = in_blocks(array, dim, lax.axis_size(axis))
    arrived = lax.all_to_all(pieces, axis, split_axis=0, concat_axis=0, tiled=True)
    return arrived.sum(axis=0)


def adam_update(mean_grad, first_old, second_old):
    new_first = beta_one * first_old + (1.0 - beta_one) * mean_grad
    new_second = beta_two * second_old + (1.0 - beta_two) * mean_grad * mean_grad
    update = new_first / correct_one / (jnp.sqrt(new_second / correct_two) + epsilon)
    return (new_first, new_second, update)


def row_adder(inputs, arrived):
    return lax.dot_general(
        inputs, arrived, (((0,), (0,)), ((), ())), preferred_element_type=jnp.float32
    )


def shards(proj_in, kv_grad, normed, norm_grad, first_moment, second_moment):
    replicas = lax.axis_size(DP)
    local_terms = jnp.sum(norm_grad.astype(jnp.float32) * normed.astype(jnp.float32), axis=1)
    gain_grad = over_axes(local_terms, DP_TP) / replicas
    inputs = proj_in[0]
    grad_rows = kv_grad[0]
    local_grad = row_adder(inputs, lax.all_gather(grad_rows, TP, axis=0, tiled=True))
    mean_grad = sent_and_summed(local_grad, DP, 1) / replicas
    new_first, new_second, update = adam_update(mean_grad, first_moment[0], second_moment[0])
    firsts = [new_first]
    seconds = [new_second]
    updates = [update]
    return (jnp.stack(firsts), jnp.stack(seconds), jnp.stack(updates), gain_grad)


def solution(mesh):
    finer = Mesh(mesh.devices.reshape(4, 2, 2, 8, 2), ("dp_0", "dp_1", "tp_0", "tp_1", "tp_2"))
    return jax.shard_map(
        shards,
        mesh=finer,
        in_specs=(
            P(None, DP, TP),
            P(None, DP_TP, None),
            P(None, DP_TP, None),
            P(None, DP_TP, None),
            P(None, TP, DP),
            P(None, TP, DP),
        ),
        out_specs=(P(None, TP, DP), P(None, TP, DP), P(None, TP, DP), P()),
        check_vma=False,
    )
```

profile of v0, /device:TPU:1, one launch (start us, length us, event | category | flops | bytes accessed | tf_op | source)
XLA Modules:
  0.0 229.3 jit_solution(13198261550055182338)
XLA Ops:
  7.2 0.0 copy-start
  7.2 0.0 all-gather.3.cloned.1.call-start
  7.2 0.7 all-gather.3.cloned.1.call-update
  7.9 2.8 %multiply_reduce_fusion = f32[8192]{0:T(1024)S(1)} fusion(bf16[1,128,8192]{2,1,0:T(8,128)(2,1)} %param.8, bf16[1,128,8192]{2,1,0:T(8,128)(2,1)} %param.9), kind=kLoop, calls=%fused_computation | loop fusion | flops 4186112 | bytes 4227072 | tf_op jit(solution)/shard_map/reduce_sum | solution.py:52
  10.7 14.3 %psum.35 = f32[1,8192]{1,0:T(1,128)S(1)} all-reduce(f32[1,8192]{1,0:T(1,128)S(1)} %bitcast.23), channel_id=1, replica_groups=mesh['dp_0'=4,'dp_1'=2,'tp_0'=2,'tp_1'=8,'tp_2'=2] {'dp_0'}, use_global_device_ids=true, to_apply=%region_2.0 | all-reduce | flops 8192 | bytes 65536 | tf_op jit(solution)/shard_map/psum | solution.py:22
  25.1 7.0 %psum.36 = f32[1,8192]{1,0:T(1,128)S(1)} all-reduce(f32[1,8192]{1,0:T(1,128)S(1)} %psum.35), channel_id=1, replica_groups=mesh['dp_0'=4,'dp_1'=2,'tp_0'=2,'tp_1'=8,'tp_2'=2] {'dp_1'}, use_global_device_ids=true, to_apply=%region_3.0 | all-reduce | flops 8192 | bytes 65536 | tf_op jit(solution)/shard_map/psum | solution.py:22
  32.1 9.2 %psum.37 = f32[1,8192]{1,0:T(1,128)S(1)} all-reduce(f32[1,8192]{1,0:T(1,128)S(1)} %psum.36), channel_id=1, replica_groups=mesh['dp_0'=4,'dp_1'=2,'tp_0'=2,'tp_1'=8,'tp_2'=2] {'tp_0'}, use_global_device_ids=true, to_apply=%region_4.0 | all-reduce | flops 8192 | bytes 65536 | tf_op jit(solution)/shard_map/psum | solution.py:22
  41.3 111.2 %all-gather.3.cloned.1.call-done = bf16[1,4096,2048]{2,1,0:T(8,128)(2,1)} async-done(((bf16[1,128,2048]{2,1,0:T(8,128)(2,1)}), bf16[1,4096,2048]{2,1,0:T(8,128)(2,1)}) %all-gather.3.cloned.1.call-update) | async-done | bytes 16777232 | tf_op jit(solution)/shard_map/all_gather | solution.py:56
  152.5 20.7 %copy.10 = bf16[2048,4096]{1,0:T(8,128)(2,1)} copy(bf16[2048,4096]{0,1:T(8,128)(2,1)} %bitcast.21) | data formatting | bytes 33554432 | tf_op jit(solution)/shard_map/dot_general | solution.py:45
  173.3 0.0 copy-done
  173.3 9.5 %fusion.2 = f32[8,256,256]{2,1,0:T(8,128)} fusion(bf16[8,256,4096]{2,1,0:T(8,128)(2,1)} %bitcast.22, bf16[1,4096,256]{2,1,0:T(8,128)(2,1)S(1)} %copy-done), kind=kOutput, calls=%fused_computation.3 | convolution fusion | flops 4294967296 | bytes 20971520 | tf_op jit(solution)/shard_map/dot_general | solution.py:45
  182.8 4.3 %all-to-all-start = ((f32[8,256,256]{2,1,0:T(8,128)}), f32[8,256,256]{2,1,0:T(8,128)}, u32[]{:S(2)}, u32[]{:S(2)}) async-start(f32[8,256,256]{2,1,0:T(8,128)} %fusion.2), calls=%async_computation | async-start | bytes 4194304 | tf_op jit(solution)/shard_map/all_to_all | solution.py:33
  187.1 0.0 copy-start.1
  187.2 0.0 copy-start.2
  187.2 24.0 %psum.38 = f32[1,8192]{1,0:T(1,128)S(1)} all-reduce(f32[1,8192]{1,0:T(1,128)S(1)} %psum.37), channel_id=1, replica_groups=mesh['dp_0'=4,'dp_1'=2,'tp_0'=2,'tp_1'=8,'tp_2'=2] {'tp_1'}, use_global_device_ids=true, to_apply=%region_5.0 | all-reduce | flops 8192 | bytes 65536 | tf_op jit(solution)/shard_map/psum | solution.py:22
  211.1 7.9 %psum.39 = f32[1,8192]{1,0:T(1,128)S(1)} all-reduce(f32[1,8192]{1,0:T(1,128)S(1)} %psum.38), channel_id=1, replica_groups=mesh['dp_0'=4,'dp_1'=2,'tp_0'=2,'tp_1'=8,'tp_2'=2] {'tp_2'}, use_global_device_ids=true, to_apply=%region_6.0 | all-reduce | flops 8192 | bytes 65536 | tf_op jit(solution)/shard_map/psum | solution.py:22
  219.1 0.6 broadcast_multiply_fusion
  219.7 0.0 all-to-all-done
  219.7 1.8 reduce_sum.20
  221.5 0.0 copy-done.1
  221.5 0.0 copy-done.2
  221.5 1.0 add_divide_fusion
Async XLA Ops:
  7.2 166.1 %copy-start = (bf16[1,4096,256]{2,1,0:T(8,128)(2,1)S(1)}, bf16[1,4096,256]{2,1,0:T(8,128)(2,1)}, u32[]{:S(2)}) copy-start(bf16[1,4096,256]{2,1,0:T(8,128)(2,1)} %param.6) | copy-start | bytes 6291460
  7.2 145.3 %all-gather.3.cloned.1.call-start = ((), (), s32[]{:S(2)}) async-start(), calls=%async_computation.1 | async-start | bytes 17301504 | tf_op jit(solution)/shard_map/all_gather | solution.py:56
  182.8 36.9 %all-to-all-start = ((f32[8,256,256]{2,1,0:T(8,128)}), f32[8,256,256]{2,1,0:T(8,128)}, u32[]{:S(2)}, u32[]{:S(2)}) async-start(f32[8,256,256]{2,1,0:T(8,128)} %fusion.2), calls=%async_computation | async-start | bytes 4194304 | tf_op jit(solution)/shard_map/all_to_all | solution.py:33
  187.1 34.3 %copy-start.1 = (f32[1,256,256]{2,1,0:T(8,128)S(1)}, f32[1,256,256]{2,1,0:T(8,128)}, u32[]{:S(2)}) copy-start(f32[1,256,256]{2,1,0:T(8,128)} %param.11) | copy-start | bytes 786436
  187.2 34.3 %copy-start.2 = (f32[1,256,256]{2,1,0:T(8,128)S(1)}, f32[1,256,256]{2,1,0:T(8,128)}, u32[]{:S(2)}) copy-start(f32[1,256,256]{2,1,0:T(8,128)} %param.10) | copy-start | bytes 786436
Sparse Core Ops, SparseCore 0:
  10.8 141.7 all-gather.2
where the time goes:
time: 230 us; the launch traced here: 229 us
  waiting for transfers between devices  112 us (49%)
  blocking collectives  62.4 us (27%)
  local copies, waits for them, and re-layouts  20.8 us (9%)
  between operations  14.1 us (6%)
  matrix products  9.54 us (4%)
  other arithmetic  6.19 us (3%)
  starting transfers between devices  4.38 us (2%)
    all_gather x1, waiting for transfers between devices, shards(): lax.all_gather(grad_rows, TP, axis=0, tiled=True)  111 us
    psum x5, blocking collectives, over_axes(): return functools.reduce(lax.psum, axes, array)  62.4 us
    dot_general x1, local copies, waits for them, and re-layouts, row_adder(): lax.dot_general(inputs, arrived, (((0,), (0,)), ((), ())), preferred_elem...  20.7 us
    dot_general x1, matrix products, row_adder(): lax.dot_general(inputs, arrived, (((0,), (0,)), ((), ())), preferred_elem...  9.54 us
  transfers between devices with their start and end apart: 2, of which 1 were waited for; matrix products, arithmetic and copies ran while one was open for 2% of the time, Pallas kernels for 0%

commit v1 on v0

v1 whole, which is shorter than its diff:
```python
import functools

import jax
import jax.numpy as jnp
from jax import lax
from jax.experimental import pallas as pl
from jax.experimental.pallas import tpu as pltpu
from jax.sharding import Mesh
from jax.sharding import PartitionSpec as P

AXES = ("x", "yl", "yh", "z", "c")
DP = ("x", "yl")
TP = ("yh", "z", "c")
DP_TP = AXES

beta_one = 0.9
beta_two = 0.95
correct_one = 0.19
correct_two = 0.0975
epsilon = 1e-08

F32 = jnp.float32
BF16 = jnp.bfloat16
VMEM = pl.BlockSpec(memory_space=pltpu.VMEM)
ANY = pl.BlockSpec(memory_space=pl.ANY)
STEPS = (0, -1, 1, -2, 2, -3, 3, 4)


def struct(shape, dtype):
    return jax.ShapeDtypeStruct(shape, dtype)


def cost(flops, bytes_moved):
    return pl.CostEstimate(flops=flops, bytes_accessed=bytes_moved, transcendentals=0)


def swap(array, axis, mask):
    size = lax.axis_size(axis)
    return lax.ppermute(array, axis, [(i, i ^ mask) for i in range(size)])


def shift(array, step):
    size = lax.axis_size("z")
    return lax.ppermute(array, "z", [(i, (i + step) % size) for i in range(size)])


def along_y(array, ab):
    if ab == 1:
        return swap(array, "yl", 1)
    if ab == 2:
        return swap(array, "yh", 1)
    return swap(array, ("yl", "yh"), 3)


def kernel_call(kernel, in_specs, out_shape, limit, estimate, operands, scratch=()):
    return pl.pallas_call(
        kernel,
        in_specs=in_specs,
        out_specs=[VMEM] * len(out_shape),
        out_shape=out_shape,
        scratch_shapes=list(scratch),
        cost_estimate=cost(*estimate),
        compiler_params=pltpu.CompilerParams(vmem_limit_bytes=limit << 20),
    )(*operands)


def order_kernel(k, rows_ref, *refs):
    out = refs[-1]
    x, yl = lax.axis_index("x"), lax.axis_index("yl")
    for j in range(4):
        for b in range(2):
            owner = (x ^ j) * 2 + (yl ^ b)
            to = (j * 2 + b) * 128
            start = pl.multiple_of(owner * 256 + k * 128, 128)
            out[:128, to : to + 128] = rows_ref[:, pl.ds(start, 128)]
    if k == 0:
        for q in range(8):
            sums = refs[0][q * 8 : (q + 1) * 8, :]
            high = sums.astype(BF16).astype(F32)
            out[128:144, q * 128 : (q + 1) * 128] = jnp.concatenate([high, sums - high]).astype(BF16)


def ordered(k, rows, gain):
    out = struct((144 if k == 0 else 128, 1024), BF16)
    specs = [VMEM] * (1 + len(gain))
    return kernel_call(functools.partial(order_kernel, k), specs, [out], 4, (1 << 20, 1 << 20), [rows, *gain])[0]


def turn_kernel(away, inputs_ref, out_ref):
    half, z, c = lax.axis_index("yh") ^ away, lax.axis_index("z"), lax.axis_index("c")
    for p, step in enumerate(STEPS):
        for own in range(2):
            start = half * 2048 + ((z + step + 8) % 8) * 256 + (c ^ own) * 128
            block = inputs_ref[pl.ds(pl.multiple_of(start, 128), 128), :]
            to = (p * 2 + own) * 128
            out_ref[:, to : to + 128] = block.T


def turned(inputs, away):
    return kernel_call(
        functools.partial(turn_kernel, away), [VMEM], [struct((256, 2048), BF16)], 6, (1 << 22, 2 << 20), [inputs]
    )[0]


def product_kernel(k, mine_ref, other_ref, *refs):
    blocks, outs = refs[:16], refs[16:24]
    rows, result, sems = refs[24:27]
    copies = [
        pltpu.make_async_copy(block.at[pl.ds(0, 128), :], rows.at[pl.ds(i * 128, 128), :], sems.at[i])
        for i, block in enumerate(blocks)
    ]
    if k == 0:
        gains, gain_sems = refs[27:]
        z, c = lax.axis_index("z"), lax.axis_index("c")
        for i, block in enumerate(blocks):
            source = ((z + STEPS[i // 2] + 8) % 8) * 2 + (c ^ (i % 2))
            copies.append(
                pltpu.make_async_copy(block.at[pl.ds(128, 16), :], gains.at[source], gain_sems.at[i])
            )
    for copy in copies:
        copy.start()
    for copy in copies:
        copy.wait()
    if k == 0:
        total = jnp.zeros((16, 1024), F32)
        for i in range(16):
            total = total + gains[i].astype(F32)
        total = total[:8] + total[8:]
        for q in range(8):
            at = slice(256 + (q % 4) * 8, 264 + (q % 4) * 8)
            to = slice((q // 4) * 128, (q // 4) * 128 + 128)
            for j in range(4):
                outs[j][at, to] = total[:, q * 128 : (q + 1) * 128]

    @pl.loop(0, 4)
    def _(j):
        start = pl.multiple_of(j * 256, 256)
        right = rows[:, pl.ds(start, 256)]
        result[:256, :] = jnp.dot(mine_ref[...], right, preferred_element_type=F32)
        result[256:, :] = jnp.dot(other_ref[...], right, preferred_element_type=F32)
        for at in range(4):

            @pl.when(j == at)
            def _():
                outs[at][:128, :] = result[:128, :]
                outs[at][128:256, :] = result[256:384, :]

        to = pl.multiple_of(j * 128, 128)
        for a in range(2):
            for b in range(2):
                outs[4 + a * 2 + b][:, pl.ds(to, 128)] = result[
                    a * 256 + 128 : a * 256 + 256, b * 128 : (b + 1) * 128
                ]


def product(k, mine, other, blocks):
    scratch = [pltpu.VMEM((2048, 1024), BF16), pltpu.VMEM((512, 256), F32), pltpu.SemaphoreType.DMA((16,))]
    if k == 0:
        scratch += [pltpu.VMEM((16, 16, 1024), BF16), pltpu.SemaphoreType.DMA((16,))]
    return kernel_call(
        functools.partial(product_kernel, k),
        [VMEM, VMEM] + [ANY] * 16,
        [struct((288 if k == 0 else 256, 256), F32)] * 4 + [struct((128, 512), F32)] * 4,
        14,
        (2 * 512 * 2048 * 1024, 8 << 20),
        [mine, other, *blocks],
        scratch,
    )


def sum_of(refs, at=slice(None)):
    own, one, two, three = (ref[at, :] for ref in refs)
    return (own + one) + (two + three)


def sum_rows_kernel(*refs):
    outs = refs[8:]
    for k in range(2):
        total = sum_of(refs[k * 4 : k * 4 + 4])
        for a in range(2):
            for b in range(2):
                outs[a * 2 + b][:128, k * 128 : (k + 1) * 128] = total[
                    a * 128 : (a + 1) * 128, b * 128 : (b + 1) * 128
                ]
        if k == 0:
            for out in outs:
                out[128:160, :] = total[256:288, :]


def sum_columns_kernel(*refs):
    outs = refs[8:]
    for k in range(2):
        total = sum_of(refs[k * 4 : k * 4 + 4])
        for j in range(4):
            outs[j][:, k * 128 : (k + 1) * 128] = total[:, j * 128 : (j + 1) * 128]


def cut_sum(kernel, parts, rows):
    return kernel_call(kernel, [VMEM] * 8, [struct((rows, 256), F32)] * 4, 5, (1 << 18, 1 << 20), parts)


def adam_kernel(scale, first_ref, second_ref, *refs):
    pieces, (new_first_ref, new_second_ref, update_ref, gain_ref) = refs[:8], refs[8:]
    gain = sum_of(pieces[:4], slice(128, 160)) * scale
    gain_ref[:32, :] = gain[:, :128]
    gain_ref[32:, :] = gain[:, 128:]
    for r in range(2):
        grad = sum_of(pieces[r * 4 : r * 4 + 4], slice(0, 128)) * scale
        at = (slice(r * 128, (r + 1) * 128), slice(None))
        new_first = beta_one * first_ref[at] + (1.0 - beta_one) * grad
        new_second = beta_two * second_ref[at] + (1.0 - beta_two) * grad * grad
        new_first_ref[at] = new_first
        new_second_ref[at] = new_second
        update_ref[at] = new_first / correct_one / (jnp.sqrt(new_second / correct_two) + epsilon)


def adam(scale, first_old, second_old, pieces):
    return kernel_call(
        functools.partial(adam_kernel, scale),
        [VMEM] * 10,
        [struct((256, 256), F32)] * 3 + [struct((64, 128), F32)],
        5,
        (1 << 20, 2 << 20),
        [first_old, second_old, *pieces],
    )


def shards(proj_in, kv_grad, normed, norm_grad, first_moment, second_moment):
    return update_of(proj_in[0], kv_grad[0], normed, norm_grad, first_moment[0], second_moment[0])


def update_of(inputs, rows, normed, norm_grad, first_moment, second_moment):
    replicas = lax.axis_size(DP)
    gain = jnp.sum(norm_grad.astype(F32) * normed.astype(F32), axis=1).reshape(64, 128)
    starts = [ordered(0, rows, [gain]), ordered(1, rows, [])]

    def gathered(k):
        own = {0: starts[k]}
        up = down = starts[k]
        for step in (1, 2, 3, 4):
            if step < 4 or k == 0:
                up = shift(up, 1)
                own[4 if step == 4 else -step] = up
            if step < 4 or k == 1:
                down = shift(down, -1)
                own[step] = down
        blocks = []
        for step in STEPS:
            blocks += [own[step], swap(own[step], "c", 1)]
        return blocks

    gathers = [gathered(k) for k in range(2)]
    mine = turned(inputs, 0)
    other = swap(turned(inputs, 1), "yh", 1)

    in_x, in_y = [], []
    for k in range(2):
        outs = product(k, mine, other, gathers[k])
        by_x, by_y = outs[:4], outs[4:]
        in_x += [by_x[0]] + [swap(by_x[j], "x", j) for j in (1, 2, 3)]
        in_y += [by_y[0]] + [along_y(by_y[ab], ab) for ab in (1, 2, 3)]
    by_y = cut_sum(sum_rows_kernel, in_x, 160)
    by_x = cut_sum(sum_columns_kernel, in_y, 128)
    pieces = [by_y[0]] + [along_y(by_y[ab], ab) for ab in (1, 2, 3)]
    pieces += [by_x[0]] + [swap(by_x[j], "x", j) for j in (1, 2, 3)]
    new_first, new_second, update, gain = adam(1.0 / replicas, first_moment, second_moment, pieces)
    return (new_first[None], new_second[None], update[None], gain.reshape(1, 8192))


def solution(mesh):
    finer = Mesh(mesh.devices.reshape(4, 2, 2, 8, 2), AXES)
    return jax.shard_map(
        shards,
        mesh=finer,
        in_specs=(
            P(None, DP, TP),
            P(None, DP_TP, None),
            P(None, DP_TP, None),
            P(None, DP_TP, None),
            P(None, TP, DP),
            P(None, TP, DP),
        ),
        out_specs=(P(None, TP, DP), P(None, TP, DP), P(None, TP, DP), P()),
        check_vma=False,
    )
```

time: 230 us -> 127 us (0.55)
  blocking collectives: 62.4 us -> 0 us
  waiting for transfers between devices: 112 us -> 51.5 us
  starting transfers between devices: 4.38 us -> 60.5 us
  local copies, waits for them, and re-layouts: 20.8 us -> 1.06 us
  between operations: 14.1 us -> 0.85 us
  Pallas kernels: 0 us -> 10.3 us
  matrix products: 9.54 us -> 0 us
  other arithmetic: 6.19 us -> 2.82 us
    all_gather x1 -> x0, waiting for transfers between devices: 111 us -> none  [shards(): lax.all_gather(grad_rows, TP, axis=0, tiled=True)]
    psum x5 -> x0, blocking collectives: 62.4 us -> none  [over_axes(): return functools.reduce(lax.psum, axes, array)]
    ppermute x0 -> x49, starting transfers between devices: none -> 60.5 us  [the longest x35 45.5 us: swap(): return lax.ppermute(array, axis, [(i, i ^ mask) for i in range(size)])]
    ppermute x0 -> x49, waiting for transfers between devices: none -> 51.5 us  [the longest x35 29.4 us: swap(): return lax.ppermute(array, axis, [(i, i ^ mask) for i in range(size)])]
    dot_general x1 -> x0, local copies, waits for them, and re-layouts: 20.7 us -> none  [row_adder(): lax.dot_general(inputs, arrived, (((0,), (0,)), ((), ())), preferred_elem...]
    pallas_call x0 -> x9, Pallas kernels: none -> 10.3 us  [kernel_call(): pl.pallas_call(kernel, in_specs=in_specs, out_specs=[VMEM] * len(out_shap...]
    dot_general x1 -> x0, matrix products: 9.54 us -> none  [row_adder(): lax.dot_general(inputs, arrived, (((0,), (0,)), ((), ())), preferred_elem...]
    all_to_all x1 -> x0, starting transfers between devices: 4.34 us -> none  [sent_and_summed(): lax.all_to_all(pieces, axis, split_axis=0, concat_axis=0, tiled=True)]
  transfers between devices with their start and end apart: 2 -> 49, of which waited for: 1 -> 13; matrix products, arithmetic and copies ran while one was open for 2% -> 2% of each run, Pallas kernels for 0% -> 7%
where the time goes in v1:
time: 127 us
  starting transfers between devices  60.5 us (48%)
  waiting for transfers between devices  51.5 us (41%)
  Pallas kernels  10.3 us (8%)
  other arithmetic  2.82 us (2%)
    ppermute x35, starting transfers between devices, swap(): return lax.ppermute(array, axis, [(i, i ^ mask) for i in range(size)])  45.5 us
    ppermute x35, waiting for transfers between devices, swap(): return lax.ppermute(array, axis, [(i, i ^ mask) for i in range(size)])  29.4 us
    ppermute x14, waiting for transfers between devices, shift(): lax.ppermute(array, 'z', [(i, (i + step) % size) for i in range(size)])  22.1 us
    ppermute x14, starting transfers between devices, shift(): lax.ppermute(array, 'z', [(i, (i + step) % size) for i in range(size)])  15 us
    pallas_call x9, Pallas kernels, kernel_call(): pl.pallas_call(kernel, in_specs=in_specs, out_specs=[VMEM] * len(out_shap...  10.3 us
    reduce_sum x1, other arithmetic, update_of(): jnp.sum(norm_grad.astype(F32) * normed.astype(F32), axis=1).reshape(64, 128)  2.82 us
  transfers between devices with their start and end apart: 49, of which 13 were waited for; matrix products, arithmetic and copies ran while one was open for 2% of the time, Pallas kernels for 7%

profile of v1, /device:TPU:1, one launch (start us, length us, event | category | flops | bytes accessed | tf_op | source)
XLA Modules:
  0.0 127.1 jit_solution(2132238325591812181)
XLA Ops:
  1.8 3.3 %collective-permute-start.19 = (bf16[128,1024]{1,0:T(8,128)(2,1)S(1)}, bf16[128,1024]{1,0:T(8,128)(2,1)S(1)}, u32[]{:S(2)}, u32[]{:S(2)}) collective-permute-start(bf16[128,1024]{1,0:T(8,128)(2,1)S(1)} %shard_map.97.refs_0_), channel_id=1, source_target_pairs={{0,1},{1,0},{2,3},{3,2},{4,5},{5,4},{6,7},{7,6},{8,9},{9,8},{10,11... | collective-permute-start | bytes 786440 | tf_op jit(solution)/shard_map/ppermute | solution.py:39
  5.1 2.8 %multiply_reduce_fusion = f32[8192]{0:T(1024)S(1)} fusion(bf16[1,128,8192]{2,1,0:T(8,128)(2,1)} %param.8, bf16[1,128,8192]{2,1,0:T(8,128)(2,1)} %param.9), kind=kLoop, calls=%fused_computation | loop fusion | flops 4186112 | bytes 4227072 | tf_op jit(solution)/shard_map/reduce_sum | solution.py:234
  8.2 3.9 %collective-permute-start.22 = (bf16[128,1024]{1,0:T(8,128)(2,1)S(1)}, bf16[128,1024]{1,0:T(8,128)(2,1)S(1)}, u32[]{:S(2)}, u32[]{:S(2)}) collective-permute-start(bf16[128,1024]{1,0:T(8,128)(2,1)S(1)} %shard_map.97.refs_0_), channel_id=1, source_target_pairs={{0,14},{2,0},{4,2},{6,4},{8,6},{10,8},{12,10},{14,12},{1,15},{3,1}... | collective-permute-start | bytes 786440 | tf_op jit(solution)/shard_map/ppermute | solution.py:44
  12.2 2.7 %collective-permute-start.4 = (bf16[144,1024]{1,0:T(8,128)(2,1)S(1)}, bf16[144,1024]{1,0:T(8,128)(2,1)S(1)}, u32[]{:S(2)}, u32[]{:S(2)}) collective-permute-start(bf16[144,1024]{1,0:T(8,128)(2,1)S(1)} %shard_map.95.refs_0_), channel_id=1, source_target_pairs={{0,14},{2,0},{4,2},{6,4},{8,6},{10,8},{12,10},{14,12},{1,15},{3,1}... | collective-permute-start | bytes 884744 | tf_op jit(solution)/shard_map/ppermute | solution.py:44
  14.8 3.6 %collective-permute-done.20.refs_2_ = bf16[128,1024]{1,0:T(8,128)(2,1)S(1)} collective-permute-done((bf16[128,1024]{1,0:T(8,128)(2,1)S(1)}, bf16[128,1024]{1,0:T(8,128)(2,1)S(1)}, u32[]{:S(2)}, u32[]{:S(2)}) %collective-permute-start.20) | collective-permute-done | bytes 262176 | tf_op jit(solution)/shard_map/ppermute | solution.py:44
  20.0 4.7 %collective-permute-done.2.refs_2_ = bf16[144,1024]{1,0:T(8,128)(2,1)S(1)} collective-permute-done((bf16[144,1024]{1,0:T(8,128)(2,1)S(1)}, bf16[144,1024]{1,0:T(8,128)(2,1)S(1)}, u32[]{:S(2)}, u32[]{:S(2)}) %collective-permute-start.2) | collective-permute-done | bytes 294944 | tf_op jit(solution)/shard_map/ppermute | solution.py:44
  25.9 2.3 %collective-permute-start.3 = (bf16[144,1024]{1,0:T(8,128)(2,1)S(1)}, bf16[144,1024]{1,0:T(8,128)(2,1)S(1)}, u32[]{:S(2)}, u32[]{:S(2)}) collective-permute-start(bf16[144,1024]{1,0:T(8,128)(2,1)S(1)} %collective-permute-done.2.refs_2_), channel_id=1, source_target_pairs={{0,1},{1,0},{2,3},{3,2},{4,5},{5,4},{6,7},{7,6},{8,9},{9,8},{10,11... | collective-permute-start | bytes 884744 | tf_op jit(solution)/shard_map/ppermute | solution.py:39
  28.7 3.0 %collective-permute-start = (bf16[256,2048]{1,0:T(8,128)(2,1)S(1)}, bf16[256,2048]{1,0:T(8,128)(2,1)S(1)}, u32[]{:S(2)}, u32[]{:S(2)}) collective-permute-start(bf16[256,2048]{1,0:T(8,128)(2,1)S(1)} %shard_map.94), channel_id=1, source_target_pairs={{0,16},{16,0},{1,17},{17,1},{2,18},{18,2},{3,19},{19,3},{4,20},{20... | collective-permute-start | bytes 3145736 | tf_op jit(solution)/shard_map/ppermute | solution.py:39
  31.7 2.7 %collective-permute-start.8 = (bf16[144,1024]{1,0:T(8,128)(2,1)S(1)}, bf16[144,1024]{1,0:T(8,128)(2,1)S(1)}, u32[]{:S(2)}, u32[]{:S(2)}) collective-permute-start(bf16[144,1024]{1,0:T(8,128)(2,1)S(1)} %collective-permute-done.4.refs_4_), channel_id=1, source_target_pairs={{0,14},{2,0},{4,2},{6,4},{8,6},{10,8},{12,10},{14,12},{1,15},{3,1}... | collective-permute-start | bytes 884744 | tf_op jit(solution)/shard_map/ppermute | solution.py:44
  36.4 4.4 %collective-permute-done.6.refs_6_ = bf16[144,1024]{1,0:T(8,128)(2,1)S(1)} collective-permute-done((bf16[144,1024]{1,0:T(8,128)(2,1)S(1)}, bf16[144,1024]{1,0:T(8,128)(2,1)S(1)}, u32[]{:S(2)}, u32[]{:S(2)}) %collective-permute-start.6) | collective-permute-done | bytes 294944 | tf_op jit(solution)/shard_map/ppermute | solution.py:44
  43.8 3.4 %collective-permute-done.30.refs_12_ = bf16[128,1024]{1,0:T(8,128)(2,1)S(1)} collective-permute-done((bf16[128,1024]{1,0:T(8,128)(2,1)S(1)}, bf16[128,1024]{1,0:T(8,128)(2,1)S(1)}, u32[]{:S(2)}, u32[]{:S(2)}) %collective-permute-start.30) | collective-permute-done | bytes 262176 | tf_op jit(solution)/shard_map/ppermute | solution.py:44
  49.0 5.6 %collective-permute-done.28.refs_10_ = bf16[128,1024]{1,0:T(8,128)(2,1)S(1)} collective-permute-done((bf16[128,1024]{1,0:T(8,128)(2,1)S(1)}, bf16[128,1024]{1,0:T(8,128)(2,1)S(1)}, u32[]{:S(2)}, u32[]{:S(2)}) %collective-permute-start.28) | collective-permute-done | bytes 262176 | tf_op jit(solution)/shard_map/ppermute | solution.py:44
  54.7 4.4 %collective-permute-start.29 = (bf16[128,1024]{1,0:T(8,128)(2,1)S(1)}, bf16[128,1024]{1,0:T(8,128)(2,1)S(1)}, u32[]{:S(2)}, u32[]{:S(2)}) collective-permute-start(bf16[128,1024]{1,0:T(8,128)(2,1)S(1)} %collective-permute-done.28.refs_10_), channel_id=1, source_target_pairs={{0,1},{1,0},{2,3},{3,2},{4,5},{5,4},{6,7},{7,6},{8,9},{9,8},{10,11... | collective-permute-start | bytes 786440 | tf_op jit(solution)/shard_map/ppermute | solution.py:39
  59.1 2.4 %collective-permute-start.33 = (bf16[128,1024]{1,0:T(8,128)(2,1)S(1)}, bf16[128,1024]{1,0:T(8,128)(2,1)S(1)}, u32[]{:S(2)}, u32[]{:S(2)}) collective-permute-start(bf16[128,1024]{1,0:T(8,128)(2,1)S(1)} %collective-permute-done.32.refs_14_), channel_id=1, source_target_pairs={{0,1},{1,0},{2,3},{3,2},{4,5},{5,4},{6,7},{7,6},{8,9},{9,8},{10,11... | collective-permute-start | bytes 786440 | tf_op jit(solution)/shard_map/ppermute | solution.py:39
  63.8 3.6 %shard_map.98 = (f32[256,256]{1,0:T(8,128)S(1)}, f32[256,256]{1,0:T(8,128)S(1)}, f32[256,256]{1,0:T(8,128)S(1)}, f32[256,256]{1,0:T(8,128)S(1)}, f32[128,512]{1,...) custom-call(bf16[256,2048]{1,0:T(8,128)(2,1)S(1)} %shard_map.93.mine_ref, ...), custom_call_target="tpu_custom_call" | custom-call | flops 2147483648 | bytes 8388608 | tf_op jit(solution)/shard_map/pallas_call | solution.py:56
  72.5 4.6 %shard_map.96 = (f32[288,256]{1,0:T(8,128)S(1)}, f32[288,256]{1,0:T(8,128)S(1)}, f32[288,256]{1,0:T(8,128)S(1)}, f32[288,256]{1,0:T(8,128)S(1)}, f32[128,512]{1,...) custom-call(bf16[256,2048]{1,0:T(8,128)(2,1)S(1)} %shard_map.93.mine_ref, ...), custom_call_target="tpu_custom_call" | custom-call | flops 2147483648 | bytes 8388608 | tf_op jit(solution)/shard_map/pallas_call | solution.py:56
  82.2 2.5 %collective-permute-start.35 = (f32[256,256]{1,0:T(8,128)S(1)}, f32[256,256]{1,0:T(8,128)S(1)}, u32[]{:S(2)}, u32[]{:S(2)}) collective-permute-start(f32[256,256]{1,0:T(8,128)S(1)} %get-tuple-element.38), channel_id=1, source_target_pairs={{0,128},{64,192},{128,0},{192,64},{1,129},{65,193},{129,1},{193,65... | collective-permute-start | bytes 786440 | tf_op jit(solution)/shard_map/ppermute | solution.py:39
  84.7 2.3 %collective-permute-done.40.refs_1_ = f32[128,512]{1,0:T(8,128)S(1)} collective-permute-done((f32[128,512]{1,0:T(8,128)S(1)}, f32[128,512]{1,0:T(8,128)S(1)}, u32[]{:S(2)}, u32[]{:S(2)}) %collective-permute-start.40) | collective-permute-done | bytes 262176 | tf_op jit(solution)/shard_map/ppermute | solution.py:39
  87.0 2.5 %collective-permute-start.17 = (f32[288,256]{1,0:T(8,128)S(1)}, f32[288,256]{1,0:T(8,128)S(1)}, u32[]{:S(2)}, u32[]{:S(2)}) collective-permute-start(f32[288,256]{1,0:T(8,128)S(1)} %get-tuple-element.34), channel_id=1, source_target_pairs={{0,128},{64,192},{128,0},{192,64},{1,129},{65,193},{129,1},{193,65... | collective-permute-start | bytes 884744 | tf_op jit(solution)/shard_map/ppermute | solution.py:39
  89.5 4.0 %collective-permute-done.41.refs_2_ = f32[128,512]{1,0:T(8,128)S(1)} collective-permute-done((f32[128,512]{1,0:T(8,128)S(1)}, f32[128,512]{1,0:T(8,128)S(1)}, u32[]{:S(2)}, u32[]{:S(2)}) %collective-permute-start.41) | collective-permute-done | bytes 262176 | tf_op jit(solution)/shard_map/ppermute | solution.py:39
  98.0 15.4 %collective-permute-done.36.refs_7_ = f32[256,256]{1,0:T(8,128)S(1)} collective-permute-done((f32[256,256]{1,0:T(8,128)S(1)}, f32[256,256]{1,0:T(8,128)S(1)}, u32[]{:S(2)}, u32[]{:S(2)}) %collective-permute-start.36) | collective-permute-done | bytes 262176 | tf_op jit(solution)/shard_map/ppermute | solution.py:39
  113.6 2.7 %collective-permute-start.38 = (f32[160,256]{1,0:T(8,128)S(1)}, f32[160,256]{1,0:T(8,128)S(1)}, u32[]{:S(2)}, u32[]{:S(2)}) collective-permute-start(f32[160,256]{1,0:T(8,128)S(1)} %get-tuple-element.42), channel_id=1, source_target_pairs={{0,16},{16,0},{1,17},{17,1},{2,18},{18,2},{3,19},{19,3},{4,20},{20... | collective-permute-start | bytes 491528 | tf_op jit(solution)/shard_map/ppermute | solution.py:39
  119.9 3.2 %collective-permute-done.47.refs_6_ = f32[128,256]{1,0:T(8,128)S(1)} collective-permute-done((f32[128,256]{1,0:T(8,128)S(1)}, f32[128,256]{1,0:T(8,128)S(1)}, u32[]{:S(2)}, u32[]{:S(2)}) %collective-permute-start.47) | collective-permute-done | bytes 131104 | tf_op jit(solution)/shard_map/ppermute | solution.py:39
  123.1 3.0 %collective-permute-done.48.refs_7_ = f32[128,256]{1,0:T(8,128)S(1)} collective-permute-done((f32[128,256]{1,0:T(8,128)S(1)}, f32[128,256]{1,0:T(8,128)S(1)}, u32[]{:S(2)}, u32[]{:S(2)}) %collective-permute-start.48) | collective-permute-done | bytes 131104 | tf_op jit(solution)/shard_map/ppermute | solution.py:39
  (94 shorter events, 33.3 us)
Async XLA Ops:
  1.8 10.4 %collective-permute-start.19 = (bf16[128,1024]{1,0:T(8,128)(2,1)S(1)}, bf16[128,1024]{1,0:T(8,128)(2,1)S(1)}, u32[]{:S(2)}, u32[]{:S(2)}) collective-permute-start(bf16[128,1024]{1,0:T(8,128)(2,1)S(1)} %shard_map.97.refs_0_), channel_id=1, source_target_pairs={{0,1},{1,0},{2,3},{3,2},{4,5},{5,4},{6,7},{7,6},{8,9},{9,8},{10,11... | collective-permute-start | bytes 786440 | tf_op jit(solution)/shard_map/ppermute | solution.py:39
  8.0 11.9 %collective-permute-start.1 = (bf16[144,1024]{1,0:T(8,128)(2,1)S(1)}, bf16[144,1024]{1,0:T(8,128)(2,1)S(1)}, u32[]{:S(2)}, u32[]{:S(2)}) collective-permute-start(bf16[144,1024]{1,0:T(8,128)(2,1)S(1)} %shard_map.95.refs_0_), channel_id=1, source_target_pairs={{0,1},{1,0},{2,3},{3,2},{4,5},{5,4},{6,7},{7,6},{8,9},{9,8},{10,11... | collective-permute-start | bytes 884744 | tf_op jit(solution)/shard_map/ppermute | solution.py:39
  8.2 11.7 %collective-permute-start.22 = (bf16[128,1024]{1,0:T(8,128)(2,1)S(1)}, bf16[128,1024]{1,0:T(8,128)(2,1)S(1)}, u32[]{:S(2)}, u32[]{:S(2)}) collective-permute-start(bf16[128,1024]{1,0:T(8,128)(2,1)S(1)} %shard_map.97.refs_0_), channel_id=1, source_target_pairs={{0,14},{2,0},{4,2},{6,4},{8,6},{10,8},{12,10},{14,12},{1,15},{3,1}... | collective-permute-start | bytes 786440 | tf_op jit(solution)/shard_map/ppermute | solution.py:44
  12.2 12.6 %collective-permute-start.2 = (bf16[144,1024]{1,0:T(8,128)(2,1)S(1)}, bf16[144,1024]{1,0:T(8,128)(2,1)S(1)}, u32[]{:S(2)}, u32[]{:S(2)}) collective-permute-start(bf16[144,1024]{1,0:T(8,128)(2,1)S(1)} %shard_map.95.refs_0_), channel_id=1, source_target_pairs={{0,2},{2,4},{4,6},{6,8},{8,10},{10,12},{12,14},{14,0},{1,3},{3,5},... | collective-permute-start | bytes 884744 | tf_op jit(solution)/shard_map/ppermute | solution.py:44
  12.2 13.8 %collective-permute-start.4 = (bf16[144,1024]{1,0:T(8,128)(2,1)S(1)}, bf16[144,1024]{1,0:T(8,128)(2,1)S(1)}, u32[]{:S(2)}, u32[]{:S(2)}) collective-permute-start(bf16[144,1024]{1,0:T(8,128)(2,1)S(1)} %shard_map.95.refs_0_), channel_id=1, source_target_pairs={{0,14},{2,0},{4,2},{6,4},{8,6},{10,8},{12,10},{14,12},{1,15},{3,1}... | collective-permute-start | bytes 884744 | tf_op jit(solution)/shard_map/ppermute | solution.py:44
  19.9 11.8 %collective-permute-start.24 = (bf16[128,1024]{1,0:T(8,128)(2,1)S(1)}, bf16[128,1024]{1,0:T(8,128)(2,1)S(1)}, u32[]{:S(2)}, u32[]{:S(2)}) collective-permute-start(bf16[128,1024]{1,0:T(8,128)(2,1)S(1)} %collective-permute-done.20.refs_2_), channel_id=1, source_target_pairs={{0,2},{2,4},{4,6},{6,8},{8,10},{10,12},{12,14},{14,0},{1,3},{3,5},... | collective-permute-start | bytes 786440 | tf_op jit(solution)/shard_map/ppermute | solution.py:44
  28.7 32.7 %collective-permute-start = (bf16[256,2048]{1,0:T(8,128)(2,1)S(1)}, bf16[256,2048]{1,0:T(8,128)(2,1)S(1)}, u32[]{:S(2)}, u32[]{:S(2)}) collective-permute-start(bf16[256,2048]{1,0:T(8,128)(2,1)S(1)} %shard_map.94), channel_id=1, source_target_pairs={{0,16},{16,0},{1,17},{17,1},{2,18},{18,2},{3,19},{19,3},{4,20},{20... | collective-permute-start | bytes 3145736 | tf_op jit(solution)/shard_map/ppermute | solution.py:39
  42.3 16.8 %collective-permute-start.12 = (bf16[144,1024]{1,0:T(8,128)(2,1)S(1)}, bf16[144,1024]{1,0:T(8,128)(2,1)S(1)}, u32[]{:S(2)}, u32[]{:S(2)}) collective-permute-start(bf16[144,1024]{1,0:T(8,128)(2,1)S(1)} %collective-permute-done.8.refs_8_), channel_id=1, source_target_pairs={{0,14},{2,0},{4,2},{6,4},{8,6},{10,8},{12,10},{14,12},{1,15},{3,1}... | collective-permute-start | bytes 884744 | tf_op jit(solution)/shard_map/ppermute | solution.py:44
  43.5 11.2 %collective-permute-start.28 = (bf16[128,1024]{1,0:T(8,128)(2,1)S(1)}, bf16[128,1024]{1,0:T(8,128)(2,1)S(1)}, u32[]{:S(2)}, u32[]{:S(2)}) collective-permute-start(bf16[128,1024]{1,0:T(8,128)(2,1)S(1)} %collective-permute-done.24.refs_6_), channel_id=1, source_target_pairs={{0,2},{2,4},{4,6},{6,8},{8,10},{10,12},{12,14},{14,0},{1,3},{3,5},... | collective-permute-start | bytes 786440 | tf_op jit(solution)/shard_map/ppermute | solution.py:44
  47.1 12.0 %collective-permute-start.32 = (bf16[128,1024]{1,0:T(8,128)(2,1)S(1)}, bf16[128,1024]{1,0:T(8,128)(2,1)S(1)}, u32[]{:S(2)}, u32[]{:S(2)}) collective-permute-start(bf16[128,1024]{1,0:T(8,128)(2,1)S(1)} %collective-permute-done.30.refs_12_), channel_id=1, source_target_pairs={{0,14},{2,0},{4,2},{6,4},{8,6},{10,8},{12,10},{14,12},{1,15},{3,1}... | collective-permute-start | bytes 786440 | tf_op jit(solution)/shard_map/ppermute | solution.py:44
  49.0 13.0 %collective-permute-start.14 = (bf16[144,1024]{1,0:T(8,128)(2,1)S(1)}, bf16[144,1024]{1,0:T(8,128)(2,1)S(1)}, u32[]{:S(2)}, u32[]{:S(2)}) collective-permute-start(bf16[144,1024]{1,0:T(8,128)(2,1)S(1)} %collective-permute-done.10.refs_10_), channel_id=1, source_target_pairs={{0,2},{2,4},{4,6},{6,8},{8,10},{10,12},{12,14},{14,0},{1,3},{3,5},... | collective-permute-start | bytes 884744 | tf_op jit(solution)/shard_map/ppermute | solution.py:44
  68.6 10.9 %collective-permute-start.43 = (f32[128,512]{1,0:T(8,128)S(1)}, f32[128,512]{1,0:T(8,128)S(1)}, u32[]{:S(2)}, u32[]{:S(2)}) collective-permute-start(f32[128,512]{1,0:T(8,128)S(1)} %get-tuple-element.49), channel_id=1, source_target_pairs={{0,32},{32,0},{1,33},{33,1},{2,34},{34,2},{3,35},{35,3},{4,36},{36... | collective-permute-start | bytes 786440 | tf_op jit(solution)/shard_map/ppermute | solution.py:39
  69.0 13.2 %collective-permute-start.44 = (f32[128,512]{1,0:T(8,128)S(1)}, f32[128,512]{1,0:T(8,128)S(1)}, u32[]{:S(2)}, u32[]{:S(2)}) collective-permute-start(f32[128,512]{1,0:T(8,128)S(1)} %get-tuple-element.50), channel_id=1, source_target_pairs={{0,16},{16,0},{1,17},{17,1},{2,18},{18,2},{3,19},{19,3},{4,20},{20... | collective-permute-start | bytes 786440 | tf_op jit(solution)/shard_map/ppermute | solution.py:39
  70.9 13.7 %collective-permute-start.45 = (f32[128,512]{1,0:T(8,128)S(1)}, f32[128,512]{1,0:T(8,128)S(1)}, u32[]{:S(2)}, u32[]{:S(2)}) collective-permute-start(f32[128,512]{1,0:T(8,128)S(1)} %get-tuple-element.51), channel_id=1, source_target_pairs={{0,48},{16,32},{32,16},{48,0},{1,49},{17,33},{33,17},{49,1},{2,50}... | collective-permute-start | bytes 786440 | tf_op jit(solution)/shard_map/ppermute | solution.py:39
  77.2 16.2 %collective-permute-start.41 = (f32[128,512]{1,0:T(8,128)S(1)}, f32[128,512]{1,0:T(8,128)S(1)}, u32[]{:S(2)}, u32[]{:S(2)}) collective-permute-start(f32[128,512]{1,0:T(8,128)S(1)} %get-tuple-element.46), channel_id=1, source_target_pairs={{0,16},{16,0},{1,17},{17,1},{2,18},{18,2},{3,19},{19,3},{4,20},{20... | collective-permute-start | bytes 786440 | tf_op jit(solution)/shard_map/ppermute | solution.py:39
  79.5 16.1 %collective-permute-start.42 = (f32[128,512]{1,0:T(8,128)S(1)}, f32[128,512]{1,0:T(8,128)S(1)}, u32[]{:S(2)}, u32[]{:S(2)}) collective-permute-start(f32[128,512]{1,0:T(8,128)S(1)} %get-tuple-element.47), channel_id=1, source_target_pairs={{0,48},{16,32},{32,16},{48,0},{1,49},{17,33},{33,17},{49,1},{2,50}... | collective-permute-start | bytes 786440 | tf_op jit(solution)/shard_map/ppermute | solution.py:39
  82.2 15.3 %collective-permute-start.35 = (f32[256,256]{1,0:T(8,128)S(1)}, f32[256,256]{1,0:T(8,128)S(1)}, u32[]{:S(2)}, u32[]{:S(2)}) collective-permute-start(f32[256,256]{1,0:T(8,128)S(1)} %get-tuple-element.38), channel_id=1, source_target_pairs={{0,128},{64,192},{128,0},{192,64},{1,129},{65,193},{129,1},{193,65... | collective-permute-start | bytes 786440 | tf_op jit(solution)/shard_map/ppermute | solution.py:39
  84.7 28.7 %collective-permute-start.16 = (f32[288,256]{1,0:T(8,128)S(1)}, f32[288,256]{1,0:T(8,128)S(1)}, u32[]{:S(2)}, u32[]{:S(2)}) collective-permute-start(f32[288,256]{1,0:T(8,128)S(1)} %get-tuple-element.33), channel_id=1, source_target_pairs={{0,64},{64,0},{128,192},{192,128},{1,65},{65,1},{129,193},{193,129... | collective-permute-start | bytes 884744 | tf_op jit(solution)/shard_map/ppermute | solution.py:39
  87.0 26.4 %collective-permute-start.17 = (f32[288,256]{1,0:T(8,128)S(1)}, f32[288,256]{1,0:T(8,128)S(1)}, u32[]{:S(2)}, u32[]{:S(2)}) collective-permute-start(f32[288,256]{1,0:T(8,128)S(1)} %get-tuple-element.34), channel_id=1, source_target_pairs={{0,128},{64,192},{128,0},{192,64},{1,129},{65,193},{129,1},{193,65... | collective-permute-start | bytes 884744 | tf_op jit(solution)/shard_map/ppermute | solution.py:39
  93.5 19.9 %collective-permute-start.18 = (f32[288,256]{1,0:T(8,128)S(1)}, f32[288,256]{1,0:T(8,128)S(1)}, u32[]{:S(2)}, u32[]{:S(2)}) collective-permute-start(f32[288,256]{1,0:T(8,128)S(1)} %get-tuple-element.35), channel_id=1, source_target_pairs={{0,192},{64,128},{128,64},{192,0},{1,193},{65,129},{129,65},{193,1... | collective-permute-start | bytes 884744 | tf_op jit(solution)/shard_map/ppermute | solution.py:39
  95.6 17.8 %collective-permute-start.36 = (f32[256,256]{1,0:T(8,128)S(1)}, f32[256,256]{1,0:T(8,128)S(1)}, u32[]{:S(2)}, u32[]{:S(2)}) collective-permute-start(f32[256,256]{1,0:T(8,128)S(1)} %get-tuple-element.39), channel_id=1, source_target_pairs={{0,192},{64,128},{128,64},{192,0},{1,193},{65,129},{129,65},{193,1... | collective-permute-start | bytes 786440 | tf_op jit(solution)/shard_map/ppermute | solution.py:39
  97.6 21.8 %collective-permute-start.46 = (f32[128,256]{1,0:T(8,128)S(1)}, f32[128,256]{1,0:T(8,128)S(1)}, u32[]{:S(2)}, u32[]{:S(2)}) collective-permute-start(f32[128,256]{1,0:T(8,128)S(1)} %get-tuple-element.53), channel_id=1, source_target_pairs={{0,64},{64,0},{128,192},{192,128},{1,65},{65,1},{129,193},{193,129... | collective-permute-start | bytes 393224 | tf_op jit(solution)/shard_map/ppermute | solution.py:39
  113.5 12.5 %collective-permute-start.37 = (f32[160,256]{1,0:T(8,128)S(1)}, f32[160,256]{1,0:T(8,128)S(1)}, u32[]{:S(2)}, u32[]{:S(2)}) collective-permute-start(f32[160,256]{1,0:T(8,128)S(1)} %get-tuple-element.41), channel_id=1, source_target_pairs={{0,32},{32,0},{1,33},{33,1},{2,34},{34,2},{3,35},{35,3},{4,36},{36... | collective-permute-start | bytes 491528 | tf_op jit(solution)/shard_map/ppermute | solution.py:39
  113.6 12.4 %collective-permute-start.38 = (f32[160,256]{1,0:T(8,128)S(1)}, f32[160,256]{1,0:T(8,128)S(1)}, u32[]{:S(2)}, u32[]{:S(2)}) collective-permute-start(f32[160,256]{1,0:T(8,128)S(1)} %get-tuple-element.42), channel_id=1, source_target_pairs={{0,16},{16,0},{1,17},{17,1},{2,18},{18,2},{3,19},{19,3},{4,20},{20... | collective-permute-start | bytes 491528 | tf_op jit(solution)/shard_map/ppermute | solution.py:39
  (30 other events, 285.1 us)

commit v2 on v1

--- a/solution.py
+++ b/solution.py
@@ -83,7 +83,9 @@
 def ordered(k, rows, gain):
     out = struct((144 if k == 0 else 128, 1024), BF16)
     specs = [VMEM] * (1 + len(gain))
-    return kernel_call(functools.partial(order_kernel, k), specs, [out], 4, (1 << 20, 1 << 20), [rows, *gain])[0]
+    return kernel_call(
+        functools.partial(order_kernel, k), specs, [out], 4, (1 << 20, 1 << 20), [rows, *gain]
+    )[0]
 
 
 def turn_kernel(away, inputs_ref, out_ref):
@@ -98,28 +100,67 @@
 
 def turned(inputs, away):
     return kernel_call(
-        functools.partial(turn_kernel, away), [VMEM], [struct((256, 2048), BF16)], 6, (1 << 22, 2 << 20), [inputs]
+        functools.partial(turn_kernel, away),
+        [VMEM],
+        [struct((256, 2048), BF16)],
+        6,
+        (1 << 22, 2 << 20),
+        [inputs],
     )[0]
 
 
 def product_kernel(k, mine_ref, other_ref, *refs):
     blocks, outs = refs[:16], refs[16:24]
     rows, result, sems = refs[24:27]
-    copies = [
-        pltpu.make_async_copy(block.at[pl.ds(0, 128), :], rows.at[pl.ds(i * 128, 128), :], sems.at[i])
-        for i, block in enumerate(blocks)
-    ]
+
+    def copies_of(j):
+        columns = pl.ds(pl.multiple_of(j * 256, 256), 256)
+        return [
+            pltpu.make_async_copy(
+                block.at[pl.ds(0, 128), columns], rows.at[j, pl.ds(i * 128, 128), :], sems.at[j, i]
+            )
+            for i, block in enumerate(blocks)
+        ]
+
+    @pl.loop(0, 4)
+    def _(j):
+        for copy in copies_of(j):
+            copy.start()
+
+    gain_copies = []
     if k == 0:
         gains, gain_sems = refs[27:]
         z, c = lax.axis_index("z"), lax.axis_index("c")
         for i, block in enumerate(blocks):
             source = ((z + STEPS[i // 2] + 8) % 8) * 2 + (c ^ (i % 2))
-            copies.append(
+            gain_copies.append(
                 pltpu.make_async_copy(block.at[pl.ds(128, 16), :], gains.at[source], gain_sems.at[i])
             )
-    for copy in copies:
+    for copy in gain_copies:
         copy.start()
-    for copy in copies:
+
+    @pl.loop(0, 4)
+    def _(j):
+        for copy in copies_of(j):
+            copy.wait()
+        right = rows[j]
+        result[:256, :] = jnp.dot(mine_ref[...], right, preferred_element_type=F32)
+        result[256:, :] = jnp.dot(other_ref[...], right, preferred_element_type=F32)
+        for at in range(4):
+
+            @pl.when(j == at)
+            def _():
+                outs[at][:128, :] = result[:128, :]
+                outs[at][128:256, :] = result[256:384, :]
+
+        to = pl.multiple_of(j * 128, 128)
+        for a in range(2):
+            for b in range(2):
+                outs[4 + a * 2 + b][:, pl.ds(to, 128)] = result[
+                    a * 256 + 128 : a * 256 + 256, b * 128 : (b + 1) * 128
+                ]
+
+    for copy in gain_copies:
         copy.wait()
     if k == 0:
         total = jnp.zeros((16, 1024), F32)
@@ -132,29 +173,9 @@
             for j in range(4):
                 outs[j][at, to] = total[:, q * 128 : (q + 1) * 128]
 
-    @pl.loop(0, 4)
-    def _(j):
-        start = pl.multiple_of(j * 256, 256)
-        right = rows[:, pl.ds(start, 256)]
-        result[:256, :] = jnp.dot(mine_ref[...], right, preferred_element_type=F32)
-        result[256:, :] = jnp.dot(other_ref[...], right, preferred_element_type=F32)
-        for at in range(4):
-
-            @pl.when(j == at)
-            def _():
-                outs[at][:128, :] = result[:128, :]
-                outs[at][128:256, :] = result[256:384, :]
-
-        to = pl.multiple_of(j * 128, 128)
-        for a in range(2):
-            for b in range(2):
-                outs[4 + a * 2 + b][:, pl.ds(to, 128)] = result[
-                    a * 256 + 128 : a * 256 + 256, b * 128 : (b + 1) * 128
-                ]
-
 
 def product(k, mine, other, blocks):
-    scratch = [pltpu.VMEM((2048, 1024), BF16), pltpu.VMEM((512, 256), F32), pltpu.SemaphoreType.DMA((16,))]
+    scratch = [pltpu.VMEM((4, 2048, 256), BF16), pltpu.VMEM((512, 256), F32), pltpu.SemaphoreType.DMA((4, 16))]
     if k == 0:
         scratch += [pltpu.VMEM((16, 16, 1024), BF16), pltpu.SemaphoreType.DMA((16,))]
     return kernel_call(
@@ -196,7 +217,9 @@
 
 
 def cut_sum(kernel, parts, rows):
-    return kernel_call(kernel, [VMEM] * 8, [struct((rows, 256), F32)] * 4, 5, (1 << 18, 1 << 20), parts)
+    return kernel_call(
+        kernel, [VMEM] * 8, [struct((rows, 256), F32)] * 4, 5, (1 << 18, 1 << 20), parts
+    )
 
 
 def adam_kernel(scale, first_ref, second_ref, *refs):

time: 127 us -> 128 us (level)
  Pallas kernels: 10.3 us -> 12.3 us
    pallas_call x9, Pallas kernels: 10.3 us -> 12.3 us  [kernel_call(): pl.pallas_call(kernel, in_specs=in_specs, out_specs=[VMEM] * len(out_shap...]
  transfers between devices with their start and end apart: 49 -> 49, of which waited for: 13 -> 13; matrix products, arithmetic and copies ran while one was open for 2% -> 2% of each run, Pallas kernels for 7% -> 9%
where the time goes in v2:
time: 128 us
  starting transfers between devices  60.5 us (47%)
  waiting for transfers between devices  50.5 us (39%)
  Pallas kernels  12.3 us (10%)
  other arithmetic  2.82 us (2%)
    ppermute x35, starting transfers between devices, swap(): return lax.ppermute(array, axis, [(i, i ^ mask) for i in range(size)])  45.5 us
    ppermute x35, waiting for transfers between devices, swap(): return lax.ppermute(array, axis, [(i, i ^ mask) for i in range(size)])  28.4 us
    ppermute x14, waiting for transfers between devices, shift(): lax.ppermute(array, 'z', [(i, (i + step) % size) for i in range(size)])  22.1 us
    ppermute x14, starting transfers between devices, shift(): lax.ppermute(array, 'z', [(i, (i + step) % size) for i in range(size)])  15 us
    pallas_call x9, Pallas kernels, kernel_call(): pl.pallas_call(kernel, in_specs=in_specs, out_specs=[VMEM] * len(out_shap...  12.3 us
    reduce_sum x1, other arithmetic, update_of(): jnp.sum(norm_grad.astype(F32) * normed.astype(F32), axis=1).reshape(64, 128)  2.82 us
  transfers between devices with their start and end apart: 49, of which 13 were waited for; matrix products, arithmetic and copies ran while one was open for 2% of the time, Pallas kernels for 9%

profile of v2, /device:TPU:1, one launch (start us, length us, event | category | flops | bytes accessed | tf_op | source)
XLA Modules:
  0.0 128.1 jit_solution(9859188006618047732)
XLA Ops:
  1.8 3.3 %collective-permute-start.19 = (bf16[128,1024]{1,0:T(8,128)(2,1)S(1)}, bf16[128,1024]{1,0:T(8,128)(2,1)S(1)}, u32[]{:S(2)}, u32[]{:S(2)}) collective-permute-start(bf16[128,1024]{1,0:T(8,128)(2,1)S(1)} %shard_map.97.refs_0_), channel_id=1, source_target_pairs={{0,1},{1,0},{2,3},{3,2},{4,5},{5,4},{6,7},{7,6},{8,9},{9,8},{10,11... | collective-permute-start | bytes 786440 | tf_op jit(solution)/shard_map/ppermute | solution.py:39
  5.1 2.8 %multiply_reduce_fusion = f32[8192]{0:T(1024)S(1)} fusion(bf16[1,128,8192]{2,1,0:T(8,128)(2,1)} %param.8, bf16[1,128,8192]{2,1,0:T(8,128)(2,1)} %param.9), kind=kLoop, calls=%fused_computation | loop fusion | flops 4186112 | bytes 4227072 | tf_op jit(solution)/shard_map/reduce_sum | solution.py:257
  8.2 3.9 %collective-permute-start.22 = (bf16[128,1024]{1,0:T(8,128)(2,1)S(1)}, bf16[128,1024]{1,0:T(8,128)(2,1)S(1)}, u32[]{:S(2)}, u32[]{:S(2)}) collective-permute-start(bf16[128,1024]{1,0:T(8,128)(2,1)S(1)} %shard_map.97.refs_0_), channel_id=1, source_target_pairs={{0,14},{2,0},{4,2},{6,4},{8,6},{10,8},{12,10},{14,12},{1,15},{3,1}... | collective-permute-start | bytes 786440 | tf_op jit(solution)/shard_map/ppermute | solution.py:44
  12.2 2.7 %collective-permute-start.4 = (bf16[144,1024]{1,0:T(8,128)(2,1)S(1)}, bf16[144,1024]{1,0:T(8,128)(2,1)S(1)}, u32[]{:S(2)}, u32[]{:S(2)}) collective-permute-start(bf16[144,1024]{1,0:T(8,128)(2,1)S(1)} %shard_map.95.refs_0_), channel_id=1, source_target_pairs={{0,14},{2,0},{4,2},{6,4},{8,6},{10,8},{12,10},{14,12},{1,15},{3,1}... | collective-permute-start | bytes 884744 | tf_op jit(solution)/shard_map/ppermute | solution.py:44
  14.8 3.6 %collective-permute-done.20.refs_2_ = bf16[128,1024]{1,0:T(8,128)(2,1)S(1)} collective-permute-done((bf16[128,1024]{1,0:T(8,128)(2,1)S(1)}, bf16[128,1024]{1,0:T(8,128)(2,1)S(1)}, u32[]{:S(2)}, u32[]{:S(2)}) %collective-permute-start.20) | collective-permute-done | bytes 262176 | tf_op jit(solution)/shard_map/ppermute | solution.py:44
  20.0 4.7 %collective-permute-done.2.refs_2_ = bf16[144,1024]{1,0:T(8,128)(2,1)S(1)} collective-permute-done((bf16[144,1024]{1,0:T(8,128)(2,1)S(1)}, bf16[144,1024]{1,0:T(8,128)(2,1)S(1)}, u32[]{:S(2)}, u32[]{:S(2)}) %collective-permute-start.2) | collective-permute-done | bytes 294944 | tf_op jit(solution)/shard_map/ppermute | solution.py:44
  25.9 2.3 %collective-permute-start.3 = (bf16[144,1024]{1,0:T(8,128)(2,1)S(1)}, bf16[144,1024]{1,0:T(8,128)(2,1)S(1)}, u32[]{:S(2)}, u32[]{:S(2)}) collective-permute-start(bf16[144,1024]{1,0:T(8,128)(2,1)S(1)} %collective-permute-done.2.refs_2_), channel_id=1, source_target_pairs={{0,1},{1,0},{2,3},{3,2},{4,5},{5,4},{6,7},{7,6},{8,9},{9,8},{10,11... | collective-permute-start | bytes 884744 | tf_op jit(solution)/shard_map/ppermute | solution.py:39
  28.7 3.0 %collective-permute-start = (bf16[256,2048]{1,0:T(8,128)(2,1)S(1)}, bf16[256,2048]{1,0:T(8,128)(2,1)S(1)}, u32[]{:S(2)}, u32[]{:S(2)}) collective-permute-start(bf16[256,2048]{1,0:T(8,128)(2,1)S(1)} %shard_map.94), channel_id=1, source_target_pairs={{0,16},{16,0},{1,17},{17,1},{2,18},{18,2},{3,19},{19,3},{4,20},{20... | collective-permute-start | bytes 3145736 | tf_op jit(solution)/shard_map/ppermute | solution.py:39
  31.7 2.7 %collective-permute-start.8 = (bf16[144,1024]{1,0:T(8,128)(2,1)S(1)}, bf16[144,1024]{1,0:T(8,128)(2,1)S(1)}, u32[]{:S(2)}, u32[]{:S(2)}) collective-permute-start(bf16[144,1024]{1,0:T(8,128)(2,1)S(1)} %collective-permute-done.4.refs_4_), channel_id=1, source_target_pairs={{0,14},{2,0},{4,2},{6,4},{8,6},{10,8},{12,10},{14,12},{1,15},{3,1}... | collective-permute-start | bytes 884744 | tf_op jit(solution)/shard_map/ppermute | solution.py:44
  36.4 4.4 %collective-permute-done.6.refs_6_ = bf16[144,1024]{1,0:T(8,128)(2,1)S(1)} collective-permute-done((bf16[144,1024]{1,0:T(8,128)(2,1)S(1)}, bf16[144,1024]{1,0:T(8,128)(2,1)S(1)}, u32[]{:S(2)}, u32[]{:S(2)}) %collective-permute-start.6) | collective-permute-done | bytes 294944 | tf_op jit(solution)/shard_map/ppermute | solution.py:44
  43.8 3.4 %collective-permute-done.30.refs_12_ = bf16[128,1024]{1,0:T(8,128)(2,1)S(1)} collective-permute-done((bf16[128,1024]{1,0:T(8,128)(2,1)S(1)}, bf16[128,1024]{1,0:T(8,128)(2,1)S(1)}, u32[]{:S(2)}, u32[]{:S(2)}) %collective-permute-start.30) | collective-permute-done | bytes 262176 | tf_op jit(solution)/shard_map/ppermute | solution.py:44
  49.0 5.6 %collective-permute-done.28.refs_10_ = bf16[128,1024]{1,0:T(8,128)(2,1)S(1)} collective-permute-done((bf16[128,1024]{1,0:T(8,128)(2,1)S(1)}, bf16[128,1024]{1,0:T(8,128)(2,1)S(1)}, u32[]{:S(2)}, u32[]{:S(2)}) %collective-permute-start.28) | collective-permute-done | bytes 262176 | tf_op jit(solution)/shard_map/ppermute | solution.py:44
  54.7 4.4 %collective-permute-start.29 = (bf16[128,1024]{1,0:T(8,128)(2,1)S(1)}, bf16[128,1024]{1,0:T(8,128)(2,1)S(1)}, u32[]{:S(2)}, u32[]{:S(2)}) collective-permute-start(bf16[128,1024]{1,0:T(8,128)(2,1)S(1)} %collective-permute-done.28.refs_10_), channel_id=1, source_target_pairs={{0,1},{1,0},{2,3},{3,2},{4,5},{5,4},{6,7},{7,6},{8,9},{9,8},{10,11... | collective-permute-start | bytes 786440 | tf_op jit(solution)/shard_map/ppermute | solution.py:39
  59.1 2.4 %collective-permute-start.33 = (bf16[128,1024]{1,0:T(8,128)(2,1)S(1)}, bf16[128,1024]{1,0:T(8,128)(2,1)S(1)}, u32[]{:S(2)}, u32[]{:S(2)}) collective-permute-start(bf16[128,1024]{1,0:T(8,128)(2,1)S(1)} %collective-permute-done.32.refs_14_), channel_id=1, source_target_pairs={{0,1},{1,0},{2,3},{3,2},{4,5},{5,4},{6,7},{7,6},{8,9},{9,8},{10,11... | collective-permute-start | bytes 786440 | tf_op jit(solution)/shard_map/ppermute | solution.py:39
  63.8 4.5 %shard_map.98 = (f32[256,256]{1,0:T(8,128)S(1)}, f32[256,256]{1,0:T(8,128)S(1)}, f32[256,256]{1,0:T(8,128)S(1)}, f32[256,256]{1,0:T(8,128)S(1)}, f32[128,512]{1,...) custom-call(bf16[256,2048]{1,0:T(8,128)(2,1)S(1)} %shard_map.93.mine_ref, ...), custom_call_target="tpu_custom_call" | custom-call | flops 2147483648 | bytes 8388608 | tf_op jit(solution)/shard_map/pallas_call | solution.py:56
  73.5 5.6 %shard_map.96 = (f32[288,256]{1,0:T(8,128)S(1)}, f32[288,256]{1,0:T(8,128)S(1)}, f32[288,256]{1,0:T(8,128)S(1)}, f32[288,256]{1,0:T(8,128)S(1)}, f32[128,512]{1,...) custom-call(bf16[256,2048]{1,0:T(8,128)(2,1)S(1)} %shard_map.93.mine_ref, ...), custom_call_target="tpu_custom_call" | custom-call | flops 2147483648 | bytes 8388608 | tf_op jit(solution)/shard_map/pallas_call | solution.py:56
  83.2 2.5 %collective-permute-start.35 = (f32[256,256]{1,0:T(8,128)S(1)}, f32[256,256]{1,0:T(8,128)S(1)}, u32[]{:S(2)}, u32[]{:S(2)}) collective-permute-start(f32[256,256]{1,0:T(8,128)S(1)} %get-tuple-element.38), channel_id=1, source_target_pairs={{0,128},{64,192},{128,0},{192,64},{1,129},{65,193},{129,1},{193,65... | collective-permute-start | bytes 786440 | tf_op jit(solution)/shard_map/ppermute | solution.py:39
  85.6 2.3 %collective-permute-done.40.refs_1_ = f32[128,512]{1,0:T(8,128)S(1)} collective-permute-done((f32[128,512]{1,0:T(8,128)S(1)}, f32[128,512]{1,0:T(8,128)S(1)}, u32[]{:S(2)}, u32[]{:S(2)}) %collective-permute-start.40) | collective-permute-done | bytes 262176 | tf_op jit(solution)/shard_map/ppermute | solution.py:39
  88.0 2.5 %collective-permute-start.17 = (f32[288,256]{1,0:T(8,128)S(1)}, f32[288,256]{1,0:T(8,128)S(1)}, u32[]{:S(2)}, u32[]{:S(2)}) collective-permute-start(f32[288,256]{1,0:T(8,128)S(1)} %get-tuple-element.34), channel_id=1, source_target_pairs={{0,128},{64,192},{128,0},{192,64},{1,129},{65,193},{129,1},{193,65... | collective-permute-start | bytes 884744 | tf_op jit(solution)/shard_map/ppermute | solution.py:39
  90.4 4.0 %collective-permute-done.41.refs_2_ = f32[128,512]{1,0:T(8,128)S(1)} collective-permute-done((f32[128,512]{1,0:T(8,128)S(1)}, f32[128,512]{1,0:T(8,128)S(1)}, u32[]{:S(2)}, u32[]{:S(2)}) %collective-permute-start.41) | collective-permute-done | bytes 262176 | tf_op jit(solution)/shard_map/ppermute | solution.py:39
  99.2 15.2 %collective-permute-done.36.refs_7_ = f32[256,256]{1,0:T(8,128)S(1)} collective-permute-done((f32[256,256]{1,0:T(8,128)S(1)}, f32[256,256]{1,0:T(8,128)S(1)}, u32[]{:S(2)}, u32[]{:S(2)}) %collective-permute-start.36) | collective-permute-done | bytes 262176 | tf_op jit(solution)/shard_map/ppermute | solution.py:39
  114.6 2.7 %collective-permute-start.38 = (f32[160,256]{1,0:T(8,128)S(1)}, f32[160,256]{1,0:T(8,128)S(1)}, u32[]{:S(2)}, u32[]{:S(2)}) collective-permute-start(f32[160,256]{1,0:T(8,128)S(1)} %get-tuple-element.42), channel_id=1, source_target_pairs={{0,16},{16,0},{1,17},{17,1},{2,18},{18,2},{3,19},{19,3},{4,20},{20... | collective-permute-start | bytes 491528 | tf_op jit(solution)/shard_map/ppermute | solution.py:39
  120.8 3.2 %collective-permute-done.47.refs_6_ = f32[128,256]{1,0:T(8,128)S(1)} collective-permute-done((f32[128,256]{1,0:T(8,128)S(1)}, f32[128,256]{1,0:T(8,128)S(1)}, u32[]{:S(2)}, u32[]{:S(2)}) %collective-permute-start.47) | collective-permute-done | bytes 131104 | tf_op jit(solution)/shard_map/ppermute | solution.py:39
  124.1 3.0 %collective-permute-done.48.refs_7_ = f32[128,256]{1,0:T(8,128)S(1)} collective-permute-done((f32[128,256]{1,0:T(8,128)S(1)}, f32[128,256]{1,0:T(8,128)S(1)}, u32[]{:S(2)}, u32[]{:S(2)}) %collective-permute-start.48) | collective-permute-done | bytes 131104 | tf_op jit(solution)/shard_map/ppermute | solution.py:39
  (94 shorter events, 32.5 us)
Async XLA Ops:
  8.0 11.9 %collective-permute-start.1 = (bf16[144,1024]{1,0:T(8,128)(2,1)S(1)}, bf16[144,1024]{1,0:T(8,128)(2,1)S(1)}, u32[]{:S(2)}, u32[]{:S(2)}) collective-permute-start(bf16[144,1024]{1,0:T(8,128)(2,1)S(1)} %shard_map.95.refs_0_), channel_id=1, source_target_pairs={{0,1},{1,0},{2,3},{3,2},{4,5},{5,4},{6,7},{7,6},{8,9},{9,8},{10,11... | collective-permute-start | bytes 884744 | tf_op jit(solution)/shard_map/ppermute | solution.py:39
  8.2 11.7 %collective-permute-start.22 = (bf16[128,1024]{1,0:T(8,128)(2,1)S(1)}, bf16[128,1024]{1,0:T(8,128)(2,1)S(1)}, u32[]{:S(2)}, u32[]{:S(2)}) collective-permute-start(bf16[128,1024]{1,0:T(8,128)(2,1)S(1)} %shard_map.97.refs_0_), channel_id=1, source_target_pairs={{0,14},{2,0},{4,2},{6,4},{8,6},{10,8},{12,10},{14,12},{1,15},{3,1}... | collective-permute-start | bytes 786440 | tf_op jit(solution)/shard_map/ppermute | solution.py:44
  12.2 12.6 %collective-permute-start.2 = (bf16[144,1024]{1,0:T(8,128)(2,1)S(1)}, bf16[144,1024]{1,0:T(8,128)(2,1)S(1)}, u32[]{:S(2)}, u32[]{:S(2)}) collective-permute-start(bf16[144,1024]{1,0:T(8,128)(2,1)S(1)} %shard_map.95.refs_0_), channel_id=1, source_target_pairs={{0,2},{2,4},{4,6},{6,8},{8,10},{10,12},{12,14},{14,0},{1,3},{3,5},... | collective-permute-start | bytes 884744 | tf_op jit(solution)/shard_map/ppermute | solution.py:44
  12.2 13.8 %collective-permute-start.4 = (bf16[144,1024]{1,0:T(8,128)(2,1)S(1)}, bf16[144,1024]{1,0:T(8,128)(2,1)S(1)}, u32[]{:S(2)}, u32[]{:S(2)}) collective-permute-start(bf16[144,1024]{1,0:T(8,128)(2,1)S(1)} %shard_map.95.refs_0_), channel_id=1, source_target_pairs={{0,14},{2,0},{4,2},{6,4},{8,6},{10,8},{12,10},{14,12},{1,15},{3,1}... | collective-permute-start | bytes 884744 | tf_op jit(solution)/shard_map/ppermute | solution.py:44
  19.9 11.8 %collective-permute-start.24 = (bf16[128,1024]{1,0:T(8,128)(2,1)S(1)}, bf16[128,1024]{1,0:T(8,128)(2,1)S(1)}, u32[]{:S(2)}, u32[]{:S(2)}) collective-permute-start(bf16[128,1024]{1,0:T(8,128)(2,1)S(1)} %collective-permute-done.20.refs_2_), channel_id=1, source_target_pairs={{0,2},{2,4},{4,6},{6,8},{8,10},{10,12},{12,14},{14,0},{1,3},{3,5},... | collective-permute-start | bytes 786440 | tf_op jit(solution)/shard_map/ppermute | solution.py:44
  28.7 32.7 %collective-permute-start = (bf16[256,2048]{1,0:T(8,128)(2,1)S(1)}, bf16[256,2048]{1,0:T(8,128)(2,1)S(1)}, u32[]{:S(2)}, u32[]{:S(2)}) collective-permute-start(bf16[256,2048]{1,0:T(8,128)(2,1)S(1)} %shard_map.94), channel_id=1, source_target_pairs={{0,16},{16,0},{1,17},{17,1},{2,18},{18,2},{3,19},{19,3},{4,20},{20... | collective-permute-start | bytes 3145736 | tf_op jit(solution)/shard_map/ppermute | solution.py:39
  42.3 16.8 %collective-permute-start.12 = (bf16[144,1024]{1,0:T(8,128)(2,1)S(1)}, bf16[144,1024]{1,0:T(8,128)(2,1)S(1)}, u32[]{:S(2)}, u32[]{:S(2)}) collective-permute-start(bf16[144,1024]{1,0:T(8,128)(2,1)S(1)} %collective-permute-done.8.refs_8_), channel_id=1, source_target_pairs={{0,14},{2,0},{4,2},{6,4},{8,6},{10,8},{12,10},{14,12},{1,15},{3,1}... | collective-permute-start | bytes 884744 | tf_op jit(solution)/shard_map/ppermute | solution.py:44
  43.5 11.2 %collective-permute-start.28 = (bf16[128,1024]{1,0:T(8,128)(2,1)S(1)}, bf16[128,1024]{1,0:T(8,128)(2,1)S(1)}, u32[]{:S(2)}, u32[]{:S(2)}) collective-permute-start(bf16[128,1024]{1,0:T(8,128)(2,1)S(1)} %collective-permute-done.24.refs_6_), channel_id=1, source_target_pairs={{0,2},{2,4},{4,6},{6,8},{8,10},{10,12},{12,14},{14,0},{1,3},{3,5},... | collective-permute-start | bytes 786440 | tf_op jit(solution)/shard_map/ppermute | solution.py:44
  47.1 12.0 %collective-permute-start.32 = (bf16[128,1024]{1,0:T(8,128)(2,1)S(1)}, bf16[128,1024]{1,0:T(8,128)(2,1)S(1)}, u32[]{:S(2)}, u32[]{:S(2)}) collective-permute-start(bf16[128,1024]{1,0:T(8,128)(2,1)S(1)} %collective-permute-done.30.refs_12_), channel_id=1, source_target_pairs={{0,14},{2,0},{4,2},{6,4},{8,6},{10,8},{12,10},{14,12},{1,15},{3,1}... | collective-permute-start | bytes 786440 | tf_op jit(solution)/shard_map/ppermute | solution.py:44
  49.0 13.0 %collective-permute-start.14 = (bf16[144,1024]{1,0:T(8,128)(2,1)S(1)}, bf16[144,1024]{1,0:T(8,128)(2,1)S(1)}, u32[]{:S(2)}, u32[]{:S(2)}) collective-permute-start(bf16[144,1024]{1,0:T(8,128)(2,1)S(1)} %collective-permute-done.10.refs_10_), channel_id=1, source_target_pairs={{0,2},{2,4},{4,6},{6,8},{8,10},{10,12},{12,14},{14,0},{1,3},{3,5},... | collective-permute-start | bytes 884744 | tf_op jit(solution)/shard_map/ppermute | solution.py:44
  68.3 10.9 %collective-permute-start.34 = (f32[256,256]{1,0:T(8,128)S(1)}, f32[256,256]{1,0:T(8,128)S(1)}, u32[]{:S(2)}, u32[]{:S(2)}) collective-permute-start(f32[256,256]{1,0:T(8,128)S(1)} %get-tuple-element.37), channel_id=1, source_target_pairs={{0,64},{64,0},{128,192},{192,128},{1,65},{65,1},{129,193},{193,129... | collective-permute-start | bytes 786440 | tf_op jit(solution)/shard_map/ppermute | solution.py:39
  69.6 11.9 %collective-permute-start.43 = (f32[128,512]{1,0:T(8,128)S(1)}, f32[128,512]{1,0:T(8,128)S(1)}, u32[]{:S(2)}, u32[]{:S(2)}) collective-permute-start(f32[128,512]{1,0:T(8,128)S(1)} %get-tuple-element.49), channel_id=1, source_target_pairs={{0,32},{32,0},{1,33},{33,1},{2,34},{34,2},{3,35},{35,3},{4,36},{36... | collective-permute-start | bytes 786440 | tf_op jit(solution)/shard_map/ppermute | solution.py:39
  70.0 13.2 %collective-permute-start.44 = (f32[128,512]{1,0:T(8,128)S(1)}, f32[128,512]{1,0:T(8,128)S(1)}, u32[]{:S(2)}, u32[]{:S(2)}) collective-permute-start(f32[128,512]{1,0:T(8,128)S(1)} %get-tuple-element.50), channel_id=1, source_target_pairs={{0,16},{16,0},{1,17},{17,1},{2,18},{18,2},{3,19},{19,3},{4,20},{20... | collective-permute-start | bytes 786440 | tf_op jit(solution)/shard_map/ppermute | solution.py:39
  71.9 13.7 %collective-permute-start.45 = (f32[128,512]{1,0:T(8,128)S(1)}, f32[128,512]{1,0:T(8,128)S(1)}, u32[]{:S(2)}, u32[]{:S(2)}) collective-permute-start(f32[128,512]{1,0:T(8,128)S(1)} %get-tuple-element.51), channel_id=1, source_target_pairs={{0,48},{16,32},{32,16},{48,0},{1,49},{17,33},{33,17},{49,1},{2,50}... | collective-permute-start | bytes 786440 | tf_op jit(solution)/shard_map/ppermute | solution.py:39
  79.3 15.2 %collective-permute-start.41 = (f32[128,512]{1,0:T(8,128)S(1)}, f32[128,512]{1,0:T(8,128)S(1)}, u32[]{:S(2)}, u32[]{:S(2)}) collective-permute-start(f32[128,512]{1,0:T(8,128)S(1)} %get-tuple-element.46), channel_id=1, source_target_pairs={{0,16},{16,0},{1,17},{17,1},{2,18},{18,2},{3,19},{19,3},{4,20},{20... | collective-permute-start | bytes 786440 | tf_op jit(solution)/shard_map/ppermute | solution.py:39
  81.5 15.3 %collective-permute-start.42 = (f32[128,512]{1,0:T(8,128)S(1)}, f32[128,512]{1,0:T(8,128)S(1)}, u32[]{:S(2)}, u32[]{:S(2)}) collective-permute-start(f32[128,512]{1,0:T(8,128)S(1)} %get-tuple-element.47), channel_id=1, source_target_pairs={{0,48},{16,32},{32,16},{48,0},{1,49},{17,33},{33,17},{49,1},{2,50}... | collective-permute-start | bytes 786440 | tf_op jit(solution)/shard_map/ppermute | solution.py:39
  83.2 15.6 %collective-permute-start.35 = (f32[256,256]{1,0:T(8,128)S(1)}, f32[256,256]{1,0:T(8,128)S(1)}, u32[]{:S(2)}, u32[]{:S(2)}) collective-permute-start(f32[256,256]{1,0:T(8,128)S(1)} %get-tuple-element.38), channel_id=1, source_target_pairs={{0,128},{64,192},{128,0},{192,64},{1,129},{65,193},{129,1},{193,65... | collective-permute-start | bytes 786440 | tf_op jit(solution)/shard_map/ppermute | solution.py:39
  85.6 28.7 %collective-permute-start.16 = (f32[288,256]{1,0:T(8,128)S(1)}, f32[288,256]{1,0:T(8,128)S(1)}, u32[]{:S(2)}, u32[]{:S(2)}) collective-permute-start(f32[288,256]{1,0:T(8,128)S(1)} %get-tuple-element.33), channel_id=1, source_target_pairs={{0,64},{64,0},{128,192},{192,128},{1,65},{65,1},{129,193},{193,129... | collective-permute-start | bytes 884744 | tf_op jit(solution)/shard_map/ppermute | solution.py:39
  88.0 26.4 %collective-permute-start.17 = (f32[288,256]{1,0:T(8,128)S(1)}, f32[288,256]{1,0:T(8,128)S(1)}, u32[]{:S(2)}, u32[]{:S(2)}) collective-permute-start(f32[288,256]{1,0:T(8,128)S(1)} %get-tuple-element.34), channel_id=1, source_target_pairs={{0,128},{64,192},{128,0},{192,64},{1,129},{65,193},{129,1},{193,65... | collective-permute-start | bytes 884744 | tf_op jit(solution)/shard_map/ppermute | solution.py:39
  94.5 19.9 %collective-permute-start.18 = (f32[288,256]{1,0:T(8,128)S(1)}, f32[288,256]{1,0:T(8,128)S(1)}, u32[]{:S(2)}, u32[]{:S(2)}) collective-permute-start(f32[288,256]{1,0:T(8,128)S(1)} %get-tuple-element.35), channel_id=1, source_target_pairs={{0,192},{64,128},{128,64},{192,0},{1,193},{65,129},{129,65},{193,1... | collective-permute-start | bytes 884744 | tf_op jit(solution)/shard_map/ppermute | solution.py:39
  96.8 17.6 %collective-permute-start.36 = (f32[256,256]{1,0:T(8,128)S(1)}, f32[256,256]{1,0:T(8,128)S(1)}, u32[]{:S(2)}, u32[]{:S(2)}) collective-permute-start(f32[256,256]{1,0:T(8,128)S(1)} %get-tuple-element.39), channel_id=1, source_target_pairs={{0,192},{64,128},{128,64},{192,0},{1,193},{65,129},{129,65},{193,1... | collective-permute-start | bytes 786440 | tf_op jit(solution)/shard_map/ppermute | solution.py:39
  98.8 21.5 %collective-permute-start.46 = (f32[128,256]{1,0:T(8,128)S(1)}, f32[128,256]{1,0:T(8,128)S(1)}, u32[]{:S(2)}, u32[]{:S(2)}) collective-permute-start(f32[128,256]{1,0:T(8,128)S(1)} %get-tuple-element.53), channel_id=1, source_target_pairs={{0,64},{64,0},{128,192},{192,128},{1,65},{65,1},{129,193},{193,129... | collective-permute-start | bytes 393224 | tf_op jit(solution)/shard_map/ppermute | solution.py:39
  114.5 12.5 %collective-permute-start.37 = (f32[160,256]{1,0:T(8,128)S(1)}, f32[160,256]{1,0:T(8,128)S(1)}, u32[]{:S(2)}, u32[]{:S(2)}) collective-permute-start(f32[160,256]{1,0:T(8,128)S(1)} %get-tuple-element.41), channel_id=1, source_target_pairs={{0,32},{32,0},{1,33},{33,1},{2,34},{34,2},{3,35},{35,3},{4,36},{36... | collective-permute-start | bytes 491528 | tf_op jit(solution)/shard_map/ppermute | solution.py:39
  114.6 12.4 %collective-permute-start.38 = (f32[160,256]{1,0:T(8,128)S(1)}, f32[160,256]{1,0:T(8,128)S(1)}, u32[]{:S(2)}, u32[]{:S(2)}) collective-permute-start(f32[160,256]{1,0:T(8,128)S(1)} %get-tuple-element.42), channel_id=1, source_target_pairs={{0,16},{16,0},{1,17},{17,1},{2,18},{18,2},{3,19},{19,3},{4,20},{20... | collective-permute-start | bytes 491528 | tf_op jit(solution)/shard_map/ppermute | solution.py:39
  (30 other events, 289.0 us)

commit v3 on v1

--- a/solution.py
+++ b/solution.py
@@ -102,29 +102,74 @@
     )[0]
 
 
-def product_kernel(k, mine_ref, other_ref, *refs):
-    blocks, outs = refs[:16], refs[16:24]
-    rows, result, sems = refs[24:27]
+def part_kernel(k, mine_ref, other_ref, *refs):
+    blocks, outs, refs = refs[:14], refs[14:22], refs[22:]
+    if k == 0:
+        gains_ref, refs = refs[0], refs[1:]
+    rows, result, sems = refs[:3]
     copies = [
         pltpu.make_async_copy(block.at[pl.ds(0, 128), :], rows.at[pl.ds(i * 128, 128), :], sems.at[i])
         for i, block in enumerate(blocks)
     ]
     if k == 0:
-        gains, gain_sems = refs[27:]
-        z, c = lax.axis_index("z"), lax.axis_index("c")
         for i, block in enumerate(blocks):
-            source = ((z + STEPS[i // 2] + 8) % 8) * 2 + (c ^ (i % 2))
             copies.append(
-                pltpu.make_async_copy(block.at[pl.ds(128, 16), :], gains.at[source], gain_sems.at[i])
+                pltpu.make_async_copy(block.at[pl.ds(128, 16), :], gains_ref.at[source_of(i)], refs[3].at[i])
             )
     for copy in copies:
         copy.start()
     for copy in copies:
         copy.wait()
-    if k == 0:
+
+    @pl.loop(0, 4)
+    def _(j):
+        right = rows[:, pl.ds(pl.multiple_of(j * 256, 256), 256)]
+        result[:256, :] = jnp.dot(mine_ref[:, :1792], right, preferred_element_type=F32)
+        result[256:, :] = jnp.dot(other_ref[:, :1792], right, preferred_element_type=F32)
+        for at in range(4):
+
+            @pl.when(j == at)
+            def _():
+                outs[at][:128, :] = result[:128, :]
+                outs[at][128:256, :] = result[256:384, :]
+
+        to = pl.multiple_of(j * 128, 128)
+        for a in range(2):
+            for b in range(2):
+                outs[4 + a * 2 + b][:, pl.ds(to, 128)] = result[
+                    a * 256 + 128 : a * 256 + 256, b * 128 : (b + 1) * 128
+                ]
+
+
+def source_of(i):
+    z, c = lax.axis_index("z"), lax.axis_index("c")
+    return ((z + STEPS[i // 2] + 8) % 8) * 2 + (c ^ (i % 2))
+
+
+def product_kernel(k, mine_ref, other_ref, own_ref, swapped_ref, *refs):
+    parts, refs = refs[:8], refs[8:]
+    if k == 0:
+        gains_ref, refs = refs[0], refs[1:]
+    outs = refs
+    for j in range(4):
+        columns = slice(j * 256, (j + 1) * 256)
+        right = jnp.concatenate([own_ref[:128, columns], swapped_ref[:128, columns]], axis=0)
+        for a, left in enumerate((mine_ref, other_ref)):
+            result = jnp.dot(left[:, 1792:], right, preferred_element_type=F32)
+            at = slice(a * 128, (a + 1) * 128)
+            outs[j][at, :] = parts[j][at, :] + result[:128]
+            for b in range(2):
+                to = slice(j * 128, (j + 1) * 128)
+                piece = 4 + a * 2 + b
+                outs[piece][:, to] = parts[piece][:, to] + result[128:, b * 128 : (b + 1) * 128]
+    if k == 0:
+        late = [(source_of(14), own_ref[128:144, :].astype(F32)), (source_of(15), swapped_ref[128:144, :].astype(F32))]
         total = jnp.zeros((16, 1024), F32)
         for i in range(16):
-            total = total + gains[i].astype(F32)
+            value = gains_ref[i].astype(F32)
+            for source, here in late:
+                value = jnp.where(source == i, here, value)
+            total = total + value
         total = total[:8] + total[8:]
         for q in range(8):
             at = slice(256 + (q % 4) * 8, 264 + (q % 4) * 8)
@@ -132,39 +177,30 @@
             for j in range(4):
                 outs[j][at, to] = total[:, q * 128 : (q + 1) * 128]
 
-    @pl.loop(0, 4)
-    def _(j):
-        start = pl.multiple_of(j * 256, 256)
-        right = rows[:, pl.ds(start, 256)]
-        result[:256, :] = jnp.dot(mine_ref[...], right, preferred_element_type=F32)
-        result[256:, :] = jnp.dot(other_ref[...], right, preferred_element_type=F32)
-        for at in range(4):
-
-            @pl.when(j == at)
-            def _():
-                outs[at][:128, :] = result[:128, :]
-                outs[at][128:256, :] = result[256:384, :]
-
-        to = pl.multiple_of(j * 128, 128)
-        for a in range(2):
-            for b in range(2):
-                outs[4 + a * 2 + b][:, pl.ds(to, 128)] = result[
-                    a * 256 + 128 : a * 256 + 256, b * 128 : (b + 1) * 128
-                ]
-
 
 def product(k, mine, other, blocks):
-    scratch = [pltpu.VMEM((2048, 1024), BF16), pltpu.VMEM((512, 256), F32), pltpu.SemaphoreType.DMA((16,))]
-    if k == 0:
-        scratch += [pltpu.VMEM((16, 16, 1024), BF16), pltpu.SemaphoreType.DMA((16,))]
+    pieces = [struct((128, 512), F32)] * 4
+    scratch = [pltpu.VMEM((1792, 1024), BF16), pltpu.VMEM((512, 256), F32), pltpu.SemaphoreType.DMA((14,))]
+    gains = []
+    if k == 0:
+        scratch += [pltpu.SemaphoreType.DMA((14,))]
+        gains = [struct((16, 16, 1024), BF16)]
+    parts = kernel_call(
+        functools.partial(part_kernel, k),
+        [VMEM, VMEM] + [ANY] * 14,
+        [struct((256, 256), F32)] * 4 + pieces + gains,
+        14,
+        (2 * 512 * 1792 * 1024, 8 << 20),
+        [mine, other, *blocks[:14]],
+        scratch,
+    )
     return kernel_call(
         functools.partial(product_kernel, k),
-        [VMEM, VMEM] + [ANY] * 16,
-        [struct((288 if k == 0 else 256, 256), F32)] * 4 + [struct((128, 512), F32)] * 4,
+        [VMEM] * (4 + len(parts)),
+        [struct((288 if k == 0 else 256, 256), F32)] * 4 + pieces,
         14,
-        (2 * 512 * 2048 * 1024, 8 << 20),
-        [mine, other, *blocks],
-        scratch,
+        (2 * 512 * 256 * 1024, 4 << 20),
+        [mine, other, *blocks[14:], *parts],
     )
 
 

time: 127 us -> 132 us (1.039); the launches traced: 127 us -> 130 us
  starting transfers between devices: 60.5 us -> 62.4 us
    ppermute x14, starting transfers between devices: 15 us -> 19.3 us  [shift(): lax.ppermute(array, 'z', [(i, (i + step) % size) for i in range(size)])]
    ppermute x14, waiting for transfers between devices: 22.1 us -> 25.5 us  [shift(): lax.ppermute(array, 'z', [(i, (i + step) % size) for i in range(size)])]
    ppermute x35, waiting for transfers between devices: 29.4 us -> 26.8 us  [swap(): return lax.ppermute(array, axis, [(i, i ^ mask) for i in range(size)])]
    ppermute x35, starting transfers between devices: 45.5 us -> 43.1 us  [swap(): return lax.ppermute(array, axis, [(i, i ^ mask) for i in range(size)])]
    pallas_call x9 -> x11, Pallas kernels: 10.3 us -> 10.6 us  [kernel_call(): pl.pallas_call(kernel, in_specs=in_specs, out_specs=[VMEM] * len(out_shap...]
  transfers between devices with their start and end apart: 49 -> 49, of which waited for: 13 -> 18; matrix products, arithmetic and copies ran while one was open for 2% -> 2% of each run, Pallas kernels for 7% -> 7%
where the time goes in v3:
time: 132 us; the launch traced here: 130 us
  starting transfers between devices  62.4 us (47%)
  waiting for transfers between devices  52.3 us (40%)
  Pallas kernels  10.6 us (8%)
  other arithmetic  2.83 us (2%)
    ppermute x35, starting transfers between devices, swap(): return lax.ppermute(array, axis, [(i, i ^ mask) for i in range(size)])  43.1 us
    ppermute x35, waiting for transfers between devices, swap(): return lax.ppermute(array, axis, [(i, i ^ mask) for i in range(size)])  26.8 us
    ppermute x14, waiting for transfers between devices, shift(): lax.ppermute(array, 'z', [(i, (i + step) % size) for i in range(size)])  25.5 us
    ppermute x14, starting transfers between devices, shift(): lax.ppermute(array, 'z', [(i, (i + step) % size) for i in range(size)])  19.3 us
    pallas_call x11, Pallas kernels, kernel_call(): pl.pallas_call(kernel, in_specs=in_specs, out_specs=[VMEM] * len(out_shap...  10.6 us
    reduce_sum x1, other arithmetic, update_of(): jnp.sum(norm_grad.astype(F32) * normed.astype(F32), axis=1).reshape(64, 128)  2.83 us
  transfers between devices with their start and end apart: 49, of which 18 were waited for; matrix products, arithmetic and copies ran while one was open for 2% of the time, Pallas kernels for 7%

profile of v3, /device:TPU:1, one launch (start us, length us, event | category | flops | bytes accessed | tf_op | source)
XLA Modules:
  0.0 130.1 jit_solution(14811342789530357515)
XLA Ops:
  1.8 6.5 %collective-permute-start.19 = (bf16[128,1024]{1,0:T(8,128)(2,1)S(1)}, bf16[128,1024]{1,0:T(8,128)(2,1)S(1)}, u32[]{:S(2)}, u32[]{:S(2)}) collective-permute-start(bf16[128,1024]{1,0:T(8,128)(2,1)S(1)} %shard_map.98.refs_0_), channel_id=1, source_target_pairs={{0,14},{2,0},{4,2},{6,4},{8,6},{10,8},{12,10},{14,12},{1,15},{3,1}... | collective-permute-start | bytes 786440 | tf_op jit(solution)/shard_map/ppermute | solution.py:44
  9.2 2.8 %multiply_reduce_fusion = f32[8192]{0:T(1024)S(1)} fusion(bf16[1,128,8192]{2,1,0:T(8,128)(2,1)} %param.8, bf16[1,128,8192]{2,1,0:T(8,128)(2,1)} %param.9), kind=kLoop, calls=%fused_computation | loop fusion | flops 4186112 | bytes 4227072 | tf_op jit(solution)/shard_map/reduce_sum | solution.py:270
  13.2 3.4 %collective-permute-start.8 = (bf16[144,1024]{1,0:T(8,128)(2,1)S(1)}, bf16[144,1024]{1,0:T(8,128)(2,1)S(1)}, u32[]{:S(2)}, u32[]{:S(2)}) collective-permute-start(bf16[144,1024]{1,0:T(8,128)(2,1)S(1)} %shard_map.95.refs_0_), channel_id=1, source_target_pairs={{0,14},{2,0},{4,2},{6,4},{8,6},{10,8},{12,10},{14,12},{1,15},{3,1}... | collective-permute-start | bytes 884744 | tf_op jit(solution)/shard_map/ppermute | solution.py:44
  19.6 5.0 %collective-permute-done.1.refs_2_ = bf16[144,1024]{1,0:T(8,128)(2,1)S(1)} collective-permute-done((bf16[144,1024]{1,0:T(8,128)(2,1)S(1)}, bf16[144,1024]{1,0:T(8,128)(2,1)S(1)}, u32[]{:S(2)}, u32[]{:S(2)}) %collective-permute-start.1) | collective-permute-done | bytes 294944 | tf_op jit(solution)/shard_map/ppermute | solution.py:44
  27.1 2.4 %collective-permute-start.7 = (bf16[144,1024]{1,0:T(8,128)(2,1)S(1)}, bf16[144,1024]{1,0:T(8,128)(2,1)S(1)}, u32[]{:S(2)}, u32[]{:S(2)}) collective-permute-start(bf16[144,1024]{1,0:T(8,128)(2,1)S(1)} %collective-permute-done.1.refs_2_), channel_id=1, source_target_pairs={{0,1},{1,0},{2,3},{3,2},{4,5},{5,4},{6,7},{7,6},{8,9},{9,8},{10,11... | collective-permute-start | bytes 884744 | tf_op jit(solution)/shard_map/ppermute | solution.py:39
  29.9 3.0 %collective-permute-start = (bf16[256,2048]{1,0:T(8,128)(2,1)S(1)}, bf16[256,2048]{1,0:T(8,128)(2,1)S(1)}, u32[]{:S(2)}, u32[]{:S(2)}) collective-permute-start(bf16[256,2048]{1,0:T(8,128)(2,1)S(1)} %shard_map.94), channel_id=1, source_target_pairs={{0,16},{16,0},{1,17},{17,1},{2,18},{18,2},{3,19},{19,3},{4,20},{20... | collective-permute-start | bytes 3145736 | tf_op jit(solution)/shard_map/ppermute | solution.py:39
  36.6 4.3 %collective-permute-done.2.refs_6_ = bf16[144,1024]{1,0:T(8,128)(2,1)S(1)} collective-permute-done((bf16[144,1024]{1,0:T(8,128)(2,1)S(1)}, bf16[144,1024]{1,0:T(8,128)(2,1)S(1)}, u32[]{:S(2)}, u32[]{:S(2)}) %collective-permute-start.2) | collective-permute-done | bytes 294944 | tf_op jit(solution)/shard_map/ppermute | solution.py:44
  43.6 4.8 %collective-permute-done.21.refs_12_ = bf16[128,1024]{1,0:T(8,128)(2,1)S(1)} collective-permute-done((bf16[128,1024]{1,0:T(8,128)(2,1)S(1)}, bf16[128,1024]{1,0:T(8,128)(2,1)S(1)}, u32[]{:S(2)}, u32[]{:S(2)}) %collective-permute-start.21) | collective-permute-done | bytes 262176 | tf_op jit(solution)/shard_map/ppermute | solution.py:44
  48.3 3.4 %collective-permute-start.14 = (bf16[144,1024]{1,0:T(8,128)(2,1)S(1)}, bf16[144,1024]{1,0:T(8,128)(2,1)S(1)}, u32[]{:S(2)}, u32[]{:S(2)}) collective-permute-start(bf16[144,1024]{1,0:T(8,128)(2,1)S(1)} %collective-permute-done.11.refs_8_), channel_id=1, source_target_pairs={{0,14},{2,0},{4,2},{6,4},{8,6},{10,8},{12,10},{14,12},{1,15},{3,1}... | collective-permute-start | bytes 884744 | tf_op jit(solution)/shard_map/ppermute | solution.py:44
  51.7 2.7 %collective-permute-start.22 = (bf16[128,1024]{1,0:T(8,128)(2,1)S(1)}, bf16[128,1024]{1,0:T(8,128)(2,1)S(1)}, u32[]{:S(2)}, u32[]{:S(2)}) collective-permute-start(bf16[128,1024]{1,0:T(8,128)(2,1)S(1)} %collective-permute-done.21.refs_12_), channel_id=1, source_target_pairs={{0,14},{2,0},{4,2},{6,4},{8,6},{10,8},{12,10},{14,12},{1,15},{3,1}... | collective-permute-start | bytes 786440 | tf_op jit(solution)/shard_map/ppermute | solution.py:44
  54.4 5.0 %collective-permute-done.31.refs_10_ = bf16[128,1024]{1,0:T(8,128)(2,1)S(1)} collective-permute-done((bf16[128,1024]{1,0:T(8,128)(2,1)S(1)}, bf16[128,1024]{1,0:T(8,128)(2,1)S(1)}, u32[]{:S(2)}, u32[]{:S(2)}) %collective-permute-start.31) | collective-permute-done | bytes 262176 | tf_op jit(solution)/shard_map/ppermute | solution.py:44
  59.4 4.0 %collective-permute-start.32 = (bf16[128,1024]{1,0:T(8,128)(2,1)S(1)}, bf16[128,1024]{1,0:T(8,128)(2,1)S(1)}, u32[]{:S(2)}, u32[]{:S(2)}) collective-permute-start(bf16[128,1024]{1,0:T(8,128)(2,1)S(1)} %collective-permute-done.31.refs_10_), channel_id=1, source_target_pairs={{0,1},{1,0},{2,3},{3,2},{4,5},{5,4},{6,7},{7,6},{8,9},{9,8},{10,11... | collective-permute-start | bytes 786440 | tf_op jit(solution)/shard_map/ppermute | solution.py:39
  65.8 2.2 %collective-permute-start.15 = (bf16[144,1024]{1,0:T(8,128)(2,1)S(1)}, bf16[144,1024]{1,0:T(8,128)(2,1)S(1)}, u32[]{:S(2)}, u32[]{:S(2)}) collective-permute-start(bf16[144,1024]{1,0:T(8,128)(2,1)S(1)} %collective-permute-done.14.refs_12_), channel_id=1, source_target_pairs={{0,1},{1,0},{2,3},{3,2},{4,5},{5,4},{6,7},{7,6},{8,9},{9,8},{10,11... | collective-permute-start | bytes 884744 | tf_op jit(solution)/shard_map/ppermute | solution.py:39
  68.5 3.2 %shard_map.99 = (f32[256,256]{1,0:T(8,128)S(1)}, f32[256,256]{1,0:T(8,128)S(1)}, f32[256,256]{1,0:T(8,128)S(1)}, f32[256,256]{1,0:T(8,128)S(1)}, f32[128,512]{1,...) custom-call(bf16[256,2048]{1,0:T(8,128)(2,1)S(1)} %shard_map.93.mine_ref, ...), custom_call_target="tpu_custom_call" | custom-call | flops 1879048192 | bytes 8388608 | tf_op jit(solution)/shard_map/pallas_call | solution.py:56
  75.2 4.1 %shard_map.96 = (f32[256,256]{1,0:T(8,128)S(1)}, f32[256,256]{1,0:T(8,128)S(1)}, f32[256,256]{1,0:T(8,128)S(1)}, f32[256,256]{1,0:T(8,128)S(1)}, f32[128,512]{1,...) custom-call(bf16[256,2048]{1,0:T(8,128)(2,1)S(1)} %shard_map.93.mine, ...), custom_call_target="tpu_custom_call" | custom-call | flops 1879048192 | bytes 8388608 | tf_op jit(solution)/shard_map/pallas_call | solution.py:56
  79.3 2.3 %collective-permute-start.45 = (f32[128,512]{1,0:T(8,128)S(1)}, f32[128,512]{1,0:T(8,128)S(1)}, u32[]{:S(2)}, u32[]{:S(2)}) collective-permute-start(f32[128,512]{1,0:T(8,128)S(1)} %get-tuple-element.85), channel_id=1, source_target_pairs={{0,48},{16,32},{32,16},{48,0},{1,49},{17,33},{33,17},{49,1},{2,50}... | collective-permute-start | bytes 786440 | tf_op jit(solution)/shard_map/ppermute | solution.py:39
  84.0 2.2 %collective-permute-start.42 = (f32[128,512]{1,0:T(8,128)S(1)}, f32[128,512]{1,0:T(8,128)S(1)}, u32[]{:S(2)}, u32[]{:S(2)}) collective-permute-start(f32[128,512]{1,0:T(8,128)S(1)} %get-tuple-element.81), channel_id=1, source_target_pairs={{0,48},{16,32},{32,16},{48,0},{1,49},{17,33},{33,17},{49,1},{2,50}... | collective-permute-start | bytes 786440 | tf_op jit(solution)/shard_map/ppermute | solution.py:39
  86.5 2.5 %collective-permute-start.35 = (f32[256,256]{1,0:T(8,128)S(1)}, f32[256,256]{1,0:T(8,128)S(1)}, u32[]{:S(2)}, u32[]{:S(2)}) collective-permute-start(f32[256,256]{1,0:T(8,128)S(1)} %get-tuple-element.72), channel_id=1, source_target_pairs={{0,128},{64,192},{128,0},{192,64},{1,129},{65,193},{129,1},{193,65... | collective-permute-start | bytes 786440 | tf_op jit(solution)/shard_map/ppermute | solution.py:39
  89.0 5.3 %collective-permute-done.45.refs_7_ = f32[128,512]{1,0:T(8,128)S(1)} collective-permute-done((f32[128,512]{1,0:T(8,128)S(1)}, f32[128,512]{1,0:T(8,128)S(1)}, u32[]{:S(2)}, u32[]{:S(2)}) %collective-permute-start.45) | collective-permute-done | bytes 262176 | tf_op jit(solution)/shard_map/ppermute | solution.py:39
  94.6 2.7 %collective-permute-start.17 = (f32[288,256]{1,0:T(8,128)S(1)}, f32[288,256]{1,0:T(8,128)S(1)}, u32[]{:S(2)}, u32[]{:S(2)}) collective-permute-start(f32[288,256]{1,0:T(8,128)S(1)} %get-tuple-element.60), channel_id=1, source_target_pairs={{0,128},{64,192},{128,0},{192,64},{1,129},{65,193},{129,1},{193,65... | collective-permute-start | bytes 884744 | tf_op jit(solution)/shard_map/ppermute | solution.py:39
  99.7 4.8 %collective-permute-done.42.refs_3_ = f32[128,512]{1,0:T(8,128)S(1)} collective-permute-done((f32[128,512]{1,0:T(8,128)S(1)}, f32[128,512]{1,0:T(8,128)S(1)}, u32[]{:S(2)}, u32[]{:S(2)}) %collective-permute-start.42) | collective-permute-done | bytes 262176 | tf_op jit(solution)/shard_map/ppermute | solution.py:39
  106.9 11.1 %collective-permute-done.36.refs_7_ = f32[256,256]{1,0:T(8,128)S(1)} collective-permute-done((f32[256,256]{1,0:T(8,128)S(1)}, f32[256,256]{1,0:T(8,128)S(1)}, u32[]{:S(2)}, u32[]{:S(2)}) %collective-permute-start.36) | collective-permute-done | bytes 262176 | tf_op jit(solution)/shard_map/ppermute | solution.py:39
  118.2 3.3 %collective-permute-start.38 = (f32[160,256]{1,0:T(8,128)S(1)}, f32[160,256]{1,0:T(8,128)S(1)}, u32[]{:S(2)}, u32[]{:S(2)}) collective-permute-start(f32[160,256]{1,0:T(8,128)S(1)} %get-tuple-element.76), channel_id=1, source_target_pairs={{0,16},{16,0},{1,17},{17,1},{2,18},{18,2},{3,19},{19,3},{4,20},{20... | collective-permute-start | bytes 491528 | tf_op jit(solution)/shard_map/ppermute | solution.py:39
  124.4 3.0 %collective-permute-done.47.refs_6_ = f32[128,256]{1,0:T(8,128)S(1)} collective-permute-done((f32[128,256]{1,0:T(8,128)S(1)}, f32[128,256]{1,0:T(8,128)S(1)}, u32[]{:S(2)}, u32[]{:S(2)}) %collective-permute-start.47) | collective-permute-done | bytes 131104 | tf_op jit(solution)/shard_map/ppermute | solution.py:39
  (96 shorter events, 35.2 us)
Async XLA Ops:
  1.8 11.5 %collective-permute-start.19 = (bf16[128,1024]{1,0:T(8,128)(2,1)S(1)}, bf16[128,1024]{1,0:T(8,128)(2,1)S(1)}, u32[]{:S(2)}, u32[]{:S(2)}) collective-permute-start(bf16[128,1024]{1,0:T(8,128)(2,1)S(1)} %shard_map.98.refs_0_), channel_id=1, source_target_pairs={{0,14},{2,0},{4,2},{6,4},{8,6},{10,8},{12,10},{14,12},{1,15},{3,1}... | collective-permute-start | bytes 786440 | tf_op jit(solution)/shard_map/ppermute | solution.py:44
  12.1 12.5 %collective-permute-start.1 = (bf16[144,1024]{1,0:T(8,128)(2,1)S(1)}, bf16[144,1024]{1,0:T(8,128)(2,1)S(1)}, u32[]{:S(2)}, u32[]{:S(2)}) collective-permute-start(bf16[144,1024]{1,0:T(8,128)(2,1)S(1)} %shard_map.95.refs_0_), channel_id=1, source_target_pairs={{0,2},{2,4},{4,6},{6,8},{8,10},{10,12},{12,14},{14,0},{1,3},{3,5},... | collective-permute-start | bytes 884744 | tf_op jit(solution)/shard_map/ppermute | solution.py:44
  12.2 13.2 %collective-permute-start.6 = (bf16[144,1024]{1,0:T(8,128)(2,1)S(1)}, bf16[144,1024]{1,0:T(8,128)(2,1)S(1)}, u32[]{:S(2)}, u32[]{:S(2)}) collective-permute-start(bf16[144,1024]{1,0:T(8,128)(2,1)S(1)} %shard_map.95.refs_0_), channel_id=1, source_target_pairs={{0,1},{1,0},{2,3},{3,2},{4,5},{5,4},{6,7},{7,6},{8,9},{9,8},{10,11... | collective-permute-start | bytes 884744 | tf_op jit(solution)/shard_map/ppermute | solution.py:39
  13.2 12.2 %collective-permute-start.8 = (bf16[144,1024]{1,0:T(8,128)(2,1)S(1)}, bf16[144,1024]{1,0:T(8,128)(2,1)S(1)}, u32[]{:S(2)}, u32[]{:S(2)}) collective-permute-start(bf16[144,1024]{1,0:T(8,128)(2,1)S(1)} %shard_map.95.refs_0_), channel_id=1, source_target_pairs={{0,14},{2,0},{4,2},{6,4},{8,6},{10,8},{12,10},{14,12},{1,15},{3,1}... | collective-permute-start | bytes 884744 | tf_op jit(solution)/shard_map/ppermute | solution.py:44
  18.3 11.6 %collective-permute-start.26 = (bf16[128,1024]{1,0:T(8,128)(2,1)S(1)}, bf16[128,1024]{1,0:T(8,128)(2,1)S(1)}, u32[]{:S(2)}, u32[]{:S(2)}) collective-permute-start(bf16[128,1024]{1,0:T(8,128)(2,1)S(1)} %collective-permute-done.25.refs_2_), channel_id=1, source_target_pairs={{0,1},{1,0},{2,3},{3,2},{4,5},{5,4},{6,7},{7,6},{8,9},{9,8},{10,11... | collective-permute-start | bytes 786440 | tf_op jit(solution)/shard_map/ppermute | solution.py:39
  25.5 15.4 %collective-permute-start.2 = (bf16[144,1024]{1,0:T(8,128)(2,1)S(1)}, bf16[144,1024]{1,0:T(8,128)(2,1)S(1)}, u32[]{:S(2)}, u32[]{:S(2)}) collective-permute-start(bf16[144,1024]{1,0:T(8,128)(2,1)S(1)} %collective-permute-done.1.refs_2_), channel_id=1, source_target_pairs={{0,2},{2,4},{4,6},{6,8},{8,10},{10,12},{12,14},{14,0},{1,3},{3,5},... | collective-permute-start | bytes 884744 | tf_op jit(solution)/shard_map/ppermute | solution.py:44
  27.1 13.8 %collective-permute-start.7 = (bf16[144,1024]{1,0:T(8,128)(2,1)S(1)}, bf16[144,1024]{1,0:T(8,128)(2,1)S(1)}, u32[]{:S(2)}, u32[]{:S(2)}) collective-permute-start(bf16[144,1024]{1,0:T(8,128)(2,1)S(1)} %collective-permute-done.1.refs_2_), channel_id=1, source_target_pairs={{0,1},{1,0},{2,3},{3,2},{4,5},{5,4},{6,7},{7,6},{8,9},{9,8},{10,11... | collective-permute-start | bytes 884744 | tf_op jit(solution)/shard_map/ppermute | solution.py:39
  29.9 34.7 %collective-permute-start = (bf16[256,2048]{1,0:T(8,128)(2,1)S(1)}, bf16[256,2048]{1,0:T(8,128)(2,1)S(1)}, u32[]{:S(2)}, u32[]{:S(2)}) collective-permute-start(bf16[256,2048]{1,0:T(8,128)(2,1)S(1)} %shard_map.94), channel_id=1, source_target_pairs={{0,16},{16,0},{1,17},{17,1},{2,18},{18,2},{3,19},{19,3},{4,20},{20... | collective-permute-start | bytes 3145736 | tf_op jit(solution)/shard_map/ppermute | solution.py:39
  42.7 11.7 %collective-permute-start.3 = (bf16[144,1024]{1,0:T(8,128)(2,1)S(1)}, bf16[144,1024]{1,0:T(8,128)(2,1)S(1)}, u32[]{:S(2)}, u32[]{:S(2)}) collective-permute-start(bf16[144,1024]{1,0:T(8,128)(2,1)S(1)} %collective-permute-done.2.refs_6_), channel_id=1, source_target_pairs={{0,2},{2,4},{4,6},{6,8},{8,10},{10,12},{12,14},{14,0},{1,3},{3,5},... | collective-permute-start | bytes 884744 | tf_op jit(solution)/shard_map/ppermute | solution.py:44
  48.3 15.2 %collective-permute-start.14 = (bf16[144,1024]{1,0:T(8,128)(2,1)S(1)}, bf16[144,1024]{1,0:T(8,128)(2,1)S(1)}, u32[]{:S(2)}, u32[]{:S(2)}) collective-permute-start(bf16[144,1024]{1,0:T(8,128)(2,1)S(1)} %collective-permute-done.11.refs_8_), channel_id=1, source_target_pairs={{0,14},{2,0},{4,2},{6,4},{8,6},{10,8},{12,10},{14,12},{1,15},{3,1}... | collective-permute-start | bytes 884744 | tf_op jit(solution)/shard_map/ppermute | solution.py:44
  51.7 11.8 %collective-permute-start.22 = (bf16[128,1024]{1,0:T(8,128)(2,1)S(1)}, bf16[128,1024]{1,0:T(8,128)(2,1)S(1)}, u32[]{:S(2)}, u32[]{:S(2)}) collective-permute-start(bf16[128,1024]{1,0:T(8,128)(2,1)S(1)} %collective-permute-done.21.refs_12_), channel_id=1, source_target_pairs={{0,14},{2,0},{4,2},{6,4},{8,6},{10,8},{12,10},{14,12},{1,15},{3,1}... | collective-permute-start | bytes 786440 | tf_op jit(solution)/shard_map/ppermute | solution.py:44
  54.4 11.3 %collective-permute-start.4 = (bf16[144,1024]{1,0:T(8,128)(2,1)S(1)}, bf16[144,1024]{1,0:T(8,128)(2,1)S(1)}, u32[]{:S(2)}, u32[]{:S(2)}) collective-permute-start(bf16[144,1024]{1,0:T(8,128)(2,1)S(1)} %collective-permute-done.3.refs_10_), channel_id=1, source_target_pairs={{0,2},{2,4},{4,6},{6,8},{8,10},{10,12},{12,14},{14,0},{1,3},{3,5},... | collective-permute-start | bytes 884744 | tf_op jit(solution)/shard_map/ppermute | solution.py:44
  68.4 13.2 %collective-permute-start.5 = (bf16[144,1024]{1,0:T(8,128)(2,1)S(1)}, bf16[144,1024]{1,0:T(8,128)(2,1)S(1)}, u32[]{:S(2)}, u32[]{:S(2)}) collective-permute-start(bf16[144,1024]{1,0:T(8,128)(2,1)S(1)} %collective-permute-done.4.own_ref), channel_id=1, source_target_pairs={{0,1},{1,0},{2,3},{3,2},{4,5},{5,4},{6,7},{7,6},{8,9},{9,8},{10,11... | collective-permute-start | bytes 884744 | tf_op jit(solution)/shard_map/ppermute | solution.py:39
  74.0 12.6 %collective-permute-start.44 = (f32[128,512]{1,0:T(8,128)S(1)}, f32[128,512]{1,0:T(8,128)S(1)}, u32[]{:S(2)}, u32[]{:S(2)}) collective-permute-start(f32[128,512]{1,0:T(8,128)S(1)} %get-tuple-element.84), channel_id=1, source_target_pairs={{0,16},{16,0},{1,17},{17,1},{2,18},{18,2},{3,19},{19,3},{4,20},{20... | collective-permute-start | bytes 786440 | tf_op jit(solution)/shard_map/ppermute | solution.py:39
  79.3 15.0 %collective-permute-start.45 = (f32[128,512]{1,0:T(8,128)S(1)}, f32[128,512]{1,0:T(8,128)S(1)}, u32[]{:S(2)}, u32[]{:S(2)}) collective-permute-start(f32[128,512]{1,0:T(8,128)S(1)} %get-tuple-element.85), channel_id=1, source_target_pairs={{0,48},{16,32},{32,16},{48,0},{1,49},{17,33},{33,17},{49,1},{2,50}... | collective-permute-start | bytes 786440 | tf_op jit(solution)/shard_map/ppermute | solution.py:39
  82.2 12.3 %collective-permute-start.40 = (f32[128,512]{1,0:T(8,128)S(1)}, f32[128,512]{1,0:T(8,128)S(1)}, u32[]{:S(2)}, u32[]{:S(2)}) collective-permute-start(f32[128,512]{1,0:T(8,128)S(1)} %get-tuple-element.79), channel_id=1, source_target_pairs={{0,32},{32,0},{1,33},{33,1},{2,34},{34,2},{3,35},{35,3},{4,36},{36... | collective-permute-start | bytes 786440 | tf_op jit(solution)/shard_map/ppermute | solution.py:39
  82.3 15.5 %collective-permute-start.41 = (f32[128,512]{1,0:T(8,128)S(1)}, f32[128,512]{1,0:T(8,128)S(1)}, u32[]{:S(2)}, u32[]{:S(2)}) collective-permute-start(f32[128,512]{1,0:T(8,128)S(1)} %get-tuple-element.80), channel_id=1, source_target_pairs={{0,16},{16,0},{1,17},{17,1},{2,18},{18,2},{3,19},{19,3},{4,20},{20... | collective-permute-start | bytes 786440 | tf_op jit(solution)/shard_map/ppermute | solution.py:39
  84.0 20.5 %collective-permute-start.42 = (f32[128,512]{1,0:T(8,128)S(1)}, f32[128,512]{1,0:T(8,128)S(1)}, u32[]{:S(2)}, u32[]{:S(2)}) collective-permute-start(f32[128,512]{1,0:T(8,128)S(1)} %get-tuple-element.81), channel_id=1, source_target_pairs={{0,48},{16,32},{32,16},{48,0},{1,49},{17,33},{33,17},{49,1},{2,50}... | collective-permute-start | bytes 786440 | tf_op jit(solution)/shard_map/ppermute | solution.py:39
  86.5 19.9 %collective-permute-start.35 = (f32[256,256]{1,0:T(8,128)S(1)}, f32[256,256]{1,0:T(8,128)S(1)}, u32[]{:S(2)}, u32[]{:S(2)}) collective-permute-start(f32[256,256]{1,0:T(8,128)S(1)} %get-tuple-element.72), channel_id=1, source_target_pairs={{0,128},{64,192},{128,0},{192,64},{1,129},{65,193},{129,1},{193,65... | collective-permute-start | bytes 786440 | tf_op jit(solution)/shard_map/ppermute | solution.py:39
  94.3 23.6 %collective-permute-start.16 = (f32[288,256]{1,0:T(8,128)S(1)}, f32[288,256]{1,0:T(8,128)S(1)}, u32[]{:S(2)}, u32[]{:S(2)}) collective-permute-start(f32[288,256]{1,0:T(8,128)S(1)} %get-tuple-element.59), channel_id=1, source_target_pairs={{0,64},{64,0},{128,192},{192,128},{1,65},{65,1},{129,193},{193,129... | collective-permute-start | bytes 884744 | tf_op jit(solution)/shard_map/ppermute | solution.py:39
  94.6 23.4 %collective-permute-start.17 = (f32[288,256]{1,0:T(8,128)S(1)}, f32[288,256]{1,0:T(8,128)S(1)}, u32[]{:S(2)}, u32[]{:S(2)}) collective-permute-start(f32[288,256]{1,0:T(8,128)S(1)} %get-tuple-element.60), channel_id=1, source_target_pairs={{0,128},{64,192},{128,0},{192,64},{1,129},{65,193},{129,1},{193,65... | collective-permute-start | bytes 884744 | tf_op jit(solution)/shard_map/ppermute | solution.py:39
  97.8 20.2 %collective-permute-start.18 = (f32[288,256]{1,0:T(8,128)S(1)}, f32[288,256]{1,0:T(8,128)S(1)}, u32[]{:S(2)}, u32[]{:S(2)}) collective-permute-start(f32[288,256]{1,0:T(8,128)S(1)} %get-tuple-element.61), channel_id=1, source_target_pairs={{0,192},{64,128},{128,64},{192,0},{1,193},{65,129},{129,65},{193,1... | collective-permute-start | bytes 884744 | tf_op jit(solution)/shard_map/ppermute | solution.py:39
  104.4 13.5 %collective-permute-start.36 = (f32[256,256]{1,0:T(8,128)S(1)}, f32[256,256]{1,0:T(8,128)S(1)}, u32[]{:S(2)}, u32[]{:S(2)}) collective-permute-start(f32[256,256]{1,0:T(8,128)S(1)} %get-tuple-element.73), channel_id=1, source_target_pairs={{0,192},{64,128},{128,64},{192,0},{1,193},{65,129},{129,65},{193,1... | collective-permute-start | bytes 786440 | tf_op jit(solution)/shard_map/ppermute | solution.py:39
  106.5 16.9 %collective-permute-start.46 = (f32[128,256]{1,0:T(8,128)S(1)}, f32[128,256]{1,0:T(8,128)S(1)}, u32[]{:S(2)}, u32[]{:S(2)}) collective-permute-start(f32[128,256]{1,0:T(8,128)S(1)} %get-tuple-element.87), channel_id=1, source_target_pairs={{0,64},{64,0},{128,192},{192,128},{1,65},{65,1},{129,193},{193,129... | collective-permute-start | bytes 393224 | tf_op jit(solution)/shard_map/ppermute | solution.py:39
  (30 other events, 290.6 us)

commit v4 on v3

--- a/solution.py
+++ b/solution.py
@@ -22,7 +22,6 @@
 F32 = jnp.float32
 BF16 = jnp.bfloat16
 VMEM = pl.BlockSpec(memory_space=pltpu.VMEM)
-ANY = pl.BlockSpec(memory_space=pl.ANY)
 STEPS = (0, -1, 1, -2, 2, -3, 3, 4)
 
 
@@ -83,7 +82,9 @@
 def ordered(k, rows, gain):
     out = struct((144 if k == 0 else 128, 1024), BF16)
     specs = [VMEM] * (1 + len(gain))
-    return kernel_call(functools.partial(order_kernel, k), specs, [out], 4, (1 << 20, 1 << 20), [rows, *gain])[0]
+    return kernel_call(
+        functools.partial(order_kernel, k), specs, [out], 4, (1 << 20, 1 << 20), [rows, *gain]
+    )[0]
 
 
 def turn_kernel(away, inputs_ref, out_ref):
@@ -98,7 +99,12 @@
 
 def turned(inputs, away):
     return kernel_call(
-        functools.partial(turn_kernel, away), [VMEM], [struct((256, 2048), BF16)], 6, (1 << 22, 2 << 20), [inputs]
+        functools.partial(turn_kernel, away),
+        [VMEM],
+        [struct((256, 2048), BF16)],
+        6,
+        (1 << 22, 2 << 20),
+        [inputs],
     )[0]
 
 
@@ -106,24 +112,16 @@
     blocks, outs, refs = refs[:14], refs[14:22], refs[22:]
     if k == 0:
         gains_ref, refs = refs[0], refs[1:]
-    rows, result, sems = refs[:3]
-    copies = [
-        pltpu.make_async_copy(block.at[pl.ds(0, 128), :], rows.at[pl.ds(i * 128, 128), :], sems.at[i])
-        for i, block in enumerate(blocks)
-    ]
-    if k == 0:
         for i, block in enumerate(blocks):
-            copies.append(
-                pltpu.make_async_copy(block.at[pl.ds(128, 16), :], gains_ref.at[source_of(i)], refs[3].at[i])
-            )
-    for copy in copies:
-        copy.start()
-    for copy in copies:
-        copy.wait()
+            gains_ref[source_of(i)] = block[128:144, :]
+    rows, result = refs
 
     @pl.loop(0, 4)
     def _(j):
-        right = rows[:, pl.ds(pl.multiple_of(j * 256, 256), 256)]
+        columns = pl.ds(pl.multiple_of(j * 256, 256), 256)
+        for i, block in enumerate(blocks):
+            rows[i * 128 : (i + 1) * 128, :] = block[:128, columns]
+        right = rows[...]
         result[:256, :] = jnp.dot(mine_ref[:, :1792], right, preferred_element_type=F32)
         result[256:, :] = jnp.dot(other_ref[:, :1792], right, preferred_element_type=F32)
         for at in range(4):
@@ -180,14 +178,11 @@
 
 def product(k, mine, other, blocks):
     pieces = [struct((128, 512), F32)] * 4
-    scratch = [pltpu.VMEM((1792, 1024), BF16), pltpu.VMEM((512, 256), F32), pltpu.SemaphoreType.DMA((14,))]
-    gains = []
-    if k == 0:
-        scratch += [pltpu.SemaphoreType.DMA((14,))]
-        gains = [struct((16, 16, 1024), BF16)]
+    scratch = [pltpu.VMEM((1792, 256), BF16), pltpu.VMEM((512, 256), F32)]
+    gains = [struct((16, 16, 1024), BF16)] if k == 0 else []
     parts = kernel_call(
         functools.partial(part_kernel, k),
-        [VMEM, VMEM] + [ANY] * 14,
+        [VMEM] * 16,
         [struct((256, 256), F32)] * 4 + pieces + gains,
         14,
         (2 * 512 * 1792 * 1024, 8 << 20),
@@ -232,7 +227,9 @@
 
 
 def cut_sum(kernel, parts, rows):
-    return kernel_call(kernel, [VMEM] * 8, [struct((rows, 256), F32)] * 4, 5, (1 << 18, 1 << 20), parts)
+    return kernel_call(
+        kernel, [VMEM] * 8, [struct((rows, 256), F32)] * 4, 5, (1 << 18, 1 << 20), parts
+    )
 
 
 def adam_kernel(scale, first_ref, second_ref, *refs):

time: 132 us -> 132 us (level); the launches traced: 130 us -> 132 us
  waiting for transfers between devices: 52.3 us -> 55.4 us
  Pallas kernels: 10.6 us -> 9 us
    ppermute x35, waiting for transfers between devices: 26.8 us -> 29.8 us  [swap(): return lax.ppermute(array, axis, [(i, i ^ mask) for i in range(size)])]
    pallas_call x11, Pallas kernels: 10.6 us -> 9 us  [kernel_call(): pl.pallas_call(kernel, in_specs=in_specs, out_specs=[VMEM] * len(out_shap...]
  transfers between devices with their start and end apart: 49 -> 49, of which waited for: 18 -> 18; matrix products, arithmetic and copies ran while one was open for 2% -> 2% of each run, Pallas kernels for 7% -> 6%
where the time goes in v4:
time: 132 us
  starting transfers between devices  62.4 us (47%)
  waiting for transfers between devices  55.4 us (42%)
  Pallas kernels  9 us (7%)
  other arithmetic  2.83 us (2%)
    ppermute x35, starting transfers between devices, swap(): return lax.ppermute(array, axis, [(i, i ^ mask) for i in range(size)])  43.1 us
    ppermute x35, waiting for transfers between devices, swap(): return lax.ppermute(array, axis, [(i, i ^ mask) for i in range(size)])  29.8 us
    ppermute x14, waiting for transfers between devices, shift(): lax.ppermute(array, 'z', [(i, (i + step) % size) for i in range(size)])  25.5 us
    ppermute x14, starting transfers between devices, shift(): lax.ppermute(array, 'z', [(i, (i + step) % size) for i in range(size)])  19.3 us
    pallas_call x11, Pallas kernels, kernel_call(): pl.pallas_call(kernel, in_specs=in_specs, out_specs=[VMEM] * len(out_shap...  9 us
    reduce_sum x1, other arithmetic, update_of(): jnp.sum(norm_grad.astype(F32) * normed.astype(F32), axis=1).reshape(64, 128)  2.83 us
  transfers between devices with their start and end apart: 49, of which 18 were waited for; matrix products, arithmetic and copies ran while one was open for 2% of the time, Pallas kernels for 6%

profile of v4, /device:TPU:1, one launch (start us, length us, event | category | flops | bytes accessed | tf_op | source)
XLA Modules:
  0.0 131.5 jit_solution(10171586752496757670)
XLA Ops:
  1.8 6.5 %collective-permute-start.19 = (bf16[128,1024]{1,0:T(8,128)(2,1)S(1)}, bf16[128,1024]{1,0:T(8,128)(2,1)S(1)}, u32[]{:S(2)}, u32[]{:S(2)}) collective-permute-start(bf16[128,1024]{1,0:T(8,128)(2,1)S(1)} %shard_map.98.refs_0_), channel_id=1, source_target_pairs={{0,14},{2,0},{4,2},{6,4},{8,6},{10,8},{12,10},{14,12},{1,15},{3,1}... | collective-permute-start | bytes 786440 | tf_op jit(solution)/shard_map/ppermute | solution.py:43
  9.2 2.8 %multiply_reduce_fusion = f32[8192]{0:T(1024)S(1)} fusion(bf16[1,128,8192]{2,1,0:T(8,128)(2,1)} %param.8, bf16[1,128,8192]{2,1,0:T(8,128)(2,1)} %param.9), kind=kLoop, calls=%fused_computation | loop fusion | flops 4186112 | bytes 4227072 | tf_op jit(solution)/shard_map/reduce_sum | solution.py:267
  13.2 3.4 %collective-permute-start.8 = (bf16[144,1024]{1,0:T(8,128)(2,1)S(1)}, bf16[144,1024]{1,0:T(8,128)(2,1)S(1)}, u32[]{:S(2)}, u32[]{:S(2)}) collective-permute-start(bf16[144,1024]{1,0:T(8,128)(2,1)S(1)} %shard_map.95.refs_0_), channel_id=1, source_target_pairs={{0,14},{2,0},{4,2},{6,4},{8,6},{10,8},{12,10},{14,12},{1,15},{3,1}... | collective-permute-start | bytes 884744 | tf_op jit(solution)/shard_map/ppermute | solution.py:43
  19.6 5.0 %collective-permute-done.1.refs_2_ = bf16[144,1024]{1,0:T(8,128)(2,1)S(1)} collective-permute-done((bf16[144,1024]{1,0:T(8,128)(2,1)S(1)}, bf16[144,1024]{1,0:T(8,128)(2,1)S(1)}, u32[]{:S(2)}, u32[]{:S(2)}) %collective-permute-start.1) | collective-permute-done | bytes 294944 | tf_op jit(solution)/shard_map/ppermute | solution.py:43
  27.1 2.4 %collective-permute-start.7 = (bf16[144,1024]{1,0:T(8,128)(2,1)S(1)}, bf16[144,1024]{1,0:T(8,128)(2,1)S(1)}, u32[]{:S(2)}, u32[]{:S(2)}) collective-permute-start(bf16[144,1024]{1,0:T(8,128)(2,1)S(1)} %collective-permute-done.1.refs_2_), channel_id=1, source_target_pairs={{0,1},{1,0},{2,3},{3,2},{4,5},{5,4},{6,7},{7,6},{8,9},{9,8},{10,11... | collective-permute-start | bytes 884744 | tf_op jit(solution)/shard_map/ppermute | solution.py:38
  29.9 3.0 %collective-permute-start = (bf16[256,2048]{1,0:T(8,128)(2,1)S(1)}, bf16[256,2048]{1,0:T(8,128)(2,1)S(1)}, u32[]{:S(2)}, u32[]{:S(2)}) collective-permute-start(bf16[256,2048]{1,0:T(8,128)(2,1)S(1)} %shard_map.94), channel_id=1, source_target_pairs={{0,16},{16,0},{1,17},{17,1},{2,18},{18,2},{3,19},{19,3},{4,20},{20... | collective-permute-start | bytes 3145736 | tf_op jit(solution)/shard_map/ppermute | solution.py:38
  36.6 4.3 %collective-permute-done.2.refs_6_ = bf16[144,1024]{1,0:T(8,128)(2,1)S(1)} collective-permute-done((bf16[144,1024]{1,0:T(8,128)(2,1)S(1)}, bf16[144,1024]{1,0:T(8,128)(2,1)S(1)}, u32[]{:S(2)}, u32[]{:S(2)}) %collective-permute-start.2) | collective-permute-done | bytes 294944 | tf_op jit(solution)/shard_map/ppermute | solution.py:43
  43.6 4.8 %collective-permute-done.21.refs_12_ = bf16[128,1024]{1,0:T(8,128)(2,1)S(1)} collective-permute-done((bf16[128,1024]{1,0:T(8,128)(2,1)S(1)}, bf16[128,1024]{1,0:T(8,128)(2,1)S(1)}, u32[]{:S(2)}, u32[]{:S(2)}) %collective-permute-start.21) | collective-permute-done | bytes 262176 | tf_op jit(solution)/shard_map/ppermute | solution.py:43
  48.3 3.4 %collective-permute-start.14 = (bf16[144,1024]{1,0:T(8,128)(2,1)S(1)}, bf16[144,1024]{1,0:T(8,128)(2,1)S(1)}, u32[]{:S(2)}, u32[]{:S(2)}) collective-permute-start(bf16[144,1024]{1,0:T(8,128)(2,1)S(1)} %collective-permute-done.11.refs_8_), channel_id=1, source_target_pairs={{0,14},{2,0},{4,2},{6,4},{8,6},{10,8},{12,10},{14,12},{1,15},{3,1}... | collective-permute-start | bytes 884744 | tf_op jit(solution)/shard_map/ppermute | solution.py:43
  51.7 2.7 %collective-permute-start.22 = (bf16[128,1024]{1,0:T(8,128)(2,1)S(1)}, bf16[128,1024]{1,0:T(8,128)(2,1)S(1)}, u32[]{:S(2)}, u32[]{:S(2)}) collective-permute-start(bf16[128,1024]{1,0:T(8,128)(2,1)S(1)} %collective-permute-done.21.refs_12_), channel_id=1, source_target_pairs={{0,14},{2,0},{4,2},{6,4},{8,6},{10,8},{12,10},{14,12},{1,15},{3,1}... | collective-permute-start | bytes 786440 | tf_op jit(solution)/shard_map/ppermute | solution.py:43
  54.4 5.0 %collective-permute-done.31.refs_10_ = bf16[128,1024]{1,0:T(8,128)(2,1)S(1)} collective-permute-done((bf16[128,1024]{1,0:T(8,128)(2,1)S(1)}, bf16[128,1024]{1,0:T(8,128)(2,1)S(1)}, u32[]{:S(2)}, u32[]{:S(2)}) %collective-permute-start.31) | collective-permute-done | bytes 262176 | tf_op jit(solution)/shard_map/ppermute | solution.py:43
  59.4 4.0 %collective-permute-start.32 = (bf16[128,1024]{1,0:T(8,128)(2,1)S(1)}, bf16[128,1024]{1,0:T(8,128)(2,1)S(1)}, u32[]{:S(2)}, u32[]{:S(2)}) collective-permute-start(bf16[128,1024]{1,0:T(8,128)(2,1)S(1)} %collective-permute-done.31.refs_10_), channel_id=1, source_target_pairs={{0,1},{1,0},{2,3},{3,2},{4,5},{5,4},{6,7},{7,6},{8,9},{9,8},{10,11... | collective-permute-start | bytes 786440 | tf_op jit(solution)/shard_map/ppermute | solution.py:38
  68.5 2.8 %shard_map.99 = (f32[256,256]{1,0:T(8,128)S(1)}, f32[256,256]{1,0:T(8,128)S(1)}, f32[256,256]{1,0:T(8,128)S(1)}, f32[256,256]{1,0:T(8,128)S(1)}, f32[128,512]{1,...) custom-call(bf16[256,2048]{1,0:T(8,128)(2,1)S(1)} %shard_map.93.mine_ref, ...), custom_call_target="tpu_custom_call" | custom-call | flops 1879048192 | bytes 8388608 | tf_op jit(solution)/shard_map/pallas_call | solution.py:55
  74.8 2.9 %shard_map.96 = (f32[256,256]{1,0:T(8,128)S(1)}, f32[256,256]{1,0:T(8,128)S(1)}, f32[256,256]{1,0:T(8,128)S(1)}, f32[256,256]{1,0:T(8,128)S(1)}, f32[128,512]{1,...) custom-call(bf16[256,2048]{1,0:T(8,128)(2,1)S(1)} %shard_map.93.mine, ...), custom_call_target="tpu_custom_call" | custom-call | flops 1879048192 | bytes 8388608 | tf_op jit(solution)/shard_map/pallas_call | solution.py:55
  77.7 2.3 %collective-permute-start.45 = (f32[128,512]{1,0:T(8,128)S(1)}, f32[128,512]{1,0:T(8,128)S(1)}, u32[]{:S(2)}, u32[]{:S(2)}) collective-permute-start(f32[128,512]{1,0:T(8,128)S(1)} %get-tuple-element.85), channel_id=1, source_target_pairs={{0,48},{16,32},{32,16},{48,0},{1,49},{17,33},{33,17},{49,1},{2,50}... | collective-permute-start | bytes 786440 | tf_op jit(solution)/shard_map/ppermute | solution.py:38
  86.1 2.5 %collective-permute-start.35 = (f32[256,256]{1,0:T(8,128)S(1)}, f32[256,256]{1,0:T(8,128)S(1)}, u32[]{:S(2)}, u32[]{:S(2)}) collective-permute-start(f32[256,256]{1,0:T(8,128)S(1)} %get-tuple-element.72), channel_id=1, source_target_pairs={{0,128},{64,192},{128,0},{192,64},{1,129},{65,193},{129,1},{193,65... | collective-permute-start | bytes 786440 | tf_op jit(solution)/shard_map/ppermute | solution.py:38
  88.6 3.0 %collective-permute-done.45.refs_7_ = f32[128,512]{1,0:T(8,128)S(1)} collective-permute-done((f32[128,512]{1,0:T(8,128)S(1)}, f32[128,512]{1,0:T(8,128)S(1)}, u32[]{:S(2)}, u32[]{:S(2)}) %collective-permute-start.45) | collective-permute-done | bytes 262176 | tf_op jit(solution)/shard_map/ppermute | solution.py:38
  91.9 2.7 %collective-permute-start.17 = (f32[288,256]{1,0:T(8,128)S(1)}, f32[288,256]{1,0:T(8,128)S(1)}, u32[]{:S(2)}, u32[]{:S(2)}) collective-permute-start(f32[288,256]{1,0:T(8,128)S(1)} %get-tuple-element.60), channel_id=1, source_target_pairs={{0,128},{64,192},{128,0},{192,64},{1,129},{65,193},{129,1},{193,65... | collective-permute-start | bytes 884744 | tf_op jit(solution)/shard_map/ppermute | solution.py:38
  94.6 2.8 %collective-permute-done.41.refs_2_ = f32[128,512]{1,0:T(8,128)S(1)} collective-permute-done((f32[128,512]{1,0:T(8,128)S(1)}, f32[128,512]{1,0:T(8,128)S(1)}, u32[]{:S(2)}, u32[]{:S(2)}) %collective-permute-start.41) | collective-permute-done | bytes 262176 | tf_op jit(solution)/shard_map/ppermute | solution.py:38
  99.2 3.6 %collective-permute-done.42.refs_3_ = f32[128,512]{1,0:T(8,128)S(1)} collective-permute-done((f32[128,512]{1,0:T(8,128)S(1)}, f32[128,512]{1,0:T(8,128)S(1)}, u32[]{:S(2)}, u32[]{:S(2)}) %collective-permute-start.42) | collective-permute-done | bytes 262176 | tf_op jit(solution)/shard_map/ppermute | solution.py:38
  105.3 12.5 %collective-permute-done.36.refs_7_ = f32[256,256]{1,0:T(8,128)S(1)} collective-permute-done((f32[256,256]{1,0:T(8,128)S(1)}, f32[256,256]{1,0:T(8,128)S(1)}, u32[]{:S(2)}, u32[]{:S(2)}) %collective-permute-start.36) | collective-permute-done | bytes 262176 | tf_op jit(solution)/shard_map/ppermute | solution.py:38
  118.1 3.3 %collective-permute-start.38 = (f32[160,256]{1,0:T(8,128)S(1)}, f32[160,256]{1,0:T(8,128)S(1)}, u32[]{:S(2)}, u32[]{:S(2)}) collective-permute-start(f32[160,256]{1,0:T(8,128)S(1)} %get-tuple-element.76), channel_id=1, source_target_pairs={{0,16},{16,0},{1,17},{17,1},{2,18},{18,2},{3,19},{19,3},{4,20},{20... | collective-permute-start | bytes 491528 | tf_op jit(solution)/shard_map/ppermute | solution.py:38
  124.2 2.9 %collective-permute-done.47.refs_6_ = f32[128,256]{1,0:T(8,128)S(1)} collective-permute-done((f32[128,256]{1,0:T(8,128)S(1)}, f32[128,256]{1,0:T(8,128)S(1)}, u32[]{:S(2)}, u32[]{:S(2)}) %collective-permute-start.47) | collective-permute-done | bytes 131104 | tf_op jit(solution)/shard_map/ppermute | solution.py:38
  127.2 3.3 %collective-permute-done.48.refs_7_ = f32[128,256]{1,0:T(8,128)S(1)} collective-permute-done((f32[128,256]{1,0:T(8,128)S(1)}, f32[128,256]{1,0:T(8,128)S(1)}, u32[]{:S(2)}, u32[]{:S(2)}) %collective-permute-start.48) | collective-permute-done | bytes 131104 | tf_op jit(solution)/shard_map/ppermute | solution.py:38
  (96 shorter events, 38.7 us)
Async XLA Ops:
  1.8 11.5 %collective-permute-start.19 = (bf16[128,1024]{1,0:T(8,128)(2,1)S(1)}, bf16[128,1024]{1,0:T(8,128)(2,1)S(1)}, u32[]{:S(2)}, u32[]{:S(2)}) collective-permute-start(bf16[128,1024]{1,0:T(8,128)(2,1)S(1)} %shard_map.98.refs_0_), channel_id=1, source_target_pairs={{0,14},{2,0},{4,2},{6,4},{8,6},{10,8},{12,10},{14,12},{1,15},{3,1}... | collective-permute-start | bytes 786440 | tf_op jit(solution)/shard_map/ppermute | solution.py:43
  12.1 12.5 %collective-permute-start.1 = (bf16[144,1024]{1,0:T(8,128)(2,1)S(1)}, bf16[144,1024]{1,0:T(8,128)(2,1)S(1)}, u32[]{:S(2)}, u32[]{:S(2)}) collective-permute-start(bf16[144,1024]{1,0:T(8,128)(2,1)S(1)} %shard_map.95.refs_0_), channel_id=1, source_target_pairs={{0,2},{2,4},{4,6},{6,8},{8,10},{10,12},{12,14},{14,0},{1,3},{3,5},... | collective-permute-start | bytes 884744 | tf_op jit(solution)/shard_map/ppermute | solution.py:43
  12.2 13.2 %collective-permute-start.6 = (bf16[144,1024]{1,0:T(8,128)(2,1)S(1)}, bf16[144,1024]{1,0:T(8,128)(2,1)S(1)}, u32[]{:S(2)}, u32[]{:S(2)}) collective-permute-start(bf16[144,1024]{1,0:T(8,128)(2,1)S(1)} %shard_map.95.refs_0_), channel_id=1, source_target_pairs={{0,1},{1,0},{2,3},{3,2},{4,5},{5,4},{6,7},{7,6},{8,9},{9,8},{10,11... | collective-permute-start | bytes 884744 | tf_op jit(solution)/shard_map/ppermute | solution.py:38
  13.2 12.2 %collective-permute-start.8 = (bf16[144,1024]{1,0:T(8,128)(2,1)S(1)}, bf16[144,1024]{1,0:T(8,128)(2,1)S(1)}, u32[]{:S(2)}, u32[]{:S(2)}) collective-permute-start(bf16[144,1024]{1,0:T(8,128)(2,1)S(1)} %shard_map.95.refs_0_), channel_id=1, source_target_pairs={{0,14},{2,0},{4,2},{6,4},{8,6},{10,8},{12,10},{14,12},{1,15},{3,1}... | collective-permute-start | bytes 884744 | tf_op jit(solution)/shard_map/ppermute | solution.py:43
  18.3 11.6 %collective-permute-start.26 = (bf16[128,1024]{1,0:T(8,128)(2,1)S(1)}, bf16[128,1024]{1,0:T(8,128)(2,1)S(1)}, u32[]{:S(2)}, u32[]{:S(2)}) collective-permute-start(bf16[128,1024]{1,0:T(8,128)(2,1)S(1)} %collective-permute-done.25.refs_2_), channel_id=1, source_target_pairs={{0,1},{1,0},{2,3},{3,2},{4,5},{5,4},{6,7},{7,6},{8,9},{9,8},{10,11... | collective-permute-start | bytes 786440 | tf_op jit(solution)/shard_map/ppermute | solution.py:38
  25.5 15.4 %collective-permute-start.2 = (bf16[144,1024]{1,0:T(8,128)(2,1)S(1)}, bf16[144,1024]{1,0:T(8,128)(2,1)S(1)}, u32[]{:S(2)}, u32[]{:S(2)}) collective-permute-start(bf16[144,1024]{1,0:T(8,128)(2,1)S(1)} %collective-permute-done.1.refs_2_), channel_id=1, source_target_pairs={{0,2},{2,4},{4,6},{6,8},{8,10},{10,12},{12,14},{14,0},{1,3},{3,5},... | collective-permute-start | bytes 884744 | tf_op jit(solution)/shard_map/ppermute | solution.py:43
  27.1 13.8 %collective-permute-start.7 = (bf16[144,1024]{1,0:T(8,128)(2,1)S(1)}, bf16[144,1024]{1,0:T(8,128)(2,1)S(1)}, u32[]{:S(2)}, u32[]{:S(2)}) collective-permute-start(bf16[144,1024]{1,0:T(8,128)(2,1)S(1)} %collective-permute-done.1.refs_2_), channel_id=1, source_target_pairs={{0,1},{1,0},{2,3},{3,2},{4,5},{5,4},{6,7},{7,6},{8,9},{9,8},{10,11... | collective-permute-start | bytes 884744 | tf_op jit(solution)/shard_map/ppermute | solution.py:38
  29.9 34.7 %collective-permute-start = (bf16[256,2048]{1,0:T(8,128)(2,1)S(1)}, bf16[256,2048]{1,0:T(8,128)(2,1)S(1)}, u32[]{:S(2)}, u32[]{:S(2)}) collective-permute-start(bf16[256,2048]{1,0:T(8,128)(2,1)S(1)} %shard_map.94), channel_id=1, source_target_pairs={{0,16},{16,0},{1,17},{17,1},{2,18},{18,2},{3,19},{19,3},{4,20},{20... | collective-permute-start | bytes 3145736 | tf_op jit(solution)/shard_map/ppermute | solution.py:38
  42.7 11.7 %collective-permute-start.3 = (bf16[144,1024]{1,0:T(8,128)(2,1)S(1)}, bf16[144,1024]{1,0:T(8,128)(2,1)S(1)}, u32[]{:S(2)}, u32[]{:S(2)}) collective-permute-start(bf16[144,1024]{1,0:T(8,128)(2,1)S(1)} %collective-permute-done.2.refs_6_), channel_id=1, source_target_pairs={{0,2},{2,4},{4,6},{6,8},{8,10},{10,12},{12,14},{14,0},{1,3},{3,5},... | collective-permute-start | bytes 884744 | tf_op jit(solution)/shard_map/ppermute | solution.py:43
  48.3 15.2 %collective-permute-start.14 = (bf16[144,1024]{1,0:T(8,128)(2,1)S(1)}, bf16[144,1024]{1,0:T(8,128)(2,1)S(1)}, u32[]{:S(2)}, u32[]{:S(2)}) collective-permute-start(bf16[144,1024]{1,0:T(8,128)(2,1)S(1)} %collective-permute-done.11.refs_8_), channel_id=1, source_target_pairs={{0,14},{2,0},{4,2},{6,4},{8,6},{10,8},{12,10},{14,12},{1,15},{3,1}... | collective-permute-start | bytes 884744 | tf_op jit(solution)/shard_map/ppermute | solution.py:43
  51.7 11.8 %collective-permute-start.22 = (bf16[128,1024]{1,0:T(8,128)(2,1)S(1)}, bf16[128,1024]{1,0:T(8,128)(2,1)S(1)}, u32[]{:S(2)}, u32[]{:S(2)}) collective-permute-start(bf16[128,1024]{1,0:T(8,128)(2,1)S(1)} %collective-permute-done.21.refs_12_), channel_id=1, source_target_pairs={{0,14},{2,0},{4,2},{6,4},{8,6},{10,8},{12,10},{14,12},{1,15},{3,1}... | collective-permute-start | bytes 786440 | tf_op jit(solution)/shard_map/ppermute | solution.py:43
  68.4 11.6 %collective-permute-start.5 = (bf16[144,1024]{1,0:T(8,128)(2,1)S(1)}, bf16[144,1024]{1,0:T(8,128)(2,1)S(1)}, u32[]{:S(2)}, u32[]{:S(2)}) collective-permute-start(bf16[144,1024]{1,0:T(8,128)(2,1)S(1)} %collective-permute-done.4.own_ref), channel_id=1, source_target_pairs={{0,1},{1,0},{2,3},{3,2},{4,5},{5,4},{6,7},{7,6},{8,9},{9,8},{10,11... | collective-permute-start | bytes 884744 | tf_op jit(solution)/shard_map/ppermute | solution.py:38
  73.5 12.6 %collective-permute-start.44 = (f32[128,512]{1,0:T(8,128)S(1)}, f32[128,512]{1,0:T(8,128)S(1)}, u32[]{:S(2)}, u32[]{:S(2)}) collective-permute-start(f32[128,512]{1,0:T(8,128)S(1)} %get-tuple-element.84), channel_id=1, source_target_pairs={{0,16},{16,0},{1,17},{17,1},{2,18},{18,2},{3,19},{19,3},{4,20},{20... | collective-permute-start | bytes 786440 | tf_op jit(solution)/shard_map/ppermute | solution.py:38
  77.7 13.9 %collective-permute-start.45 = (f32[128,512]{1,0:T(8,128)S(1)}, f32[128,512]{1,0:T(8,128)S(1)}, u32[]{:S(2)}, u32[]{:S(2)}) collective-permute-start(f32[128,512]{1,0:T(8,128)S(1)} %get-tuple-element.85), channel_id=1, source_target_pairs={{0,48},{16,32},{32,16},{48,0},{1,49},{17,33},{33,17},{49,1},{2,50}... | collective-permute-start | bytes 786440 | tf_op jit(solution)/shard_map/ppermute | solution.py:38
  80.7 16.6 %collective-permute-start.41 = (f32[128,512]{1,0:T(8,128)S(1)}, f32[128,512]{1,0:T(8,128)S(1)}, u32[]{:S(2)}, u32[]{:S(2)}) collective-permute-start(f32[128,512]{1,0:T(8,128)S(1)} %get-tuple-element.80), channel_id=1, source_target_pairs={{0,16},{16,0},{1,17},{17,1},{2,18},{18,2},{3,19},{19,3},{4,20},{20... | collective-permute-start | bytes 786440 | tf_op jit(solution)/shard_map/ppermute | solution.py:38
  82.4 20.4 %collective-permute-start.42 = (f32[128,512]{1,0:T(8,128)S(1)}, f32[128,512]{1,0:T(8,128)S(1)}, u32[]{:S(2)}, u32[]{:S(2)}) collective-permute-start(f32[128,512]{1,0:T(8,128)S(1)} %get-tuple-element.81), channel_id=1, source_target_pairs={{0,48},{16,32},{32,16},{48,0},{1,49},{17,33},{33,17},{49,1},{2,50}... | collective-permute-start | bytes 786440 | tf_op jit(solution)/shard_map/ppermute | solution.py:38
  86.1 18.7 %collective-permute-start.35 = (f32[256,256]{1,0:T(8,128)S(1)}, f32[256,256]{1,0:T(8,128)S(1)}, u32[]{:S(2)}, u32[]{:S(2)}) collective-permute-start(f32[256,256]{1,0:T(8,128)S(1)} %get-tuple-element.72), channel_id=1, source_target_pairs={{0,128},{64,192},{128,0},{192,64},{1,129},{65,193},{129,1},{193,65... | collective-permute-start | bytes 786440 | tf_op jit(solution)/shard_map/ppermute | solution.py:38
  91.6 26.2 %collective-permute-start.16 = (f32[288,256]{1,0:T(8,128)S(1)}, f32[288,256]{1,0:T(8,128)S(1)}, u32[]{:S(2)}, u32[]{:S(2)}) collective-permute-start(f32[288,256]{1,0:T(8,128)S(1)} %get-tuple-element.59), channel_id=1, source_target_pairs={{0,64},{64,0},{128,192},{192,128},{1,65},{65,1},{129,193},{193,129... | collective-permute-start | bytes 884744 | tf_op jit(solution)/shard_map/ppermute | solution.py:38
  91.9 25.9 %collective-permute-start.17 = (f32[288,256]{1,0:T(8,128)S(1)}, f32[288,256]{1,0:T(8,128)S(1)}, u32[]{:S(2)}, u32[]{:S(2)}) collective-permute-start(f32[288,256]{1,0:T(8,128)S(1)} %get-tuple-element.60), channel_id=1, source_target_pairs={{0,128},{64,192},{128,0},{192,64},{1,129},{65,193},{129,1},{193,65... | collective-permute-start | bytes 884744 | tf_op jit(solution)/shard_map/ppermute | solution.py:38
  97.4 20.4 %collective-permute-start.18 = (f32[288,256]{1,0:T(8,128)S(1)}, f32[288,256]{1,0:T(8,128)S(1)}, u32[]{:S(2)}, u32[]{:S(2)}) collective-permute-start(f32[288,256]{1,0:T(8,128)S(1)} %get-tuple-element.61), channel_id=1, source_target_pairs={{0,192},{64,128},{128,64},{192,0},{1,193},{65,129},{129,65},{193,1... | collective-permute-start | bytes 884744 | tf_op jit(solution)/shard_map/ppermute | solution.py:38
  102.8 14.9 %collective-permute-start.36 = (f32[256,256]{1,0:T(8,128)S(1)}, f32[256,256]{1,0:T(8,128)S(1)}, u32[]{:S(2)}, u32[]{:S(2)}) collective-permute-start(f32[256,256]{1,0:T(8,128)S(1)} %get-tuple-element.73), channel_id=1, source_target_pairs={{0,192},{64,128},{128,64},{192,0},{1,193},{65,129},{129,65},{193,1... | collective-permute-start | bytes 786440 | tf_op jit(solution)/shard_map/ppermute | solution.py:38
  104.8 18.9 %collective-permute-start.46 = (f32[128,256]{1,0:T(8,128)S(1)}, f32[128,256]{1,0:T(8,128)S(1)}, u32[]{:S(2)}, u32[]{:S(2)}) collective-permute-start(f32[128,256]{1,0:T(8,128)S(1)} %get-tuple-element.87), channel_id=1, source_target_pairs={{0,64},{64,0},{128,192},{192,128},{1,65},{65,1},{129,193},{193,129... | collective-permute-start | bytes 393224 | tf_op jit(solution)/shard_map/ppermute | solution.py:38
  117.9 12.6 %collective-permute-start.37 = (f32[160,256]{1,0:T(8,128)S(1)}, f32[160,256]{1,0:T(8,128)S(1)}, u32[]{:S(2)}, u32[]{:S(2)}) collective-permute-start(f32[160,256]{1,0:T(8,128)S(1)} %get-tuple-element.75), channel_id=1, source_target_pairs={{0,32},{32,0},{1,33},{33,1},{2,34},{34,2},{3,35},{35,3},{4,36},{36... | collective-permute-start | bytes 491528 | tf_op jit(solution)/shard_map/ppermute | solution.py:38
  118.1 12.4 %collective-permute-start.38 = (f32[160,256]{1,0:T(8,128)S(1)}, f32[160,256]{1,0:T(8,128)S(1)}, u32[]{:S(2)}, u32[]{:S(2)}) collective-permute-start(f32[160,256]{1,0:T(8,128)S(1)} %get-tuple-element.76), channel_id=1, source_target_pairs={{0,16},{16,0},{1,17},{17,1},{2,18},{18,2},{3,19},{19,3},{4,20},{20... | collective-permute-start | bytes 491528 | tf_op jit(solution)/shard_map/ppermute | solution.py:38
  (30 other events, 296.0 us)

commit v5 on v4

--- a/solution.py
+++ b/solution.py
@@ -22,6 +22,7 @@
 F32 = jnp.float32
 BF16 = jnp.bfloat16
 VMEM = pl.BlockSpec(memory_space=pltpu.VMEM)
+BY_X, BY_Y = 112, 144
 STEPS = (0, -1, 1, -2, 2, -3, 3, 4)
 
 
@@ -128,14 +129,14 @@
 
             @pl.when(j == at)
             def _():
-                outs[at][:128, :] = result[:128, :]
-                outs[at][128:256, :] = result[256:384, :]
+                outs[at][:BY_X, :] = result[:BY_X, :]
+                outs[at][BY_X : 2 * BY_X, :] = result[256 : 256 + BY_X, :]
 
         to = pl.multiple_of(j * 128, 128)
         for a in range(2):
             for b in range(2):
                 outs[4 + a * 2 + b][:, pl.ds(to, 128)] = result[
-                    a * 256 + 128 : a * 256 + 256, b * 128 : (b + 1) * 128
+                    a * 256 + BY_X : a * 256 + 256, b * 128 : (b + 1) * 128
                 ]
 
 
@@ -154,12 +155,12 @@
         right = jnp.concatenate([own_ref[:128, columns], swapped_ref[:128, columns]], axis=0)
         for a, left in enumerate((mine_ref, other_ref)):
             result = jnp.dot(left[:, 1792:], right, preferred_element_type=F32)
-            at = slice(a * 128, (a + 1) * 128)
-            outs[j][at, :] = parts[j][at, :] + result[:128]
+            at = slice(a * BY_X, (a + 1) * BY_X)
+            outs[j][at, :] = parts[j][at, :] + result[:BY_X]
             for b in range(2):
                 to = slice(j * 128, (j + 1) * 128)
                 piece = 4 + a * 2 + b
-                outs[piece][:, to] = parts[piece][:, to] + result[128:, b * 128 : (b + 1) * 128]
+                outs[piece][:, to] = parts[piece][:, to] + result[BY_X:, b * 128 : (b + 1) * 128]
     if k == 0:
         late = [(source_of(14), own_ref[128:144, :].astype(F32)), (source_of(15), swapped_ref[128:144, :].astype(F32))]
         total = jnp.zeros((16, 1024), F32)
@@ -170,20 +171,20 @@
             total = total + value
         total = total[:8] + total[8:]
         for q in range(8):
-            at = slice(256 + (q % 4) * 8, 264 + (q % 4) * 8)
+            at = slice(2 * BY_X + (q % 4) * 8, 2 * BY_X + (q % 4) * 8 + 8)
             to = slice((q // 4) * 128, (q // 4) * 128 + 128)
             for j in range(4):
                 outs[j][at, to] = total[:, q * 128 : (q + 1) * 128]
 
 
 def product(k, mine, other, blocks):
-    pieces = [struct((128, 512), F32)] * 4
+    pieces = [struct((BY_Y, 512), F32)] * 4
     scratch = [pltpu.VMEM((1792, 256), BF16), pltpu.VMEM((512, 256), F32)]
     gains = [struct((16, 16, 1024), BF16)] if k == 0 else []
     parts = kernel_call(
         functools.partial(part_kernel, k),
         [VMEM] * 16,
-        [struct((256, 256), F32)] * 4 + pieces + gains,
+        [struct((2 * BY_X, 256), F32)] * 4 + pieces + gains,
         14,
         (2 * 512 * 1792 * 1024, 8 << 20),
         [mine, other, *blocks[:14]],
@@ -192,7 +193,7 @@
     return kernel_call(
         functools.partial(product_kernel, k),
         [VMEM] * (4 + len(parts)),
-        [struct((288 if k == 0 else 256, 256), F32)] * 4 + pieces,
+        [struct((2 * BY_X + (32 if k == 0 else 0), 256), F32)] * 4 + pieces,
         14,
         (2 * 512 * 256 * 1024, 4 << 20),
         [mine, other, *blocks[14:], *parts],
@@ -210,12 +211,12 @@
         total = sum_of(refs[k * 4 : k * 4 + 4])
         for a in range(2):
             for b in range(2):
-                outs[a * 2 + b][:128, k * 128 : (k + 1) * 128] = total[
-                    a * 128 : (a + 1) * 128, b * 128 : (b + 1) * 128
+                outs[a * 2 + b][:BY_X, k * 128 : (k + 1) * 128] = total[
+                    a * BY_X : (a + 1) * BY_X, b * 128 : (b + 1) * 128
                 ]
         if k == 0:
             for out in outs:
-                out[128:160, :] = total[256:288, :]
+                out[BY_X : BY_X + 32, :] = total[2 * BY_X : 2 * BY_X + 32, :]
 
 
 def sum_columns_kernel(*refs):
@@ -234,12 +235,12 @@
 
 def adam_kernel(scale, first_ref, second_ref, *refs):
     pieces, (new_first_ref, new_second_ref, update_ref, gain_ref) = refs[:8], refs[8:]
-    gain = sum_of(pieces[:4], slice(128, 160)) * scale
+    gain = sum_of(pieces[:4], slice(BY_X, BY_X + 32)) * scale
     gain_ref[:32, :] = gain[:, :128]
     gain_ref[32:, :] = gain[:, 128:]
-    for r in range(2):
-        grad = sum_of(pieces[r * 4 : r * 4 + 4], slice(0, 128)) * scale
-        at = (slice(r * 128, (r + 1) * 128), slice(None))
+    for four, start, rows in ((pieces[:4], 0, BY_X), (pieces[4:], BY_X, BY_Y)):
+        grad = sum_of(four, slice(0, rows)) * scale
+        at = (slice(start, start + rows), slice(None))
         new_first = beta_one * first_ref[at] + (1.0 - beta_one) * grad
         new_second = beta_two * second_ref[at] + (1.0 - beta_two) * grad * grad
         new_first_ref[at] = new_first
@@ -292,8 +293,8 @@
         by_x, by_y = outs[:4], outs[4:]
         in_x += [by_x[0]] + [swap(by_x[j], "x", j) for j in (1, 2, 3)]
         in_y += [by_y[0]] + [along_y(by_y[ab], ab) for ab in (1, 2, 3)]
-    by_y = cut_sum(sum_rows_kernel, in_x, 160)
-    by_x = cut_sum(sum_columns_kernel, in_y, 128)
+    by_y = cut_sum(sum_rows_kernel, in_x, BY_X + 32)
+    by_x = cut_sum(sum_columns_kernel, in_y, BY_Y)
     pieces = [by_y[0]] + [along_y(by_y[ab], ab) for ab in (1, 2, 3)]
     pieces += [by_x[0]] + [swap(by_x[j], "x", j) for j in (1, 2, 3)]
     new_first, new_second, update, gain = adam(1.0 / replicas, first_moment, second_moment, pieces)

time: 132 us -> 133 us (level)
  waiting for transfers between devices: 55.4 us -> 64 us
  starting transfers between devices: 62.4 us -> 54.8 us
    ppermute x35, waiting for transfers between devices: 29.8 us -> 38.5 us  [swap(): return lax.ppermute(array, axis, [(i, i ^ mask) for i in range(size)])]
    ppermute x35, starting transfers between devices: 43.1 us -> 35.5 us  [swap(): return lax.ppermute(array, axis, [(i, i ^ mask) for i in range(size)])]
  transfers between devices with their start and end apart: 49 -> 49, of which waited for: 18 -> 21; matrix products, arithmetic and copies ran while one was open for 2% -> 2% of each run, Pallas kernels for 6% -> 6%
where the time goes in v5:
time: 133 us
  waiting for transfers between devices  64 us (48%)
  starting transfers between devices  54.8 us (41%)
  Pallas kernels  9.04 us (7%)
  other arithmetic  2.83 us (2%)
    ppermute x35, waiting for transfers between devices, swap(): return lax.ppermute(array, axis, [(i, i ^ mask) for i in range(size)])  38.5 us
    ppermute x35, starting transfers between devices, swap(): return lax.ppermute(array, axis, [(i, i ^ mask) for i in range(size)])  35.5 us
    ppermute x14, waiting for transfers between devices, shift(): lax.ppermute(array, 'z', [(i, (i + step) % size) for i in range(size)])  25.5 us
    ppermute x14, starting transfers between devices, shift(): lax.ppermute(array, 'z', [(i, (i + step) % size) for i in range(size)])  19.3 us
    pallas_call x11, Pallas kernels, kernel_call(): pl.pallas_call(kernel, in_specs=in_specs, out_specs=[VMEM] * len(out_shap...  9.04 us
    reduce_sum x1, other arithmetic, update_of(): jnp.sum(norm_grad.astype(F32) * normed.astype(F32), axis=1).reshape(64, 128)  2.83 us
  transfers between devices with their start and end apart: 49, of which 21 were waited for; matrix products, arithmetic and copies ran while one was open for 2% of the time, Pallas kernels for 6%

profile of v5, /device:TPU:1, one launch (start us, length us, event | category | flops | bytes accessed | tf_op | source)
XLA Modules:
  0.0 132.6 jit_solution(6516409371555367383)
XLA Ops:
  1.8 6.5 %collective-permute-start.19 = (bf16[128,1024]{1,0:T(8,128)(2,1)S(1)}, bf16[128,1024]{1,0:T(8,128)(2,1)S(1)}, u32[]{:S(2)}, u32[]{:S(2)}) collective-permute-start(bf16[128,1024]{1,0:T(8,128)(2,1)S(1)} %shard_map.98.refs_0_), channel_id=1, source_target_pairs={{0,14},{2,0},{4,2},{6,4},{8,6},{10,8},{12,10},{14,12},{1,15},{3,1}... | collective-permute-start | bytes 786440 | tf_op jit(solution)/shard_map/ppermute | solution.py:44
  9.2 2.8 %multiply_reduce_fusion = f32[8192]{0:T(1024)S(1)} fusion(bf16[1,128,8192]{2,1,0:T(8,128)(2,1)} %param.8, bf16[1,128,8192]{2,1,0:T(8,128)(2,1)} %param.9), kind=kLoop, calls=%fused_computation | loop fusion | flops 4186112 | bytes 4227072 | tf_op jit(solution)/shard_map/reduce_sum | solution.py:268
  13.2 3.4 %collective-permute-start.8 = (bf16[144,1024]{1,0:T(8,128)(2,1)S(1)}, bf16[144,1024]{1,0:T(8,128)(2,1)S(1)}, u32[]{:S(2)}, u32[]{:S(2)}) collective-permute-start(bf16[144,1024]{1,0:T(8,128)(2,1)S(1)} %shard_map.95.refs_0_), channel_id=1, source_target_pairs={{0,14},{2,0},{4,2},{6,4},{8,6},{10,8},{12,10},{14,12},{1,15},{3,1}... | collective-permute-start | bytes 884744 | tf_op jit(solution)/shard_map/ppermute | solution.py:44
  19.6 5.0 %collective-permute-done.1.refs_2_ = bf16[144,1024]{1,0:T(8,128)(2,1)S(1)} collective-permute-done((bf16[144,1024]{1,0:T(8,128)(2,1)S(1)}, bf16[144,1024]{1,0:T(8,128)(2,1)S(1)}, u32[]{:S(2)}, u32[]{:S(2)}) %collective-permute-start.1) | collective-permute-done | bytes 294944 | tf_op jit(solution)/shard_map/ppermute | solution.py:44
  27.1 2.4 %collective-permute-start.7 = (bf16[144,1024]{1,0:T(8,128)(2,1)S(1)}, bf16[144,1024]{1,0:T(8,128)(2,1)S(1)}, u32[]{:S(2)}, u32[]{:S(2)}) collective-permute-start(bf16[144,1024]{1,0:T(8,128)(2,1)S(1)} %collective-permute-done.1.refs_2_), channel_id=1, source_target_pairs={{0,1},{1,0},{2,3},{3,2},{4,5},{5,4},{6,7},{7,6},{8,9},{9,8},{10,11... | collective-permute-start | bytes 884744 | tf_op jit(solution)/shard_map/ppermute | solution.py:39
  29.9 3.0 %collective-permute-start = (bf16[256,2048]{1,0:T(8,128)(2,1)S(1)}, bf16[256,2048]{1,0:T(8,128)(2,1)S(1)}, u32[]{:S(2)}, u32[]{:S(2)}) collective-permute-start(bf16[256,2048]{1,0:T(8,128)(2,1)S(1)} %shard_map.94), channel_id=1, source_target_pairs={{0,16},{16,0},{1,17},{17,1},{2,18},{18,2},{3,19},{19,3},{4,20},{20... | collective-permute-start | bytes 3145736 | tf_op jit(solution)/shard_map/ppermute | solution.py:39
  36.6 4.3 %collective-permute-done.2.refs_6_ = bf16[144,1024]{1,0:T(8,128)(2,1)S(1)} collective-permute-done((bf16[144,1024]{1,0:T(8,128)(2,1)S(1)}, bf16[144,1024]{1,0:T(8,128)(2,1)S(1)}, u32[]{:S(2)}, u32[]{:S(2)}) %collective-permute-start.2) | collective-permute-done | bytes 294944 | tf_op jit(solution)/shard_map/ppermute | solution.py:44
  43.6 4.8 %collective-permute-done.21.refs_12_ = bf16[128,1024]{1,0:T(8,128)(2,1)S(1)} collective-permute-done((bf16[128,1024]{1,0:T(8,128)(2,1)S(1)}, bf16[128,1024]{1,0:T(8,128)(2,1)S(1)}, u32[]{:S(2)}, u32[]{:S(2)}) %collective-permute-start.21) | collective-permute-done | bytes 262176 | tf_op jit(solution)/shard_map/ppermute | solution.py:44
  48.3 3.4 %collective-permute-start.14 = (bf16[144,1024]{1,0:T(8,128)(2,1)S(1)}, bf16[144,1024]{1,0:T(8,128)(2,1)S(1)}, u32[]{:S(2)}, u32[]{:S(2)}) collective-permute-start(bf16[144,1024]{1,0:T(8,128)(2,1)S(1)} %collective-permute-done.11.refs_8_), channel_id=1, source_target_pairs={{0,14},{2,0},{4,2},{6,4},{8,6},{10,8},{12,10},{14,12},{1,15},{3,1}... | collective-permute-start | bytes 884744 | tf_op jit(solution)/shard_map/ppermute | solution.py:44
  51.7 2.7 %collective-permute-start.22 = (bf16[128,1024]{1,0:T(8,128)(2,1)S(1)}, bf16[128,1024]{1,0:T(8,128)(2,1)S(1)}, u32[]{:S(2)}, u32[]{:S(2)}) collective-permute-start(bf16[128,1024]{1,0:T(8,128)(2,1)S(1)} %collective-permute-done.21.refs_12_), channel_id=1, source_target_pairs={{0,14},{2,0},{4,2},{6,4},{8,6},{10,8},{12,10},{14,12},{1,15},{3,1}... | collective-permute-start | bytes 786440 | tf_op jit(solution)/shard_map/ppermute | solution.py:44
  54.4 5.0 %collective-permute-done.31.refs_10_ = bf16[128,1024]{1,0:T(8,128)(2,1)S(1)} collective-permute-done((bf16[128,1024]{1,0:T(8,128)(2,1)S(1)}, bf16[128,1024]{1,0:T(8,128)(2,1)S(1)}, u32[]{:S(2)}, u32[]{:S(2)}) %collective-permute-start.31) | collective-permute-done | bytes 262176 | tf_op jit(solution)/shard_map/ppermute | solution.py:44
  59.4 4.0 %collective-permute-start.32 = (bf16[128,1024]{1,0:T(8,128)(2,1)S(1)}, bf16[128,1024]{1,0:T(8,128)(2,1)S(1)}, u32[]{:S(2)}, u32[]{:S(2)}) collective-permute-start(bf16[128,1024]{1,0:T(8,128)(2,1)S(1)} %collective-permute-done.31.refs_10_), channel_id=1, source_target_pairs={{0,1},{1,0},{2,3},{3,2},{4,5},{5,4},{6,7},{7,6},{8,9},{9,8},{10,11... | collective-permute-start | bytes 786440 | tf_op jit(solution)/shard_map/ppermute | solution.py:39
  65.8 2.2 %collective-permute-start.15 = (bf16[144,1024]{1,0:T(8,128)(2,1)S(1)}, bf16[144,1024]{1,0:T(8,128)(2,1)S(1)}, u32[]{:S(2)}, u32[]{:S(2)}) collective-permute-start(bf16[144,1024]{1,0:T(8,128)(2,1)S(1)} %collective-permute-done.14.refs_12_), channel_id=1, source_target_pairs={{0,1},{1,0},{2,3},{3,2},{4,5},{5,4},{6,7},{7,6},{8,9},{9,8},{10,11... | collective-permute-start | bytes 884744 | tf_op jit(solution)/shard_map/ppermute | solution.py:39
  68.5 2.8 %shard_map.99 = (f32[224,256]{1,0:T(8,128)S(1)}, f32[224,256]{1,0:T(8,128)S(1)}, f32[224,256]{1,0:T(8,128)S(1)}, f32[224,256]{1,0:T(8,128)S(1)}, f32[144,512]{1,...) custom-call(bf16[256,2048]{1,0:T(8,128)(2,1)S(1)} %shard_map.93.mine_ref, ...), custom_call_target="tpu_custom_call" | custom-call | flops 1879048192 | bytes 8388608 | tf_op jit(solution)/shard_map/pallas_call | solution.py:56
  73.2 2.4 %collective-permute-start.35 = (f32[224,256]{1,0:T(8,128)S(1)}, f32[224,256]{1,0:T(8,128)S(1)}, u32[]{:S(2)}, u32[]{:S(2)}) collective-permute-start(f32[224,256]{1,0:T(8,128)S(1)} %get-tuple-element.72), channel_id=1, source_target_pairs={{0,128},{64,192},{128,0},{192,64},{1,129},{65,193},{129,1},{193,65... | collective-permute-start | bytes 688136 | tf_op jit(solution)/shard_map/ppermute | solution.py:39
  76.3 2.9 %shard_map.96 = (f32[224,256]{1,0:T(8,128)S(1)}, f32[224,256]{1,0:T(8,128)S(1)}, f32[224,256]{1,0:T(8,128)S(1)}, f32[224,256]{1,0:T(8,128)S(1)}, f32[144,512]{1,...) custom-call(bf16[256,2048]{1,0:T(8,128)(2,1)S(1)} %shard_map.93.mine, ...), custom_call_target="tpu_custom_call" | custom-call | flops 1879048192 | bytes 8388608 | tf_op jit(solution)/shard_map/pallas_call | solution.py:56
  80.0 3.5 %collective-permute-start.17 = (f32[256,256]{1,0:T(8,128)S(1)}, f32[256,256]{1,0:T(8,128)S(1)}, u32[]{:S(2)}, u32[]{:S(2)}) collective-permute-start(f32[256,256]{1,0:T(8,128)S(1)} %get-tuple-element.60), channel_id=1, source_target_pairs={{0,128},{64,192},{128,0},{192,64},{1,129},{65,193},{129,1},{193,65... | collective-permute-start | bytes 786440 | tf_op jit(solution)/shard_map/ppermute | solution.py:39
  83.5 2.3 %collective-permute-done.35.refs_6_ = f32[224,256]{1,0:T(8,128)S(1)} collective-permute-done((f32[224,256]{1,0:T(8,128)S(1)}, f32[224,256]{1,0:T(8,128)S(1)}, u32[]{:S(2)}, u32[]{:S(2)}) %collective-permute-start.35) | collective-permute-done | bytes 229408 | tf_op jit(solution)/shard_map/ppermute | solution.py:39
  88.5 2.2 %collective-permute-start.45 = (f32[144,512]{1,0:T(8,128)S(1)}, f32[144,512]{1,0:T(8,128)S(1)}, u32[]{:S(2)}, u32[]{:S(2)}) collective-permute-start(f32[144,512]{1,0:T(8,128)S(1)} %get-tuple-element.85), channel_id=1, source_target_pairs={{0,48},{16,32},{32,16},{48,0},{1,49},{17,33},{33,17},{49,1},{2,50}... | collective-permute-start | bytes 884744 | tf_op jit(solution)/shard_map/ppermute | solution.py:39
  90.8 6.3 %collective-permute-done.17.refs_2_ = f32[256,256]{1,0:T(8,128)S(1)} collective-permute-done((f32[256,256]{1,0:T(8,128)S(1)}, f32[256,256]{1,0:T(8,128)S(1)}, u32[]{:S(2)}, u32[]{:S(2)}) %collective-permute-start.17) | collective-permute-done | bytes 262176 | tf_op jit(solution)/shard_map/ppermute | solution.py:39
  100.1 6.7 %collective-permute-done.45.refs_7_ = f32[144,512]{1,0:T(8,128)S(1)} collective-permute-done((f32[144,512]{1,0:T(8,128)S(1)}, f32[144,512]{1,0:T(8,128)S(1)}, u32[]{:S(2)}, u32[]{:S(2)}) %collective-permute-start.45) | collective-permute-done | bytes 294944 | tf_op jit(solution)/shard_map/ppermute | solution.py:39
  109.0 11.5 %collective-permute-done.42.refs_3_ = f32[144,512]{1,0:T(8,128)S(1)} collective-permute-done((f32[144,512]{1,0:T(8,128)S(1)}, f32[144,512]{1,0:T(8,128)S(1)}, u32[]{:S(2)}, u32[]{:S(2)}) %collective-permute-start.42) | collective-permute-done | bytes 294944 | tf_op jit(solution)/shard_map/ppermute | solution.py:39
  125.6 3.4 %collective-permute-done.47.refs_6_ = f32[144,256]{1,0:T(8,128)S(1)} collective-permute-done((f32[144,256]{1,0:T(8,128)S(1)}, f32[144,256]{1,0:T(8,128)S(1)}, u32[]{:S(2)}, u32[]{:S(2)}) %collective-permute-start.47) | collective-permute-done | bytes 147488 | tf_op jit(solution)/shard_map/ppermute | solution.py:39
  129.0 2.6 %collective-permute-done.48.refs_7_ = f32[144,256]{1,0:T(8,128)S(1)} collective-permute-done((f32[144,256]{1,0:T(8,128)S(1)}, f32[144,256]{1,0:T(8,128)S(1)}, u32[]{:S(2)}, u32[]{:S(2)}) %collective-permute-start.48) | collective-permute-done | bytes 147488 | tf_op jit(solution)/shard_map/ppermute | solution.py:39
  (96 shorter events, 35.6 us)
Async XLA Ops:
  1.8 11.5 %collective-permute-start.19 = (bf16[128,1024]{1,0:T(8,128)(2,1)S(1)}, bf16[128,1024]{1,0:T(8,128)(2,1)S(1)}, u32[]{:S(2)}, u32[]{:S(2)}) collective-permute-start(bf16[128,1024]{1,0:T(8,128)(2,1)S(1)} %shard_map.98.refs_0_), channel_id=1, source_target_pairs={{0,14},{2,0},{4,2},{6,4},{8,6},{10,8},{12,10},{14,12},{1,15},{3,1}... | collective-permute-start | bytes 786440 | tf_op jit(solution)/shard_map/ppermute | solution.py:44
  12.1 12.5 %collective-permute-start.1 = (bf16[144,1024]{1,0:T(8,128)(2,1)S(1)}, bf16[144,1024]{1,0:T(8,128)(2,1)S(1)}, u32[]{:S(2)}, u32[]{:S(2)}) collective-permute-start(bf16[144,1024]{1,0:T(8,128)(2,1)S(1)} %shard_map.95.refs_0_), channel_id=1, source_target_pairs={{0,2},{2,4},{4,6},{6,8},{8,10},{10,12},{12,14},{14,0},{1,3},{3,5},... | collective-permute-start | bytes 884744 | tf_op jit(solution)/shard_map/ppermute | solution.py:44
  12.2 13.2 %collective-permute-start.6 = (bf16[144,1024]{1,0:T(8,128)(2,1)S(1)}, bf16[144,1024]{1,0:T(8,128)(2,1)S(1)}, u32[]{:S(2)}, u32[]{:S(2)}) collective-permute-start(bf16[144,1024]{1,0:T(8,128)(2,1)S(1)} %shard_map.95.refs_0_), channel_id=1, source_target_pairs={{0,1},{1,0},{2,3},{3,2},{4,5},{5,4},{6,7},{7,6},{8,9},{9,8},{10,11... | collective-permute-start | bytes 884744 | tf_op jit(solution)/shard_map/ppermute | solution.py:39
  13.2 12.2 %collective-permute-start.8 = (bf16[144,1024]{1,0:T(8,128)(2,1)S(1)}, bf16[144,1024]{1,0:T(8,128)(2,1)S(1)}, u32[]{:S(2)}, u32[]{:S(2)}) collective-permute-start(bf16[144,1024]{1,0:T(8,128)(2,1)S(1)} %shard_map.95.refs_0_), channel_id=1, source_target_pairs={{0,14},{2,0},{4,2},{6,4},{8,6},{10,8},{12,10},{14,12},{1,15},{3,1}... | collective-permute-start | bytes 884744 | tf_op jit(solution)/shard_map/ppermute | solution.py:44
  18.3 11.6 %collective-permute-start.26 = (bf16[128,1024]{1,0:T(8,128)(2,1)S(1)}, bf16[128,1024]{1,0:T(8,128)(2,1)S(1)}, u32[]{:S(2)}, u32[]{:S(2)}) collective-permute-start(bf16[128,1024]{1,0:T(8,128)(2,1)S(1)} %collective-permute-done.25.refs_2_), channel_id=1, source_target_pairs={{0,1},{1,0},{2,3},{3,2},{4,5},{5,4},{6,7},{7,6},{8,9},{9,8},{10,11... | collective-permute-start | bytes 786440 | tf_op jit(solution)/shard_map/ppermute | solution.py:39
  25.5 15.4 %collective-permute-start.2 = (bf16[144,1024]{1,0:T(8,128)(2,1)S(1)}, bf16[144,1024]{1,0:T(8,128)(2,1)S(1)}, u32[]{:S(2)}, u32[]{:S(2)}) collective-permute-start(bf16[144,1024]{1,0:T(8,128)(2,1)S(1)} %collective-permute-done.1.refs_2_), channel_id=1, source_target_pairs={{0,2},{2,4},{4,6},{6,8},{8,10},{10,12},{12,14},{14,0},{1,3},{3,5},... | collective-permute-start | bytes 884744 | tf_op jit(solution)/shard_map/ppermute | solution.py:44
  27.1 13.8 %collective-permute-start.7 = (bf16[144,1024]{1,0:T(8,128)(2,1)S(1)}, bf16[144,1024]{1,0:T(8,128)(2,1)S(1)}, u32[]{:S(2)}, u32[]{:S(2)}) collective-permute-start(bf16[144,1024]{1,0:T(8,128)(2,1)S(1)} %collective-permute-done.1.refs_2_), channel_id=1, source_target_pairs={{0,1},{1,0},{2,3},{3,2},{4,5},{5,4},{6,7},{7,6},{8,9},{9,8},{10,11... | collective-permute-start | bytes 884744 | tf_op jit(solution)/shard_map/ppermute | solution.py:39
  29.9 34.7 %collective-permute-start = (bf16[256,2048]{1,0:T(8,128)(2,1)S(1)}, bf16[256,2048]{1,0:T(8,128)(2,1)S(1)}, u32[]{:S(2)}, u32[]{:S(2)}) collective-permute-start(bf16[256,2048]{1,0:T(8,128)(2,1)S(1)} %shard_map.94), channel_id=1, source_target_pairs={{0,16},{16,0},{1,17},{17,1},{2,18},{18,2},{3,19},{19,3},{4,20},{20... | collective-permute-start | bytes 3145736 | tf_op jit(solution)/shard_map/ppermute | solution.py:39
  42.7 11.7 %collective-permute-start.3 = (bf16[144,1024]{1,0:T(8,128)(2,1)S(1)}, bf16[144,1024]{1,0:T(8,128)(2,1)S(1)}, u32[]{:S(2)}, u32[]{:S(2)}) collective-permute-start(bf16[144,1024]{1,0:T(8,128)(2,1)S(1)} %collective-permute-done.2.refs_6_), channel_id=1, source_target_pairs={{0,2},{2,4},{4,6},{6,8},{8,10},{10,12},{12,14},{14,0},{1,3},{3,5},... | collective-permute-start | bytes 884744 | tf_op jit(solution)/shard_map/ppermute | solution.py:44
  48.3 15.2 %collective-permute-start.14 = (bf16[144,1024]{1,0:T(8,128)(2,1)S(1)}, bf16[144,1024]{1,0:T(8,128)(2,1)S(1)}, u32[]{:S(2)}, u32[]{:S(2)}) collective-permute-start(bf16[144,1024]{1,0:T(8,128)(2,1)S(1)} %collective-permute-done.11.refs_8_), channel_id=1, source_target_pairs={{0,14},{2,0},{4,2},{6,4},{8,6},{10,8},{12,10},{14,12},{1,15},{3,1}... | collective-permute-start | bytes 884744 | tf_op jit(solution)/shard_map/ppermute | solution.py:44
  51.7 11.8 %collective-permute-start.22 = (bf16[128,1024]{1,0:T(8,128)(2,1)S(1)}, bf16[128,1024]{1,0:T(8,128)(2,1)S(1)}, u32[]{:S(2)}, u32[]{:S(2)}) collective-permute-start(bf16[128,1024]{1,0:T(8,128)(2,1)S(1)} %collective-permute-done.21.refs_12_), channel_id=1, source_target_pairs={{0,14},{2,0},{4,2},{6,4},{8,6},{10,8},{12,10},{14,12},{1,15},{3,1}... | collective-permute-start | bytes 786440 | tf_op jit(solution)/shard_map/ppermute | solution.py:44
  73.2 12.6 %collective-permute-start.35 = (f32[224,256]{1,0:T(8,128)S(1)}, f32[224,256]{1,0:T(8,128)S(1)}, u32[]{:S(2)}, u32[]{:S(2)}) collective-permute-start(f32[224,256]{1,0:T(8,128)S(1)} %get-tuple-element.72), channel_id=1, source_target_pairs={{0,128},{64,192},{128,0},{192,64},{1,129},{65,193},{129,1},{193,65... | collective-permute-start | bytes 688136 | tf_op jit(solution)/shard_map/ppermute | solution.py:39
  75.6 12.4 %collective-permute-start.36 = (f32[224,256]{1,0:T(8,128)S(1)}, f32[224,256]{1,0:T(8,128)S(1)}, u32[]{:S(2)}, u32[]{:S(2)}) collective-permute-start(f32[224,256]{1,0:T(8,128)S(1)} %get-tuple-element.73), channel_id=1, source_target_pairs={{0,192},{64,128},{128,64},{192,0},{1,193},{65,129},{129,65},{193,1... | collective-permute-start | bytes 688136 | tf_op jit(solution)/shard_map/ppermute | solution.py:39
  75.8 12.7 %collective-permute-start.43 = (f32[144,512]{1,0:T(8,128)S(1)}, f32[144,512]{1,0:T(8,128)S(1)}, u32[]{:S(2)}, u32[]{:S(2)}) collective-permute-start(f32[144,512]{1,0:T(8,128)S(1)} %get-tuple-element.83), channel_id=1, source_target_pairs={{0,32},{32,0},{1,33},{33,1},{2,34},{34,2},{3,35},{35,3},{4,36},{36... | collective-permute-start | bytes 884744 | tf_op jit(solution)/shard_map/ppermute | solution.py:39
  80.0 17.1 %collective-permute-start.17 = (f32[256,256]{1,0:T(8,128)S(1)}, f32[256,256]{1,0:T(8,128)S(1)}, u32[]{:S(2)}, u32[]{:S(2)}) collective-permute-start(f32[256,256]{1,0:T(8,128)S(1)} %get-tuple-element.60), channel_id=1, source_target_pairs={{0,128},{64,192},{128,0},{192,64},{1,129},{65,193},{129,1},{193,65... | collective-permute-start | bytes 786440 | tf_op jit(solution)/shard_map/ppermute | solution.py:39
  85.8 12.9 %collective-permute-start.18 = (f32[256,256]{1,0:T(8,128)S(1)}, f32[256,256]{1,0:T(8,128)S(1)}, u32[]{:S(2)}, u32[]{:S(2)}) collective-permute-start(f32[256,256]{1,0:T(8,128)S(1)} %get-tuple-element.61), channel_id=1, source_target_pairs={{0,192},{64,128},{128,64},{192,0},{1,193},{65,129},{129,65},{193,1... | collective-permute-start | bytes 786440 | tf_op jit(solution)/shard_map/ppermute | solution.py:39
  88.0 12.0 %collective-permute-start.44 = (f32[144,512]{1,0:T(8,128)S(1)}, f32[144,512]{1,0:T(8,128)S(1)}, u32[]{:S(2)}, u32[]{:S(2)}) collective-permute-start(f32[144,512]{1,0:T(8,128)S(1)} %get-tuple-element.84), channel_id=1, source_target_pairs={{0,16},{16,0},{1,17},{17,1},{2,18},{18,2},{3,19},{19,3},{4,20},{20... | collective-permute-start | bytes 884744 | tf_op jit(solution)/shard_map/ppermute | solution.py:39
  88.5 18.3 %collective-permute-start.45 = (f32[144,512]{1,0:T(8,128)S(1)}, f32[144,512]{1,0:T(8,128)S(1)}, u32[]{:S(2)}, u32[]{:S(2)}) collective-permute-start(f32[144,512]{1,0:T(8,128)S(1)} %get-tuple-element.85), channel_id=1, source_target_pairs={{0,48},{16,32},{32,16},{48,0},{1,49},{17,33},{33,17},{49,1},{2,50}... | collective-permute-start | bytes 884744 | tf_op jit(solution)/shard_map/ppermute | solution.py:39
  90.8 16.6 %collective-permute-start.40 = (f32[144,512]{1,0:T(8,128)S(1)}, f32[144,512]{1,0:T(8,128)S(1)}, u32[]{:S(2)}, u32[]{:S(2)}) collective-permute-start(f32[144,512]{1,0:T(8,128)S(1)} %get-tuple-element.79), channel_id=1, source_target_pairs={{0,32},{32,0},{1,33},{33,1},{2,34},{34,2},{3,35},{35,3},{4,36},{36... | collective-permute-start | bytes 884744 | tf_op jit(solution)/shard_map/ppermute | solution.py:39
  97.1 11.9 %collective-permute-start.41 = (f32[144,512]{1,0:T(8,128)S(1)}, f32[144,512]{1,0:T(8,128)S(1)}, u32[]{:S(2)}, u32[]{:S(2)}) collective-permute-start(f32[144,512]{1,0:T(8,128)S(1)} %get-tuple-element.80), channel_id=1, source_target_pairs={{0,16},{16,0},{1,17},{17,1},{2,18},{18,2},{3,19},{19,3},{4,20},{20... | collective-permute-start | bytes 884744 | tf_op jit(solution)/shard_map/ppermute | solution.py:39
  98.7 21.8 %collective-permute-start.42 = (f32[144,512]{1,0:T(8,128)S(1)}, f32[144,512]{1,0:T(8,128)S(1)}, u32[]{:S(2)}, u32[]{:S(2)}) collective-permute-start(f32[144,512]{1,0:T(8,128)S(1)} %get-tuple-element.81), channel_id=1, source_target_pairs={{0,48},{16,32},{32,16},{48,0},{1,49},{17,33},{33,17},{49,1},{2,50}... | collective-permute-start | bytes 884744 | tf_op jit(solution)/shard_map/ppermute | solution.py:39
  100.0 22.5 %collective-permute-start.37 = (f32[144,256]{1,0:T(8,128)S(1)}, f32[144,256]{1,0:T(8,128)S(1)}, u32[]{:S(2)}, u32[]{:S(2)}) collective-permute-start(f32[144,256]{1,0:T(8,128)S(1)} %get-tuple-element.75), channel_id=1, source_target_pairs={{0,32},{32,0},{1,33},{33,1},{2,34},{34,2},{3,35},{35,3},{4,36},{36... | collective-permute-start | bytes 442376 | tf_op jit(solution)/shard_map/ppermute | solution.py:39
  106.8 17.9 %collective-permute-start.38 = (f32[144,256]{1,0:T(8,128)S(1)}, f32[144,256]{1,0:T(8,128)S(1)}, u32[]{:S(2)}, u32[]{:S(2)}) collective-permute-start(f32[144,256]{1,0:T(8,128)S(1)} %get-tuple-element.76), channel_id=1, source_target_pairs={{0,16},{16,0},{1,17},{17,1},{2,18},{18,2},{3,19},{19,3},{4,20},{20... | collective-permute-start | bytes 442376 | tf_op jit(solution)/shard_map/ppermute | solution.py:39
  107.4 17.3 %collective-permute-start.39 = (f32[144,256]{1,0:T(8,128)S(1)}, f32[144,256]{1,0:T(8,128)S(1)}, u32[]{:S(2)}, u32[]{:S(2)}) collective-permute-start(f32[144,256]{1,0:T(8,128)S(1)} %get-tuple-element.77), channel_id=1, source_target_pairs={{0,48},{16,32},{32,16},{48,0},{1,49},{17,33},{33,17},{49,1},{2,50}... | collective-permute-start | bytes 442376 | tf_op jit(solution)/shard_map/ppermute | solution.py:39
  (30 other events, 312.2 us)

commit v6 on v5

--- a/solution.py
+++ b/solution.py
@@ -220,27 +220,29 @@
 
 
 def sum_columns_kernel(*refs):
-    outs = refs[8:]
-    for k in range(2):
-        total = sum_of(refs[k * 4 : k * 4 + 4])
-        for j in range(4):
-            outs[j][:, k * 128 : (k + 1) * 128] = total[:, j * 128 : (j + 1) * 128]
-
-
-def cut_sum(kernel, parts, rows):
-    return kernel_call(
-        kernel, [VMEM] * 8, [struct((rows, 256), F32)] * 4, 5, (1 << 18, 1 << 20), parts
+    total = sum_of(refs[:4])
+    for j in range(4):
+        refs[4 + j][...] = total[:, j * 128 : (j + 1) * 128]
+
+
+def cut_sum(kernel, parts, shape):
+    return kernel_call(
+        kernel, [VMEM] * len(parts), [struct(shape, F32)] * 4, 5, (1 << 18, 1 << 20), parts
     )
 
 
 def adam_kernel(scale, first_ref, second_ref, *refs):
-    pieces, (new_first_ref, new_second_ref, update_ref, gain_ref) = refs[:8], refs[8:]
+    pieces, (new_first_ref, new_second_ref, update_ref, gain_ref) = refs[:12], refs[12:]
     gain = sum_of(pieces[:4], slice(BY_X, BY_X + 32)) * scale
     gain_ref[:32, :] = gain[:, :128]
     gain_ref[32:, :] = gain[:, 128:]
-    for four, start, rows in ((pieces[:4], 0, BY_X), (pieces[4:], BY_X, BY_Y)):
+    for four, start, rows, columns in (
+        (pieces[:4], 0, BY_X, slice(None)),
+        (pieces[4:8], BY_X, BY_Y, slice(0, 128)),
+        (pieces[8:], BY_X, BY_Y, slice(128, 256)),
+    ):
         grad = sum_of(four, slice(0, rows)) * scale
-        at = (slice(start, start + rows), slice(None))
+        at = (slice(start, start + rows), columns)
         new_first = beta_one * first_ref[at] + (1.0 - beta_one) * grad
         new_second = beta_two * second_ref[at] + (1.0 - beta_two) * grad * grad
         new_first_ref[at] = new_first
@@ -251,7 +253,7 @@
 def adam(scale, first_old, second_old, pieces):
     return kernel_call(
         functools.partial(adam_kernel, scale),
-        [VMEM] * 10,
+        [VMEM] * 14,
         [struct((256, 256), F32)] * 3 + [struct((64, 128), F32)],
         5,
         (1 << 20, 2 << 20),
@@ -293,10 +295,11 @@
         by_x, by_y = outs[:4], outs[4:]
         in_x += [by_x[0]] + [swap(by_x[j], "x", j) for j in (1, 2, 3)]
         in_y += [by_y[0]] + [along_y(by_y[ab], ab) for ab in (1, 2, 3)]
-    by_y = cut_sum(sum_rows_kernel, in_x, BY_X + 32)
-    by_x = cut_sum(sum_columns_kernel, in_y, BY_Y)
+    by_y = cut_sum(sum_rows_kernel, in_x, (BY_X + 32, 256))
     pieces = [by_y[0]] + [along_y(by_y[ab], ab) for ab in (1, 2, 3)]
-    pieces += [by_x[0]] + [swap(by_x[j], "x", j) for j in (1, 2, 3)]
+    for k in range(2):
+        by_x = cut_sum(sum_columns_kernel, in_y[k * 4 : k * 4 + 4], (BY_Y, 128))
+        pieces += [by_x[0]] + [swap(by_x[j], "x", j) for j in (1, 2, 3)]
     new_first, new_second, update, gain = adam(1.0 / replicas, first_moment, second_moment, pieces)
     return (new_first[None], new_second[None], update[None], gain.reshape(1, 8192))
 

time: 133 us -> 119 us (0.89); the launches traced: 133 us -> 117 us
  waiting for transfers between devices: 64 us -> 34.3 us
  starting transfers between devices: 54.8 us -> 68.6 us
    ppermute x35 -> x38, waiting for transfers between devices: 38.5 us -> 21.6 us  [swap(): return lax.ppermute(array, axis, [(i, i ^ mask) for i in range(size)])]
    ppermute x14, waiting for transfers between devices: 25.5 us -> 12.6 us  [shift(): lax.ppermute(array, 'z', [(i, (i + step) % size) for i in range(size)])]
    ppermute x35 -> x38, starting transfers between devices: 35.5 us -> 45 us  [swap(): return lax.ppermute(array, axis, [(i, i ^ mask) for i in range(size)])]
    ppermute x14, starting transfers between devices: 19.3 us -> 23.6 us  [shift(): lax.ppermute(array, 'z', [(i, (i + step) % size) for i in range(size)])]
    pallas_call x11 -> x12, Pallas kernels: 9.04 us -> 9.07 us  [kernel_call(): pl.pallas_call(kernel, in_specs=in_specs, out_specs=[VMEM] * len(out_shap...]
  transfers between devices with their start and end apart: 49 -> 52, of which waited for: 21 -> 15; matrix products, arithmetic and copies ran while one was open for 2% -> 2% of each run, Pallas kernels for 6% -> 7%
where the time goes in v6:
time: 119 us; the launch traced here: 117 us
  starting transfers between devices  68.6 us (58%)
  waiting for transfers between devices  34.3 us (29%)
  Pallas kernels  9.07 us (8%)
  other arithmetic  2.83 us (2%)
    ppermute x38, starting transfers between devices, swap(): return lax.ppermute(array, axis, [(i, i ^ mask) for i in range(size)])  45 us
    ppermute x14, starting transfers between devices, shift(): lax.ppermute(array, 'z', [(i, (i + step) % size) for i in range(size)])  23.6 us
    ppermute x38, waiting for transfers between devices, swap(): return lax.ppermute(array, axis, [(i, i ^ mask) for i in range(size)])  21.6 us
    ppermute x14, waiting for transfers between devices, shift(): lax.ppermute(array, 'z', [(i, (i + step) % size) for i in range(size)])  12.6 us
    pallas_call x12, Pallas kernels, kernel_call(): pl.pallas_call(kernel, in_specs=in_specs, out_specs=[VMEM] * len(out_shap...  9.07 us
    reduce_sum x1, other arithmetic, update_of(): jnp.sum(norm_grad.astype(F32) * normed.astype(F32), axis=1).reshape(64, 128)  2.83 us
  transfers between devices with their start and end apart: 52, of which 15 were waited for; matrix products, arithmetic and copies ran while one was open for 2% of the time, Pallas kernels for 7%

profile of v6, /device:TPU:1, one launch (start us, length us, event | category | flops | bytes accessed | tf_op | source)
XLA Modules:
  0.0 116.7 jit_solution(10906425189215574521)
XLA Ops:
  1.8 6.5 %collective-permute-start.19 = (bf16[128,1024]{1,0:T(8,128)(2,1)S(1)}, bf16[128,1024]{1,0:T(8,128)(2,1)S(1)}, u32[]{:S(2)}, u32[]{:S(2)}) collective-permute-start(bf16[128,1024]{1,0:T(8,128)(2,1)S(1)} %shard_map.98.refs_0_), channel_id=1, source_target_pairs={{0,14},{2,0},{4,2},{6,4},{8,6},{10,8},{12,10},{14,12},{1,15},{3,1}... | collective-permute-start | bytes 786440 | tf_op jit(solution)/shard_map/ppermute | solution.py:44
  8.2 2.8 %multiply_reduce_fusion = f32[8192]{0:T(1024)S(1)} fusion(bf16[1,128,8192]{2,1,0:T(8,128)(2,1)} %param.8, bf16[1,128,8192]{2,1,0:T(8,128)(2,1)} %param.9), kind=kLoop, calls=%fused_computation | loop fusion | flops 4186112 | bytes 4227072 | tf_op jit(solution)/shard_map/reduce_sum | solution.py:270
  12.3 3.0 %collective-permute-start.8 = (bf16[144,1024]{1,0:T(8,128)(2,1)S(1)}, bf16[144,1024]{1,0:T(8,128)(2,1)S(1)}, u32[]{:S(2)}, u32[]{:S(2)}) collective-permute-start(bf16[144,1024]{1,0:T(8,128)(2,1)S(1)} %shard_map.95.refs_0_), channel_id=1, source_target_pairs={{0,14},{2,0},{4,2},{6,4},{8,6},{10,8},{12,10},{14,12},{1,15},{3,1}... | collective-permute-start | bytes 884744 | tf_op jit(solution)/shard_map/ppermute | solution.py:44
  18.2 4.5 %collective-permute-done.1.refs_2_ = bf16[144,1024]{1,0:T(8,128)(2,1)S(1)} collective-permute-done((bf16[144,1024]{1,0:T(8,128)(2,1)S(1)}, bf16[144,1024]{1,0:T(8,128)(2,1)S(1)}, u32[]{:S(2)}, u32[]{:S(2)}) %collective-permute-start.1) | collective-permute-done | bytes 294944 | tf_op jit(solution)/shard_map/ppermute | solution.py:44
  22.7 3.2 %collective-permute-start.26 = (bf16[128,1024]{1,0:T(8,128)(2,1)S(1)}, bf16[128,1024]{1,0:T(8,128)(2,1)S(1)}, u32[]{:S(2)}, u32[]{:S(2)}) collective-permute-start(bf16[128,1024]{1,0:T(8,128)(2,1)S(1)} %collective-permute-done.25.refs_2_), channel_id=1, source_target_pairs={{0,1},{1,0},{2,3},{3,2},{4,5},{5,4},{6,7},{7,6},{8,9},{9,8},{10,11... | collective-permute-start | bytes 786440 | tf_op jit(solution)/shard_map/ppermute | solution.py:39
  27.1 3.4 %collective-permute-start.11 = (bf16[144,1024]{1,0:T(8,128)(2,1)S(1)}, bf16[144,1024]{1,0:T(8,128)(2,1)S(1)}, u32[]{:S(2)}, u32[]{:S(2)}) collective-permute-start(bf16[144,1024]{1,0:T(8,128)(2,1)S(1)} %collective-permute-done.8.refs_4_), channel_id=1, source_target_pairs={{0,14},{2,0},{4,2},{6,4},{8,6},{10,8},{12,10},{14,12},{1,15},{3,1}... | collective-permute-start | bytes 884744 | tf_op jit(solution)/shard_map/ppermute | solution.py:44
  32.2 3.0 %collective-permute-start = (bf16[256,2048]{1,0:T(8,128)(2,1)S(1)}, bf16[256,2048]{1,0:T(8,128)(2,1)S(1)}, u32[]{:S(2)}, u32[]{:S(2)}) collective-permute-start(bf16[256,2048]{1,0:T(8,128)(2,1)S(1)} %shard_map.94), channel_id=1, source_target_pairs={{0,16},{16,0},{1,17},{17,1},{2,18},{18,2},{3,19},{19,3},{4,20},{20... | collective-permute-start | bytes 3145736 | tf_op jit(solution)/shard_map/ppermute | solution.py:39
  38.8 2.3 %collective-permute-start.3 = (bf16[144,1024]{1,0:T(8,128)(2,1)S(1)}, bf16[144,1024]{1,0:T(8,128)(2,1)S(1)}, u32[]{:S(2)}, u32[]{:S(2)}) collective-permute-start(bf16[144,1024]{1,0:T(8,128)(2,1)S(1)} %collective-permute-done.2.refs_6_), channel_id=1, source_target_pairs={{0,2},{2,4},{4,6},{6,8},{8,10},{10,12},{12,14},{14,0},{1,3},{3,5},... | collective-permute-start | bytes 884744 | tf_op jit(solution)/shard_map/ppermute | solution.py:44
  42.2 3.2 %collective-permute-start.14 = (bf16[144,1024]{1,0:T(8,128)(2,1)S(1)}, bf16[144,1024]{1,0:T(8,128)(2,1)S(1)}, u32[]{:S(2)}, u32[]{:S(2)}) collective-permute-start(bf16[144,1024]{1,0:T(8,128)(2,1)S(1)} %collective-permute-done.11.refs_8_), channel_id=1, source_target_pairs={{0,14},{2,0},{4,2},{6,4},{8,6},{10,8},{12,10},{14,12},{1,15},{3,1}... | collective-permute-start | bytes 884744 | tf_op jit(solution)/shard_map/ppermute | solution.py:44
  45.5 4.1 %collective-permute-start.30 = (bf16[128,1024]{1,0:T(8,128)(2,1)S(1)}, bf16[128,1024]{1,0:T(8,128)(2,1)S(1)}, u32[]{:S(2)}, u32[]{:S(2)}) collective-permute-start(bf16[128,1024]{1,0:T(8,128)(2,1)S(1)} %collective-permute-done.20.refs_8_), channel_id=1, source_target_pairs={{0,1},{1,0},{2,3},{3,2},{4,5},{5,4},{6,7},{7,6},{8,9},{9,8},{10,11... | collective-permute-start | bytes 786440 | tf_op jit(solution)/shard_map/ppermute | solution.py:39
  53.1 4.4 %collective-permute-done.22.own_ref = bf16[128,1024]{1,0:T(8,128)(2,1)S(1)} collective-permute-done((bf16[128,1024]{1,0:T(8,128)(2,1)S(1)}, bf16[128,1024]{1,0:T(8,128)(2,1)S(1)}, u32[]{:S(2)}, u32[]{:S(2)}) %collective-permute-start.22) | collective-permute-done | bytes 262176 | tf_op jit(solution)/shard_map/ppermute | solution.py:44
  60.1 2.2 %collective-permute-start.15 = (bf16[144,1024]{1,0:T(8,128)(2,1)S(1)}, bf16[144,1024]{1,0:T(8,128)(2,1)S(1)}, u32[]{:S(2)}, u32[]{:S(2)}) collective-permute-start(bf16[144,1024]{1,0:T(8,128)(2,1)S(1)} %collective-permute-done.14.refs_12_), channel_id=1, source_target_pairs={{0,1},{1,0},{2,3},{3,2},{4,5},{5,4},{6,7},{7,6},{8,9},{9,8},{10,11... | collective-permute-start | bytes 884744 | tf_op jit(solution)/shard_map/ppermute | solution.py:39
  62.6 2.8 %shard_map.99 = (f32[224,256]{1,0:T(8,128)S(1)}, f32[224,256]{1,0:T(8,128)S(1)}, f32[224,256]{1,0:T(8,128)S(1)}, f32[224,256]{1,0:T(8,128)S(1)}, f32[144,512]{1,...) custom-call(bf16[256,2048]{1,0:T(8,128)(2,1)S(1)} %shard_map.93.mine_ref, ...), custom_call_target="tpu_custom_call" | custom-call | flops 1879048192 | bytes 8388608 | tf_op jit(solution)/shard_map/pallas_call | solution.py:56
  67.3 2.4 %collective-permute-start.35 = (f32[224,256]{1,0:T(8,128)S(1)}, f32[224,256]{1,0:T(8,128)S(1)}, u32[]{:S(2)}, u32[]{:S(2)}) collective-permute-start(f32[224,256]{1,0:T(8,128)S(1)} %get-tuple-element.76), channel_id=1, source_target_pairs={{0,128},{64,192},{128,0},{192,64},{1,129},{65,193},{129,1},{193,65... | collective-permute-start | bytes 688136 | tf_op jit(solution)/shard_map/ppermute | solution.py:39
  71.5 2.6 %collective-permute-start.47 = (f32[144,512]{1,0:T(8,128)S(1)}, f32[144,512]{1,0:T(8,128)S(1)}, u32[]{:S(2)}, u32[]{:S(2)}) collective-permute-start(f32[144,512]{1,0:T(8,128)S(1)} %get-tuple-element.92), channel_id=1, source_target_pairs={{0,16},{16,0},{1,17},{17,1},{2,18},{18,2},{3,19},{19,3},{4,20},{20... | collective-permute-start | bytes 884744 | tf_op jit(solution)/shard_map/ppermute | solution.py:39
  74.2 2.9 %shard_map.96 = (f32[224,256]{1,0:T(8,128)S(1)}, f32[224,256]{1,0:T(8,128)S(1)}, f32[224,256]{1,0:T(8,128)S(1)}, f32[224,256]{1,0:T(8,128)S(1)}, f32[144,512]{1,...) custom-call(bf16[256,2048]{1,0:T(8,128)(2,1)S(1)} %shard_map.93.mine, ...), custom_call_target="tpu_custom_call" | custom-call | flops 1879048192 | bytes 8388608 | tf_op jit(solution)/shard_map/pallas_call | solution.py:56
  79.9 4.1 %collective-permute-done.36.refs_7_ = f32[224,256]{1,0:T(8,128)S(1)} collective-permute-done((f32[224,256]{1,0:T(8,128)S(1)}, f32[224,256]{1,0:T(8,128)S(1)}, u32[]{:S(2)}, u32[]{:S(2)}) %collective-permute-start.36) | collective-permute-done | bytes 229408 | tf_op jit(solution)/shard_map/ppermute | solution.py:39
  85.1 1.8 %collective-permute-start.18 = (f32[256,256]{1,0:T(8,128)S(1)}, f32[256,256]{1,0:T(8,128)S(1)}, u32[]{:S(2)}, u32[]{:S(2)}) collective-permute-start(f32[256,256]{1,0:T(8,128)S(1)} %get-tuple-element.65), channel_id=1, source_target_pairs={{0,192},{64,128},{128,64},{192,0},{1,193},{65,129},{129,65},{193,1... | collective-permute-start | bytes 786440 | tf_op jit(solution)/shard_map/ppermute | solution.py:39
  87.0 2.8 %collective-permute-start.40 = (f32[144,512]{1,0:T(8,128)S(1)}, f32[144,512]{1,0:T(8,128)S(1)}, u32[]{:S(2)}, u32[]{:S(2)}) collective-permute-start(f32[144,512]{1,0:T(8,128)S(1)} %get-tuple-element.83), channel_id=1, source_target_pairs={{0,32},{32,0},{1,33},{33,1},{2,34},{34,2},{3,35},{35,3},{4,36},{36... | collective-permute-start | bytes 884744 | tf_op jit(solution)/shard_map/ppermute | solution.py:39
  89.8 1.8 %collective-permute-start.41 = (f32[144,512]{1,0:T(8,128)S(1)}, f32[144,512]{1,0:T(8,128)S(1)}, u32[]{:S(2)}, u32[]{:S(2)}) collective-permute-start(f32[144,512]{1,0:T(8,128)S(1)} %get-tuple-element.84), channel_id=1, source_target_pairs={{0,16},{16,0},{1,17},{17,1},{2,18},{18,2},{3,19},{19,3},{4,20},{20... | collective-permute-start | bytes 884744 | tf_op jit(solution)/shard_map/ppermute | solution.py:39
  92.5 7.2 %collective-permute-done.18.refs_3_ = f32[256,256]{1,0:T(8,128)S(1)} collective-permute-done((f32[256,256]{1,0:T(8,128)S(1)}, f32[256,256]{1,0:T(8,128)S(1)}, u32[]{:S(2)}, u32[]{:S(2)}) %collective-permute-start.18) | collective-permute-done | bytes 262176 | tf_op jit(solution)/shard_map/ppermute | solution.py:39
  100.7 2.5 %collective-permute-done.41.refs_2_ = f32[144,512]{1,0:T(8,128)S(1)} collective-permute-done((f32[144,512]{1,0:T(8,128)S(1)}, f32[144,512]{1,0:T(8,128)S(1)}, u32[]{:S(2)}, u32[]{:S(2)}) %collective-permute-start.41) | collective-permute-done | bytes 294944 | tf_op jit(solution)/shard_map/ppermute | solution.py:39
  107.5 2.5 %collective-permute-start.44 = (f32[144,128]{1,0:T(8,128)S(1)}, f32[144,128]{1,0:T(8,128)S(1)}, u32[]{:S(2)}, u32[]{:S(2)}) collective-permute-start(f32[144,128]{1,0:T(8,128)S(1)} %get-tuple-element.88), channel_id=1, source_target_pairs={{0,128},{64,192},{128,0},{192,64},{1,129},{65,193},{129,1},{193,65... | collective-permute-start | bytes 221192 | tf_op jit(solution)/shard_map/ppermute | solution.py:39
  112.2 2.5 %collective-permute-done.45.refs_7_ = f32[144,128]{1,0:T(8,128)S(1)} collective-permute-done((f32[144,128]{1,0:T(8,128)S(1)}, f32[144,128]{1,0:T(8,128)S(1)}, u32[]{:S(2)}, u32[]{:S(2)}) %collective-permute-start.45) | collective-permute-done | bytes 73760 | tf_op jit(solution)/shard_map/ppermute | solution.py:39
  (103 shorter events, 37.2 us)
Async XLA Ops:
  1.8 13.5 %collective-permute-start.19 = (bf16[128,1024]{1,0:T(8,128)(2,1)S(1)}, bf16[128,1024]{1,0:T(8,128)(2,1)S(1)}, u32[]{:S(2)}, u32[]{:S(2)}) collective-permute-start(bf16[128,1024]{1,0:T(8,128)(2,1)S(1)} %shard_map.98.refs_0_), channel_id=1, source_target_pairs={{0,14},{2,0},{4,2},{6,4},{8,6},{10,8},{12,10},{14,12},{1,15},{3,1}... | collective-permute-start | bytes 786440 | tf_op jit(solution)/shard_map/ppermute | solution.py:44
  11.2 11.5 %collective-permute-start.1 = (bf16[144,1024]{1,0:T(8,128)(2,1)S(1)}, bf16[144,1024]{1,0:T(8,128)(2,1)S(1)}, u32[]{:S(2)}, u32[]{:S(2)}) collective-permute-start(bf16[144,1024]{1,0:T(8,128)(2,1)S(1)} %shard_map.95.refs_0_), channel_id=1, source_target_pairs={{0,2},{2,4},{4,6},{6,8},{8,10},{10,12},{12,14},{14,0},{1,3},{3,5},... | collective-permute-start | bytes 884744 | tf_op jit(solution)/shard_map/ppermute | solution.py:44
  12.3 13.6 %collective-permute-start.8 = (bf16[144,1024]{1,0:T(8,128)(2,1)S(1)}, bf16[144,1024]{1,0:T(8,128)(2,1)S(1)}, u32[]{:S(2)}, u32[]{:S(2)}) collective-permute-start(bf16[144,1024]{1,0:T(8,128)(2,1)S(1)} %shard_map.95.refs_0_), channel_id=1, source_target_pairs={{0,14},{2,0},{4,2},{6,4},{8,6},{10,8},{12,10},{14,12},{1,15},{3,1}... | collective-permute-start | bytes 884744 | tf_op jit(solution)/shard_map/ppermute | solution.py:44
  15.3 10.7 %collective-permute-start.6 = (bf16[144,1024]{1,0:T(8,128)(2,1)S(1)}, bf16[144,1024]{1,0:T(8,128)(2,1)S(1)}, u32[]{:S(2)}, u32[]{:S(2)}) collective-permute-start(bf16[144,1024]{1,0:T(8,128)(2,1)S(1)} %shard_map.95.refs_0_), channel_id=1, source_target_pairs={{0,1},{1,0},{2,3},{3,2},{4,5},{5,4},{6,7},{7,6},{8,9},{9,8},{10,11... | collective-permute-start | bytes 884744 | tf_op jit(solution)/shard_map/ppermute | solution.py:39
  16.4 10.8 %collective-permute-start.20 = (bf16[128,1024]{1,0:T(8,128)(2,1)S(1)}, bf16[128,1024]{1,0:T(8,128)(2,1)S(1)}, u32[]{:S(2)}, u32[]{:S(2)}) collective-permute-start(bf16[128,1024]{1,0:T(8,128)(2,1)S(1)} %collective-permute-done.19.refs_4_), channel_id=1, source_target_pairs={{0,14},{2,0},{4,2},{6,4},{8,6},{10,8},{12,10},{14,12},{1,15},{3,1}... | collective-permute-start | bytes 786440 | tf_op jit(solution)/shard_map/ppermute | solution.py:44
  18.2 12.4 %collective-permute-start.28 = (bf16[128,1024]{1,0:T(8,128)(2,1)S(1)}, bf16[128,1024]{1,0:T(8,128)(2,1)S(1)}, u32[]{:S(2)}, u32[]{:S(2)}) collective-permute-start(bf16[128,1024]{1,0:T(8,128)(2,1)S(1)} %collective-permute-done.25.refs_2_), channel_id=1, source_target_pairs={{0,2},{2,4},{4,6},{6,8},{8,10},{10,12},{12,14},{14,0},{1,3},{3,5},... | collective-permute-start | bytes 786440 | tf_op jit(solution)/shard_map/ppermute | solution.py:44
  32.2 26.7 %collective-permute-start = (bf16[256,2048]{1,0:T(8,128)(2,1)S(1)}, bf16[256,2048]{1,0:T(8,128)(2,1)S(1)}, u32[]{:S(2)}, u32[]{:S(2)}) collective-permute-start(bf16[256,2048]{1,0:T(8,128)(2,1)S(1)} %shard_map.94), channel_id=1, source_target_pairs={{0,16},{16,0},{1,17},{17,1},{2,18},{18,2},{3,19},{19,3},{4,20},{20... | collective-permute-start | bytes 3145736 | tf_op jit(solution)/shard_map/ppermute | solution.py:39
  37.0 12.6 %collective-permute-start.29 = (bf16[128,1024]{1,0:T(8,128)(2,1)S(1)}, bf16[128,1024]{1,0:T(8,128)(2,1)S(1)}, u32[]{:S(2)}, u32[]{:S(2)}) collective-permute-start(bf16[128,1024]{1,0:T(8,128)(2,1)S(1)} %collective-permute-done.28.refs_6_), channel_id=1, source_target_pairs={{0,1},{1,0},{2,3},{3,2},{4,5},{5,4},{6,7},{7,6},{8,9},{9,8},{10,11... | collective-permute-start | bytes 786440 | tf_op jit(solution)/shard_map/ppermute | solution.py:39
  38.8 12.9 %collective-permute-start.3 = (bf16[144,1024]{1,0:T(8,128)(2,1)S(1)}, bf16[144,1024]{1,0:T(8,128)(2,1)S(1)}, u32[]{:S(2)}, u32[]{:S(2)}) collective-permute-start(bf16[144,1024]{1,0:T(8,128)(2,1)S(1)} %collective-permute-done.2.refs_6_), channel_id=1, source_target_pairs={{0,2},{2,4},{4,6},{6,8},{8,10},{10,12},{12,14},{14,0},{1,3},{3,5},... | collective-permute-start | bytes 884744 | tf_op jit(solution)/shard_map/ppermute | solution.py:44
  58.8 10.9 %collective-permute-start.13 = (bf16[144,1024]{1,0:T(8,128)(2,1)S(1)}, bf16[144,1024]{1,0:T(8,128)(2,1)S(1)}, u32[]{:S(2)}, u32[]{:S(2)}) collective-permute-start(bf16[144,1024]{1,0:T(8,128)(2,1)S(1)} %collective-permute-done.3.refs_10_), channel_id=1, source_target_pairs={{0,1},{1,0},{2,3},{3,2},{4,5},{5,4},{6,7},{7,6},{8,9},{9,8},{10,11... | collective-permute-start | bytes 884744 | tf_op jit(solution)/shard_map/ppermute | solution.py:39
  60.1 11.5 %collective-permute-start.15 = (bf16[144,1024]{1,0:T(8,128)(2,1)S(1)}, bf16[144,1024]{1,0:T(8,128)(2,1)S(1)}, u32[]{:S(2)}, u32[]{:S(2)}) collective-permute-start(bf16[144,1024]{1,0:T(8,128)(2,1)S(1)} %collective-permute-done.14.refs_12_), channel_id=1, source_target_pairs={{0,1},{1,0},{2,3},{3,2},{4,5},{5,4},{6,7},{7,6},{8,9},{9,8},{10,11... | collective-permute-start | bytes 884744 | tf_op jit(solution)/shard_map/ppermute | solution.py:39
  62.3 11.9 %collective-permute-start.5 = (bf16[144,1024]{1,0:T(8,128)(2,1)S(1)}, bf16[144,1024]{1,0:T(8,128)(2,1)S(1)}, u32[]{:S(2)}, u32[]{:S(2)}) collective-permute-start(bf16[144,1024]{1,0:T(8,128)(2,1)S(1)} %collective-permute-done.4.own_ref), channel_id=1, source_target_pairs={{0,1},{1,0},{2,3},{3,2},{4,5},{5,4},{6,7},{7,6},{8,9},{9,8},{10,11... | collective-permute-start | bytes 884744 | tf_op jit(solution)/shard_map/ppermute | solution.py:39
  66.0 11.1 %collective-permute-start.34 = (f32[224,256]{1,0:T(8,128)S(1)}, f32[224,256]{1,0:T(8,128)S(1)}, u32[]{:S(2)}, u32[]{:S(2)}) collective-permute-start(f32[224,256]{1,0:T(8,128)S(1)} %get-tuple-element.75), channel_id=1, source_target_pairs={{0,64},{64,0},{128,192},{192,128},{1,65},{65,1},{129,193},{193,129... | collective-permute-start | bytes 688136 | tf_op jit(solution)/shard_map/ppermute | solution.py:39
  67.3 12.5 %collective-permute-start.35 = (f32[224,256]{1,0:T(8,128)S(1)}, f32[224,256]{1,0:T(8,128)S(1)}, u32[]{:S(2)}, u32[]{:S(2)}) collective-permute-start(f32[224,256]{1,0:T(8,128)S(1)} %get-tuple-element.76), channel_id=1, source_target_pairs={{0,128},{64,192},{128,0},{192,64},{1,129},{65,193},{129,1},{193,65... | collective-permute-start | bytes 688136 | tf_op jit(solution)/shard_map/ppermute | solution.py:39
  69.8 15.3 %collective-permute-start.46 = (f32[144,512]{1,0:T(8,128)S(1)}, f32[144,512]{1,0:T(8,128)S(1)}, u32[]{:S(2)}, u32[]{:S(2)}) collective-permute-start(f32[144,512]{1,0:T(8,128)S(1)} %get-tuple-element.91), channel_id=1, source_target_pairs={{0,32},{32,0},{1,33},{33,1},{2,34},{34,2},{3,35},{35,3},{4,36},{36... | collective-permute-start | bytes 884744 | tf_op jit(solution)/shard_map/ppermute | solution.py:39
  71.5 15.4 %collective-permute-start.47 = (f32[144,512]{1,0:T(8,128)S(1)}, f32[144,512]{1,0:T(8,128)S(1)}, u32[]{:S(2)}, u32[]{:S(2)}) collective-permute-start(f32[144,512]{1,0:T(8,128)S(1)} %get-tuple-element.92), channel_id=1, source_target_pairs={{0,16},{16,0},{1,17},{17,1},{2,18},{18,2},{3,19},{19,3},{4,20},{20... | collective-permute-start | bytes 884744 | tf_op jit(solution)/shard_map/ppermute | solution.py:39
  74.2 15.6 %collective-permute-start.48 = (f32[144,512]{1,0:T(8,128)S(1)}, f32[144,512]{1,0:T(8,128)S(1)}, u32[]{:S(2)}, u32[]{:S(2)}) collective-permute-start(f32[144,512]{1,0:T(8,128)S(1)} %get-tuple-element.93), channel_id=1, source_target_pairs={{0,48},{16,32},{32,16},{48,0},{1,49},{17,33},{33,17},{49,1},{2,50}... | collective-permute-start | bytes 884744 | tf_op jit(solution)/shard_map/ppermute | solution.py:39
  79.9 11.7 %collective-permute-start.16 = (f32[256,256]{1,0:T(8,128)S(1)}, f32[256,256]{1,0:T(8,128)S(1)}, u32[]{:S(2)}, u32[]{:S(2)}) collective-permute-start(f32[256,256]{1,0:T(8,128)S(1)} %get-tuple-element.63), channel_id=1, source_target_pairs={{0,64},{64,0},{128,192},{192,128},{1,65},{65,1},{129,193},{193,129... | collective-permute-start | bytes 786440 | tf_op jit(solution)/shard_map/ppermute | solution.py:39
  85.1 14.5 %collective-permute-start.18 = (f32[256,256]{1,0:T(8,128)S(1)}, f32[256,256]{1,0:T(8,128)S(1)}, u32[]{:S(2)}, u32[]{:S(2)}) collective-permute-start(f32[256,256]{1,0:T(8,128)S(1)} %get-tuple-element.65), channel_id=1, source_target_pairs={{0,192},{64,128},{128,64},{192,0},{1,193},{65,129},{129,65},{193,1... | collective-permute-start | bytes 786440 | tf_op jit(solution)/shard_map/ppermute | solution.py:39
  87.0 13.6 %collective-permute-start.40 = (f32[144,512]{1,0:T(8,128)S(1)}, f32[144,512]{1,0:T(8,128)S(1)}, u32[]{:S(2)}, u32[]{:S(2)}) collective-permute-start(f32[144,512]{1,0:T(8,128)S(1)} %get-tuple-element.83), channel_id=1, source_target_pairs={{0,32},{32,0},{1,33},{33,1},{2,34},{34,2},{3,35},{35,3},{4,36},{36... | collective-permute-start | bytes 884744 | tf_op jit(solution)/shard_map/ppermute | solution.py:39
  89.8 13.5 %collective-permute-start.41 = (f32[144,512]{1,0:T(8,128)S(1)}, f32[144,512]{1,0:T(8,128)S(1)}, u32[]{:S(2)}, u32[]{:S(2)}) collective-permute-start(f32[144,512]{1,0:T(8,128)S(1)} %get-tuple-element.84), channel_id=1, source_target_pairs={{0,16},{16,0},{1,17},{17,1},{2,18},{18,2},{3,19},{19,3},{4,20},{20... | collective-permute-start | bytes 884744 | tf_op jit(solution)/shard_map/ppermute | solution.py:39
  91.6 14.5 %collective-permute-start.42 = (f32[144,512]{1,0:T(8,128)S(1)}, f32[144,512]{1,0:T(8,128)S(1)}, u32[]{:S(2)}, u32[]{:S(2)}) collective-permute-start(f32[144,512]{1,0:T(8,128)S(1)} %get-tuple-element.85), channel_id=1, source_target_pairs={{0,48},{16,32},{32,16},{48,0},{1,49},{17,33},{33,17},{49,1},{2,50}... | collective-permute-start | bytes 884744 | tf_op jit(solution)/shard_map/ppermute | solution.py:39
  92.4 13.9 %collective-permute-start.49 = (f32[144,128]{1,0:T(8,128)S(1)}, f32[144,128]{1,0:T(8,128)S(1)}, u32[]{:S(2)}, u32[]{:S(2)}) collective-permute-start(f32[144,128]{1,0:T(8,128)S(1)} %get-tuple-element.95), channel_id=1, source_target_pairs={{0,64},{64,0},{128,192},{192,128},{1,65},{65,1},{129,193},{193,129... | collective-permute-start | bytes 221192 | tf_op jit(solution)/shard_map/ppermute | solution.py:39
  103.3 11.4 %collective-permute-start.37 = (f32[144,256]{1,0:T(8,128)S(1)}, f32[144,256]{1,0:T(8,128)S(1)}, u32[]{:S(2)}, u32[]{:S(2)}) collective-permute-start(f32[144,256]{1,0:T(8,128)S(1)} %get-tuple-element.79), channel_id=1, source_target_pairs={{0,32},{32,0},{1,33},{33,1},{2,34},{34,2},{3,35},{35,3},{4,36},{36... | collective-permute-start | bytes 442376 | tf_op jit(solution)/shard_map/ppermute | solution.py:39
  (33 other events, 292.1 us)

commit v7 on v5

--- a/solution.py
+++ b/solution.py
@@ -145,14 +145,14 @@
     return ((z + STEPS[i // 2] + 8) % 8) * 2 + (c ^ (i % 2))
 
 
-def product_kernel(k, mine_ref, other_ref, own_ref, swapped_ref, *refs):
-    parts, refs = refs[:8], refs[8:]
+def product_kernel(k, mine_ref, other_ref, *refs):
+    late, parts, refs = refs[: 2 + 2 * k], refs[2 + 2 * k : 10 + 2 * k], refs[10 + 2 * k :]
     if k == 0:
         gains_ref, refs = refs[0], refs[1:]
     outs = refs
     for j in range(4):
         columns = slice(j * 256, (j + 1) * 256)
-        right = jnp.concatenate([own_ref[:128, columns], swapped_ref[:128, columns]], axis=0)
+        right = jnp.concatenate([ref[: 128 // (1 + k), columns] for ref in late], axis=0)
         for a, left in enumerate((mine_ref, other_ref)):
             result = jnp.dot(left[:, 1792:], right, preferred_element_type=F32)
             at = slice(a * BY_X, (a + 1) * BY_X)
@@ -162,7 +162,7 @@
                 piece = 4 + a * 2 + b
                 outs[piece][:, to] = parts[piece][:, to] + result[BY_X:, b * 128 : (b + 1) * 128]
     if k == 0:
-        late = [(source_of(14), own_ref[128:144, :].astype(F32)), (source_of(15), swapped_ref[128:144, :].astype(F32))]
+        late = [(source_of(14 + i), ref[128:144, :].astype(F32)) for i, ref in enumerate(late)]
         total = jnp.zeros((16, 1024), F32)
         for i in range(16):
             value = gains_ref[i].astype(F32)
@@ -177,7 +177,7 @@
                 outs[j][at, to] = total[:, q * 128 : (q + 1) * 128]
 
 
-def product(k, mine, other, blocks):
+def product(k, mine, other, blocks, last):
     pieces = [struct((BY_Y, 512), F32)] * 4
     scratch = [pltpu.VMEM((1792, 256), BF16), pltpu.VMEM((512, 256), F32)]
     gains = [struct((16, 16, 1024), BF16)] if k == 0 else []
@@ -187,16 +187,16 @@
         [struct((2 * BY_X, 256), F32)] * 4 + pieces + gains,
         14,
         (2 * 512 * 1792 * 1024, 8 << 20),
-        [mine, other, *blocks[:14]],
+        [mine, other, *blocks],
         scratch,
     )
     return kernel_call(
         functools.partial(product_kernel, k),
-        [VMEM] * (4 + len(parts)),
+        [VMEM] * (2 + len(last) + len(parts)),
         [struct((2 * BY_X + (32 if k == 0 else 0), 256), F32)] * 4 + pieces,
         14,
         (2 * 512 * 256 * 1024, 4 << 20),
-        [mine, other, *blocks[14:], *parts],
+        [mine, other, *last, *parts],
     )
 
 
@@ -271,17 +271,18 @@
     def gathered(k):
         own = {0: starts[k]}
         up = down = starts[k]
-        for step in (1, 2, 3, 4):
-            if step < 4 or k == 0:
-                up = shift(up, 1)
-                own[4 if step == 4 else -step] = up
-            if step < 4 or k == 1:
-                down = shift(down, -1)
-                own[step] = down
+        for step in (1, 2, 3):
+            up = shift(up, 1)
+            down = shift(down, -1)
+            own[-step], own[step] = up, down
+        if k == 0:
+            last = [shift(up, 1)]
+        else:
+            last = [shift(up[:64], 1), shift(down[64:], -1)]
         blocks = []
-        for step in STEPS:
+        for step in STEPS[:-1]:
             blocks += [own[step], swap(own[step], "c", 1)]
-        return blocks
+        return blocks, last + [swap(half, "c", 1) for half in last]
 
     gathers = [gathered(k) for k in range(2)]
     mine = turned(inputs, 0)
@@ -289,7 +290,7 @@
 
     in_x, in_y = [], []
     for k in range(2):
-        outs = product(k, mine, other, gathers[k])
+        outs = product(k, mine, other, *gathers[k])
         by_x, by_y = outs[:4], outs[4:]
         in_x += [by_x[0]] + [swap(by_x[j], "x", j) for j in (1, 2, 3)]
         in_y += [by_y[0]] + [along_y(by_y[ab], ab) for ab in (1, 2, 3)]

time: 133 us -> 134 us (level)
  starting transfers between devices: 54.8 us -> 57 us
    ppermute x14 -> x15, starting transfers between devices: 19.3 us -> 22.4 us  [shift(): lax.ppermute(array, 'z', [(i, (i + step) % size) for i in range(size)])]
    ppermute x14 -> x15, waiting for transfers between devices: 25.5 us -> 24 us  [shift(): lax.ppermute(array, 'z', [(i, (i + step) % size) for i in range(size)])]
    ppermute x35 -> x36, starting transfers between devices: 35.5 us -> 34.6 us  [swap(): return lax.ppermute(array, axis, [(i, i ^ mask) for i in range(size)])]
    ppermute x35 -> x36, waiting for transfers between devices: 38.5 us -> 39.2 us  [swap(): return lax.ppermute(array, axis, [(i, i ^ mask) for i in range(size)])]
  transfers between devices with their start and end apart: 49 -> 51, of which waited for: 21 -> 19; matrix products, arithmetic and copies ran while one was open for 2% -> 2% of each run, Pallas kernels for 6% -> 6%
where the time goes in v7:
time: 134 us
  waiting for transfers between devices  63.2 us (47%)
  starting transfers between devices  57 us (43%)
  Pallas kernels  9.03 us (7%)
  other arithmetic  2.82 us (2%)
    ppermute x36, waiting for transfers between devices, swap(): return lax.ppermute(array, axis, [(i, i ^ mask) for i in range(size)])  39.2 us
    ppermute x36, starting transfers between devices, swap(): return lax.ppermute(array, axis, [(i, i ^ mask) for i in range(size)])  34.6 us
    ppermute x15, waiting for transfers between devices, shift(): lax.ppermute(array, 'z', [(i, (i + step) % size) for i in range(size)])  24 us
    ppermute x15, starting transfers between devices, shift(): lax.ppermute(array, 'z', [(i, (i + step) % size) for i in range(size)])  22.4 us
    pallas_call x11, Pallas kernels, kernel_call(): pl.pallas_call(kernel, in_specs=in_specs, out_specs=[VMEM] * len(out_shap...  9.03 us
    reduce_sum x1, other arithmetic, update_of(): jnp.sum(norm_grad.astype(F32) * normed.astype(F32), axis=1).reshape(64, 128)  2.82 us
  transfers between devices with their start and end apart: 51, of which 19 were waited for; matrix products, arithmetic and copies ran while one was open for 2% of the time, Pallas kernels for 6%

profile of v7, /device:TPU:1, one launch (start us, length us, event | category | flops | bytes accessed | tf_op | source)
XLA Modules:
  0.0 134.1 jit_solution(1591514336493076387)
XLA Ops:
  1.8 2.5 %collective-permute-start.19 = (bf16[128,1024]{1,0:T(8,128)(2,1)S(1)}, bf16[128,1024]{1,0:T(8,128)(2,1)S(1)}, u32[]{:S(2)}, u32[]{:S(2)}) collective-permute-start(bf16[128,1024]{1,0:T(8,128)(2,1)S(1)} %shard_map.98.refs_0_), channel_id=1, source_target_pairs={{0,2},{2,4},{4,6},{6,8},{8,10},{10,12},{12,14},{14,0},{1,3},{3,5},... | collective-permute-start | bytes 786440 | tf_op jit(solution)/shard_map/ppermute | solution.py:44
  4.3 4.0 %collective-permute-start.23 = (bf16[128,1024]{1,0:T(8,128)(2,1)S(1)}, bf16[128,1024]{1,0:T(8,128)(2,1)S(1)}, u32[]{:S(2)}, u32[]{:S(2)}) collective-permute-start(bf16[128,1024]{1,0:T(8,128)(2,1)S(1)} %shard_map.98.refs_0_), channel_id=1, source_target_pairs={{0,14},{2,0},{4,2},{6,4},{8,6},{10,8},{12,10},{14,12},{1,15},{3,1}... | collective-permute-start | bytes 786440 | tf_op jit(solution)/shard_map/ppermute | solution.py:44
  9.3 2.8 %multiply_reduce_fusion = f32[8192]{0:T(1024)S(1)} fusion(bf16[1,128,8192]{2,1,0:T(8,128)(2,1)} %param.8, bf16[1,128,8192]{2,1,0:T(8,128)(2,1)} %param.9), kind=kLoop, calls=%fused_computation | loop fusion | flops 4186112 | bytes 4227072 | tf_op jit(solution)/shard_map/reduce_sum | solution.py:268
  18.1 3.9 %collective-permute-done.1.refs_2_ = bf16[144,1024]{1,0:T(8,128)(2,1)S(1)} collective-permute-done((bf16[144,1024]{1,0:T(8,128)(2,1)S(1)}, bf16[144,1024]{1,0:T(8,128)(2,1)S(1)}, u32[]{:S(2)}, u32[]{:S(2)}) %collective-permute-start.1) | collective-permute-done | bytes 294944 | tf_op jit(solution)/shard_map/ppermute | solution.py:44
  23.5 4.2 %collective-permute-done.20.refs_6_ = bf16[128,1024]{1,0:T(8,128)(2,1)S(1)} collective-permute-done((bf16[128,1024]{1,0:T(8,128)(2,1)S(1)}, bf16[128,1024]{1,0:T(8,128)(2,1)S(1)}, u32[]{:S(2)}, u32[]{:S(2)}) %collective-permute-start.20) | collective-permute-done | bytes 262176 | tf_op jit(solution)/shard_map/ppermute | solution.py:44
  29.4 3.0 %collective-permute-start = (bf16[256,2048]{1,0:T(8,128)(2,1)S(1)}, bf16[256,2048]{1,0:T(8,128)(2,1)S(1)}, u32[]{:S(2)}, u32[]{:S(2)}) collective-permute-start(bf16[256,2048]{1,0:T(8,128)(2,1)S(1)} %shard_map.94), channel_id=1, source_target_pairs={{0,16},{16,0},{1,17},{17,1},{2,18},{18,2},{3,19},{19,3},{4,20},{20... | collective-permute-start | bytes 3145736 | tf_op jit(solution)/shard_map/ppermute | solution.py:39
  34.9 2.7 %collective-permute-start.25 = (bf16[128,1024]{1,0:T(8,128)(2,1)S(1)}, bf16[128,1024]{1,0:T(8,128)(2,1)S(1)}, u32[]{:S(2)}, u32[]{:S(2)}) collective-permute-start(bf16[128,1024]{1,0:T(8,128)(2,1)S(1)} %collective-permute-done.24.refs_8_), channel_id=1, source_target_pairs={{0,14},{2,0},{4,2},{6,4},{8,6},{10,8},{12,10},{14,12},{1,15},{3,1}... | collective-permute-start | bytes 786440 | tf_op jit(solution)/shard_map/ppermute | solution.py:44
  38.5 2.7 %collective-permute-done.11.refs_8_ = bf16[144,1024]{1,0:T(8,128)(2,1)S(1)} collective-permute-done((bf16[144,1024]{1,0:T(8,128)(2,1)S(1)}, bf16[144,1024]{1,0:T(8,128)(2,1)S(1)}, u32[]{:S(2)}, u32[]{:S(2)}) %collective-permute-start.11) | collective-permute-done | bytes 294944 | tf_op jit(solution)/shard_map/ppermute | solution.py:44
  43.6 3.2 %collective-permute-done.25.refs_12_ = bf16[128,1024]{1,0:T(8,128)(2,1)S(1)} collective-permute-done((bf16[128,1024]{1,0:T(8,128)(2,1)S(1)}, bf16[128,1024]{1,0:T(8,128)(2,1)S(1)}, u32[]{:S(2)}, u32[]{:S(2)}) %collective-permute-start.25) | collective-permute-done | bytes 262176 | tf_op jit(solution)/shard_map/ppermute | solution.py:44
  46.8 3.4 %collective-permute-start.14 = (bf16[144,1024]{1,0:T(8,128)(2,1)S(1)}, bf16[144,1024]{1,0:T(8,128)(2,1)S(1)}, u32[]{:S(2)}, u32[]{:S(2)}) collective-permute-start(bf16[144,1024]{1,0:T(8,128)(2,1)S(1)} %collective-permute-done.11.refs_8_), channel_id=1, source_target_pairs={{0,14},{2,0},{4,2},{6,4},{8,6},{10,8},{12,10},{14,12},{1,15},{3,1}... | collective-permute-start | bytes 884744 | tf_op jit(solution)/shard_map/ppermute | solution.py:44
  50.3 2.7 %collective-permute-start.26 = (bf16[64,1024]{1,0:T(8,128)(2,1)S(1)}, bf16[64,1024]{1,0:T(8,128)(2,1)S(1)}, u32[]{:S(2)}, u32[]{:S(2)}) collective-permute-start(bf16[64,1024]{1,0:T(8,128)(2,1)S(1)} %slice.9), channel_id=1, source_target_pairs={{0,14},{2,0},{4,2},{6,4},{8,6},{10,8},{12,10},{14,12},{1,15},{3,1}... | collective-permute-start | bytes 393224 | tf_op jit(solution)/shard_map/ppermute | solution.py:44
  53.1 2.5 %collective-permute-done.22.refs_0_ = bf16[64,1024]{1,0:T(8,128)(2,1)S(1)} collective-permute-done((bf16[64,1024]{1,0:T(8,128)(2,1)S(1)}, bf16[64,1024]{1,0:T(8,128)(2,1)S(1)}, u32[]{:S(2)}, u32[]{:S(2)}) %collective-permute-start.22) | collective-permute-done | bytes 131104 | tf_op jit(solution)/shard_map/ppermute | solution.py:44
  63.4 4.8 %collective-permute-done.4.refs_0_ = bf16[144,1024]{1,0:T(8,128)(2,1)S(1)} collective-permute-done((bf16[144,1024]{1,0:T(8,128)(2,1)S(1)}, bf16[144,1024]{1,0:T(8,128)(2,1)S(1)}, u32[]{:S(2)}, u32[]{:S(2)}) %collective-permute-start.4) | collective-permute-done | bytes 294944 | tf_op jit(solution)/shard_map/ppermute | solution.py:44
  70.2 2.8 %shard_map.99 = (f32[224,256]{1,0:T(8,128)S(1)}, f32[224,256]{1,0:T(8,128)S(1)}, f32[224,256]{1,0:T(8,128)S(1)}, f32[224,256]{1,0:T(8,128)S(1)}, f32[144,512]{1,...) custom-call(bf16[256,2048]{1,0:T(8,128)(2,1)S(1)} %shard_map.93.mine_ref, ...), custom_call_target="tpu_custom_call" | custom-call | flops 1879048192 | bytes 8388608 | tf_op jit(solution)/shard_map/pallas_call | solution.py:56
  74.9 2.4 %collective-permute-start.37 = (f32[224,256]{1,0:T(8,128)S(1)}, f32[224,256]{1,0:T(8,128)S(1)}, u32[]{:S(2)}, u32[]{:S(2)}) collective-permute-start(f32[224,256]{1,0:T(8,128)S(1)} %get-tuple-element.72), channel_id=1, source_target_pairs={{0,128},{64,192},{128,0},{192,64},{1,129},{65,193},{129,1},{193,65... | collective-permute-start | bytes 688136 | tf_op jit(solution)/shard_map/ppermute | solution.py:39
  78.0 2.9 %shard_map.96 = (f32[224,256]{1,0:T(8,128)S(1)}, f32[224,256]{1,0:T(8,128)S(1)}, f32[224,256]{1,0:T(8,128)S(1)}, f32[224,256]{1,0:T(8,128)S(1)}, f32[144,512]{1,...) custom-call(bf16[256,2048]{1,0:T(8,128)(2,1)S(1)} %shard_map.93.mine, ...), custom_call_target="tpu_custom_call" | custom-call | flops 1879048192 | bytes 8388608 | tf_op jit(solution)/shard_map/pallas_call | solution.py:56
  81.7 3.6 %collective-permute-start.17 = (f32[256,256]{1,0:T(8,128)S(1)}, f32[256,256]{1,0:T(8,128)S(1)}, u32[]{:S(2)}, u32[]{:S(2)}) collective-permute-start(f32[256,256]{1,0:T(8,128)S(1)} %get-tuple-element.60), channel_id=1, source_target_pairs={{0,128},{64,192},{128,0},{192,64},{1,129},{65,193},{129,1},{193,65... | collective-permute-start | bytes 786440 | tf_op jit(solution)/shard_map/ppermute | solution.py:39
  85.2 2.7 %collective-permute-done.37.refs_6_ = f32[224,256]{1,0:T(8,128)S(1)} collective-permute-done((f32[224,256]{1,0:T(8,128)S(1)}, f32[224,256]{1,0:T(8,128)S(1)}, u32[]{:S(2)}, u32[]{:S(2)}) %collective-permute-start.37) | collective-permute-done | bytes 229408 | tf_op jit(solution)/shard_map/ppermute | solution.py:39
  90.1 2.7 %collective-permute-start.47 = (f32[144,512]{1,0:T(8,128)S(1)}, f32[144,512]{1,0:T(8,128)S(1)}, u32[]{:S(2)}, u32[]{:S(2)}) collective-permute-start(f32[144,512]{1,0:T(8,128)S(1)} %get-tuple-element.85), channel_id=1, source_target_pairs={{0,48},{16,32},{32,16},{48,0},{1,49},{17,33},{33,17},{49,1},{2,50}... | collective-permute-start | bytes 884744 | tf_op jit(solution)/shard_map/ppermute | solution.py:39
  92.8 6.4 %collective-permute-done.17.refs_2_ = f32[256,256]{1,0:T(8,128)S(1)} collective-permute-done((f32[256,256]{1,0:T(8,128)S(1)}, f32[256,256]{1,0:T(8,128)S(1)}, u32[]{:S(2)}, u32[]{:S(2)}) %collective-permute-start.17) | collective-permute-done | bytes 262176 | tf_op jit(solution)/shard_map/ppermute | solution.py:39
  102.3 5.5 %collective-permute-done.47.refs_7_ = f32[144,512]{1,0:T(8,128)S(1)} collective-permute-done((f32[144,512]{1,0:T(8,128)S(1)}, f32[144,512]{1,0:T(8,128)S(1)}, u32[]{:S(2)}, u32[]{:S(2)}) %collective-permute-start.47) | collective-permute-done | bytes 294944 | tf_op jit(solution)/shard_map/ppermute | solution.py:39
  111.5 10.8 %collective-permute-done.44.refs_3_ = f32[144,512]{1,0:T(8,128)S(1)} collective-permute-done((f32[144,512]{1,0:T(8,128)S(1)}, f32[144,512]{1,0:T(8,128)S(1)}, u32[]{:S(2)}, u32[]{:S(2)}) %collective-permute-start.44) | collective-permute-done | bytes 294944 | tf_op jit(solution)/shard_map/ppermute | solution.py:39
  127.0 3.5 %collective-permute-done.49.refs_6_ = f32[144,256]{1,0:T(8,128)S(1)} collective-permute-done((f32[144,256]{1,0:T(8,128)S(1)}, f32[144,256]{1,0:T(8,128)S(1)}, u32[]{:S(2)}, u32[]{:S(2)}) %collective-permute-start.49) | collective-permute-done | bytes 147488 | tf_op jit(solution)/shard_map/ppermute | solution.py:39
  130.5 2.6 %collective-permute-done.50.refs_7_ = f32[144,256]{1,0:T(8,128)S(1)} collective-permute-done((f32[144,256]{1,0:T(8,128)S(1)}, f32[144,256]{1,0:T(8,128)S(1)}, u32[]{:S(2)}, u32[]{:S(2)}) %collective-permute-start.50) | collective-permute-done | bytes 147488 | tf_op jit(solution)/shard_map/ppermute | solution.py:39
  (102 shorter events, 44.8 us)
Async XLA Ops:
  1.8 12.5 %collective-permute-start.19 = (bf16[128,1024]{1,0:T(8,128)(2,1)S(1)}, bf16[128,1024]{1,0:T(8,128)(2,1)S(1)}, u32[]{:S(2)}, u32[]{:S(2)}) collective-permute-start(bf16[128,1024]{1,0:T(8,128)(2,1)S(1)} %shard_map.98.refs_0_), channel_id=1, source_target_pairs={{0,2},{2,4},{4,6},{6,8},{8,10},{10,12},{12,14},{14,0},{1,3},{3,5},... | collective-permute-start | bytes 786440 | tf_op jit(solution)/shard_map/ppermute | solution.py:44
  15.4 12.2 %collective-permute-start.20 = (bf16[128,1024]{1,0:T(8,128)(2,1)S(1)}, bf16[128,1024]{1,0:T(8,128)(2,1)S(1)}, u32[]{:S(2)}, u32[]{:S(2)}) collective-permute-start(bf16[128,1024]{1,0:T(8,128)(2,1)S(1)} %collective-permute-done.19.refs_2_), channel_id=1, source_target_pairs={{0,2},{2,4},{4,6},{6,8},{8,10},{10,12},{12,14},{14,0},{1,3},{3,5},... | collective-permute-start | bytes 786440 | tf_op jit(solution)/shard_map/ppermute | solution.py:44
  15.7 13.6 %collective-permute-start.24 = (bf16[128,1024]{1,0:T(8,128)(2,1)S(1)}, bf16[128,1024]{1,0:T(8,128)(2,1)S(1)}, u32[]{:S(2)}, u32[]{:S(2)}) collective-permute-start(bf16[128,1024]{1,0:T(8,128)(2,1)S(1)} %collective-permute-done.23.refs_4_), channel_id=1, source_target_pairs={{0,14},{2,0},{4,2},{6,4},{8,6},{10,8},{12,10},{14,12},{1,15},{3,1}... | collective-permute-start | bytes 786440 | tf_op jit(solution)/shard_map/ppermute | solution.py:44
  29.4 33.0 %collective-permute-start = (bf16[256,2048]{1,0:T(8,128)(2,1)S(1)}, bf16[256,2048]{1,0:T(8,128)(2,1)S(1)}, u32[]{:S(2)}, u32[]{:S(2)}) collective-permute-start(bf16[256,2048]{1,0:T(8,128)(2,1)S(1)} %shard_map.94), channel_id=1, source_target_pairs={{0,16},{16,0},{1,17},{17,1},{2,18},{18,2},{3,19},{19,3},{4,20},{20... | collective-permute-start | bytes 3145736 | tf_op jit(solution)/shard_map/ppermute | solution.py:39
  34.9 11.9 %collective-permute-start.25 = (bf16[128,1024]{1,0:T(8,128)(2,1)S(1)}, bf16[128,1024]{1,0:T(8,128)(2,1)S(1)}, u32[]{:S(2)}, u32[]{:S(2)}) collective-permute-start(bf16[128,1024]{1,0:T(8,128)(2,1)S(1)} %collective-permute-done.24.refs_8_), channel_id=1, source_target_pairs={{0,14},{2,0},{4,2},{6,4},{8,6},{10,8},{12,10},{14,12},{1,15},{3,1}... | collective-permute-start | bytes 786440 | tf_op jit(solution)/shard_map/ppermute | solution.py:44
  37.6 12.6 %collective-permute-start.32 = (bf16[128,1024]{1,0:T(8,128)(2,1)S(1)}, bf16[128,1024]{1,0:T(8,128)(2,1)S(1)}, u32[]{:S(2)}, u32[]{:S(2)}) collective-permute-start(bf16[128,1024]{1,0:T(8,128)(2,1)S(1)} %collective-permute-done.20.refs_6_), channel_id=1, source_target_pairs={{0,1},{1,0},{2,3},{3,2},{4,5},{5,4},{6,7},{7,6},{8,9},{9,8},{10,11... | collective-permute-start | bytes 786440 | tf_op jit(solution)/shard_map/ppermute | solution.py:39
  43.6 14.1 %collective-permute-start.3 = (bf16[144,1024]{1,0:T(8,128)(2,1)S(1)}, bf16[144,1024]{1,0:T(8,128)(2,1)S(1)}, u32[]{:S(2)}, u32[]{:S(2)}) collective-permute-start(bf16[144,1024]{1,0:T(8,128)(2,1)S(1)} %collective-permute-done.2.refs_6_), channel_id=1, source_target_pairs={{0,2},{2,4},{4,6},{6,8},{8,10},{10,12},{12,14},{14,0},{1,3},{3,5},... | collective-permute-start | bytes 884744 | tf_op jit(solution)/shard_map/ppermute | solution.py:44
  62.4 12.5 %collective-permute-start.12 = (bf16[144,1024]{1,0:T(8,128)(2,1)S(1)}, bf16[144,1024]{1,0:T(8,128)(2,1)S(1)}, u32[]{:S(2)}, u32[]{:S(2)}) collective-permute-start(bf16[144,1024]{1,0:T(8,128)(2,1)S(1)} %collective-permute-done.11.refs_8_), channel_id=1, source_target_pairs={{0,1},{1,0},{2,3},{3,2},{4,5},{5,4},{6,7},{7,6},{8,9},{9,8},{10,11... | collective-permute-start | bytes 884744 | tf_op jit(solution)/shard_map/ppermute | solution.py:39
  62.6 14.8 %collective-permute-start.13 = (bf16[144,1024]{1,0:T(8,128)(2,1)S(1)}, bf16[144,1024]{1,0:T(8,128)(2,1)S(1)}, u32[]{:S(2)}, u32[]{:S(2)}) collective-permute-start(bf16[144,1024]{1,0:T(8,128)(2,1)S(1)} %collective-permute-done.3.refs_10_), channel_id=1, source_target_pairs={{0,1},{1,0},{2,3},{3,2},{4,5},{5,4},{6,7},{7,6},{8,9},{9,8},{10,11... | collective-permute-start | bytes 884744 | tf_op jit(solution)/shard_map/ppermute | solution.py:39
  62.9 14.7 %collective-permute-start.15 = (bf16[144,1024]{1,0:T(8,128)(2,1)S(1)}, bf16[144,1024]{1,0:T(8,128)(2,1)S(1)}, u32[]{:S(2)}, u32[]{:S(2)}) collective-permute-start(bf16[144,1024]{1,0:T(8,128)(2,1)S(1)} %collective-permute-done.14.refs_12_), channel_id=1, source_target_pairs={{0,1},{1,0},{2,3},{3,2},{4,5},{5,4},{6,7},{7,6},{8,9},{9,8},{10,11... | collective-permute-start | bytes 884744 | tf_op jit(solution)/shard_map/ppermute | solution.py:39
  68.2 12.7 %collective-permute-start.5 = (bf16[144,1024]{1,0:T(8,128)(2,1)S(1)}, bf16[144,1024]{1,0:T(8,128)(2,1)S(1)}, u32[]{:S(2)}, u32[]{:S(2)}) collective-permute-start(bf16[144,1024]{1,0:T(8,128)(2,1)S(1)} %collective-permute-done.4.refs_0_), channel_id=1, source_target_pairs={{0,1},{1,0},{2,3},{3,2},{4,5},{5,4},{6,7},{7,6},{8,9},{9,8},{10,11... | collective-permute-start | bytes 884744 | tf_op jit(solution)/shard_map/ppermute | solution.py:39
  74.9 13.1 %collective-permute-start.37 = (f32[224,256]{1,0:T(8,128)S(1)}, f32[224,256]{1,0:T(8,128)S(1)}, u32[]{:S(2)}, u32[]{:S(2)}) collective-permute-start(f32[224,256]{1,0:T(8,128)S(1)} %get-tuple-element.72), channel_id=1, source_target_pairs={{0,128},{64,192},{128,0},{192,64},{1,129},{65,193},{129,1},{193,65... | collective-permute-start | bytes 688136 | tf_op jit(solution)/shard_map/ppermute | solution.py:39
  77.3 12.7 %collective-permute-start.38 = (f32[224,256]{1,0:T(8,128)S(1)}, f32[224,256]{1,0:T(8,128)S(1)}, u32[]{:S(2)}, u32[]{:S(2)}) collective-permute-start(f32[224,256]{1,0:T(8,128)S(1)} %get-tuple-element.73), channel_id=1, source_target_pairs={{0,192},{64,128},{128,64},{192,0},{1,193},{65,129},{129,65},{193,1... | collective-permute-start | bytes 688136 | tf_op jit(solution)/shard_map/ppermute | solution.py:39
  77.6 12.5 %collective-permute-start.45 = (f32[144,512]{1,0:T(8,128)S(1)}, f32[144,512]{1,0:T(8,128)S(1)}, u32[]{:S(2)}, u32[]{:S(2)}) collective-permute-start(f32[144,512]{1,0:T(8,128)S(1)} %get-tuple-element.83), channel_id=1, source_target_pairs={{0,32},{32,0},{1,33},{33,1},{2,34},{34,2},{3,35},{35,3},{4,36},{36... | collective-permute-start | bytes 884744 | tf_op jit(solution)/shard_map/ppermute | solution.py:39
  81.7 17.6 %collective-permute-start.17 = (f32[256,256]{1,0:T(8,128)S(1)}, f32[256,256]{1,0:T(8,128)S(1)}, u32[]{:S(2)}, u32[]{:S(2)}) collective-permute-start(f32[256,256]{1,0:T(8,128)S(1)} %get-tuple-element.60), channel_id=1, source_target_pairs={{0,128},{64,192},{128,0},{192,64},{1,129},{65,193},{129,1},{193,65... | collective-permute-start | bytes 786440 | tf_op jit(solution)/shard_map/ppermute | solution.py:39
  88.0 13.4 %collective-permute-start.18 = (f32[256,256]{1,0:T(8,128)S(1)}, f32[256,256]{1,0:T(8,128)S(1)}, u32[]{:S(2)}, u32[]{:S(2)}) collective-permute-start(f32[256,256]{1,0:T(8,128)S(1)} %get-tuple-element.61), channel_id=1, source_target_pairs={{0,192},{64,128},{128,64},{192,0},{1,193},{65,129},{129,65},{193,1... | collective-permute-start | bytes 786440 | tf_op jit(solution)/shard_map/ppermute | solution.py:39
  90.0 12.2 %collective-permute-start.46 = (f32[144,512]{1,0:T(8,128)S(1)}, f32[144,512]{1,0:T(8,128)S(1)}, u32[]{:S(2)}, u32[]{:S(2)}) collective-permute-start(f32[144,512]{1,0:T(8,128)S(1)} %get-tuple-element.84), channel_id=1, source_target_pairs={{0,16},{16,0},{1,17},{17,1},{2,18},{18,2},{3,19},{19,3},{4,20},{20... | collective-permute-start | bytes 884744 | tf_op jit(solution)/shard_map/ppermute | solution.py:39
  90.1 17.7 %collective-permute-start.47 = (f32[144,512]{1,0:T(8,128)S(1)}, f32[144,512]{1,0:T(8,128)S(1)}, u32[]{:S(2)}, u32[]{:S(2)}) collective-permute-start(f32[144,512]{1,0:T(8,128)S(1)} %get-tuple-element.85), channel_id=1, source_target_pairs={{0,48},{16,32},{32,16},{48,0},{1,49},{17,33},{33,17},{49,1},{2,50}... | collective-permute-start | bytes 884744 | tf_op jit(solution)/shard_map/ppermute | solution.py:39
  92.8 15.8 %collective-permute-start.42 = (f32[144,512]{1,0:T(8,128)S(1)}, f32[144,512]{1,0:T(8,128)S(1)}, u32[]{:S(2)}, u32[]{:S(2)}) collective-permute-start(f32[144,512]{1,0:T(8,128)S(1)} %get-tuple-element.79), channel_id=1, source_target_pairs={{0,32},{32,0},{1,33},{33,1},{2,34},{34,2},{3,35},{35,3},{4,36},{36... | collective-permute-start | bytes 884744 | tf_op jit(solution)/shard_map/ppermute | solution.py:39
  99.2 12.2 %collective-permute-start.43 = (f32[144,512]{1,0:T(8,128)S(1)}, f32[144,512]{1,0:T(8,128)S(1)}, u32[]{:S(2)}, u32[]{:S(2)}) collective-permute-start(f32[144,512]{1,0:T(8,128)S(1)} %get-tuple-element.80), channel_id=1, source_target_pairs={{0,16},{16,0},{1,17},{17,1},{2,18},{18,2},{3,19},{19,3},{4,20},{20... | collective-permute-start | bytes 884744 | tf_op jit(solution)/shard_map/ppermute | solution.py:39
  101.4 20.9 %collective-permute-start.44 = (f32[144,512]{1,0:T(8,128)S(1)}, f32[144,512]{1,0:T(8,128)S(1)}, u32[]{:S(2)}, u32[]{:S(2)}) collective-permute-start(f32[144,512]{1,0:T(8,128)S(1)} %get-tuple-element.81), channel_id=1, source_target_pairs={{0,48},{16,32},{32,16},{48,0},{1,49},{17,33},{33,17},{49,1},{2,50}... | collective-permute-start | bytes 884744 | tf_op jit(solution)/shard_map/ppermute | solution.py:39
  102.2 22.1 %collective-permute-start.39 = (f32[144,256]{1,0:T(8,128)S(1)}, f32[144,256]{1,0:T(8,128)S(1)}, u32[]{:S(2)}, u32[]{:S(2)}) collective-permute-start(f32[144,256]{1,0:T(8,128)S(1)} %get-tuple-element.75), channel_id=1, source_target_pairs={{0,32},{32,0},{1,33},{33,1},{2,34},{34,2},{3,35},{35,3},{4,36},{36... | collective-permute-start | bytes 442376 | tf_op jit(solution)/shard_map/ppermute | solution.py:39
  107.8 18.6 %collective-permute-start.40 = (f32[144,256]{1,0:T(8,128)S(1)}, f32[144,256]{1,0:T(8,128)S(1)}, u32[]{:S(2)}, u32[]{:S(2)}) collective-permute-start(f32[144,256]{1,0:T(8,128)S(1)} %get-tuple-element.76), channel_id=1, source_target_pairs={{0,16},{16,0},{1,17},{17,1},{2,18},{18,2},{3,19},{19,3},{4,20},{20... | collective-permute-start | bytes 442376 | tf_op jit(solution)/shard_map/ppermute | solution.py:39
  108.6 17.8 %collective-permute-start.41 = (f32[144,256]{1,0:T(8,128)S(1)}, f32[144,256]{1,0:T(8,128)S(1)}, u32[]{:S(2)}, u32[]{:S(2)}) collective-permute-start(f32[144,256]{1,0:T(8,128)S(1)} %get-tuple-element.77), channel_id=1, source_target_pairs={{0,48},{16,32},{32,16},{48,0},{1,49},{17,33},{33,17},{49,1},{2,50}... | collective-permute-start | bytes 442376 | tf_op jit(solution)/shard_map/ppermute | solution.py:39
  (32 other events, 321.9 us)

commit v8 on v5

--- a/solution.py
+++ b/solution.py
@@ -110,12 +110,12 @@
 
 
 def part_kernel(k, mine_ref, other_ref, *refs):
-    blocks, outs, refs = refs[:14], refs[14:22], refs[22:]
+    blocks, by_x_ref, by_y_ref, refs = refs[:14], refs[14], refs[15], refs[16:]
     if k == 0:
         gains_ref, refs = refs[0], refs[1:]
         for i, block in enumerate(blocks):
             gains_ref[source_of(i)] = block[128:144, :]
-    rows, result = refs
+    rows = refs[0]
 
     @pl.loop(0, 4)
     def _(j):
@@ -123,21 +123,12 @@
         for i, block in enumerate(blocks):
             rows[i * 128 : (i + 1) * 128, :] = block[:128, columns]
         right = rows[...]
-        result[:256, :] = jnp.dot(mine_ref[:, :1792], right, preferred_element_type=F32)
-        result[256:, :] = jnp.dot(other_ref[:, :1792], right, preferred_element_type=F32)
-        for at in range(4):
-
-            @pl.when(j == at)
-            def _():
-                outs[at][:BY_X, :] = result[:BY_X, :]
-                outs[at][BY_X : 2 * BY_X, :] = result[256 : 256 + BY_X, :]
-
-        to = pl.multiple_of(j * 128, 128)
-        for a in range(2):
+        to = pl.ds(pl.multiple_of(j * 128, 128), 128)
+        for a, left in enumerate((mine_ref, other_ref)):
+            result = jnp.dot(left[:, :1792], right, preferred_element_type=F32)
+            by_x_ref[j, a * BY_X : (a + 1) * BY_X, :] = result[:BY_X]
             for b in range(2):
-                outs[4 + a * 2 + b][:, pl.ds(to, 128)] = result[
-                    a * 256 + BY_X : a * 256 + 256, b * 128 : (b + 1) * 128
-                ]
+                by_y_ref[a * 2 + b, :, to] = result[BY_X:, b * 128 : (b + 1) * 128]
 
 
 def source_of(i):
@@ -146,7 +137,7 @@
 
 
 def product_kernel(k, mine_ref, other_ref, own_ref, swapped_ref, *refs):
-    parts, refs = refs[:8], refs[8:]
+    by_x_ref, by_y_ref, refs = refs[0], refs[1], refs[2:]
     if k == 0:
         gains_ref, refs = refs[0], refs[1:]
     outs = refs
@@ -156,11 +147,11 @@
         for a, left in enumerate((mine_ref, other_ref)):
             result = jnp.dot(left[:, 1792:], right, preferred_element_type=F32)
             at = slice(a * BY_X, (a + 1) * BY_X)
-            outs[j][at, :] = parts[j][at, :] + result[:BY_X]
+            outs[j][at, :] = by_x_ref[j, at, :] + result[:BY_X]
             for b in range(2):
                 to = slice(j * 128, (j + 1) * 128)
-                piece = 4 + a * 2 + b
-                outs[piece][:, to] = parts[piece][:, to] + result[BY_X:, b * 128 : (b + 1) * 128]
+                here = by_y_ref[a * 2 + b, :, to]
+                outs[4 + a * 2 + b][:, to] = here + result[BY_X:, b * 128 : (b + 1) * 128]
     if k == 0:
         late = [(source_of(14), own_ref[128:144, :].astype(F32)), (source_of(15), swapped_ref[128:144, :].astype(F32))]
         total = jnp.zeros((16, 1024), F32)
@@ -179,16 +170,15 @@
 
 def product(k, mine, other, blocks):
     pieces = [struct((BY_Y, 512), F32)] * 4
-    scratch = [pltpu.VMEM((1792, 256), BF16), pltpu.VMEM((512, 256), F32)]
     gains = [struct((16, 16, 1024), BF16)] if k == 0 else []
     parts = kernel_call(
         functools.partial(part_kernel, k),
         [VMEM] * 16,
-        [struct((2 * BY_X, 256), F32)] * 4 + pieces + gains,
+        [struct((4, 2 * BY_X, 256), F32), struct((4, BY_Y, 512), F32)] + gains,
         14,
         (2 * 512 * 1792 * 1024, 8 << 20),
         [mine, other, *blocks[:14]],
-        scratch,
+        [pltpu.VMEM((1792, 256), BF16)],
     )
     return kernel_call(
         functools.partial(product_kernel, k),

time: 133 us -> 133 us (level)
  no operation moved by 1% of the time
where the time goes in v8:
time: 133 us; the launch traced here: 132 us
  waiting for transfers between devices  64.5 us (48%)
  starting transfers between devices  54.6 us (41%)
  Pallas kernels  8.58 us (6%)
  other arithmetic  2.83 us (2%)
    ppermute x35, waiting for transfers between devices, swap(): return lax.ppermute(array, axis, [(i, i ^ mask) for i in range(size)])  39 us
    ppermute x35, starting transfers between devices, swap(): return lax.ppermute(array, axis, [(i, i ^ mask) for i in range(size)])  35.3 us
    ppermute x14, waiting for transfers between devices, shift(): lax.ppermute(array, 'z', [(i, (i + step) % size) for i in range(size)])  25.5 us
    ppermute x14, starting transfers between devices, shift(): lax.ppermute(array, 'z', [(i, (i + step) % size) for i in range(size)])  19.3 us
    pallas_call x11, Pallas kernels, kernel_call(): pl.pallas_call(kernel, in_specs=in_specs, out_specs=[VMEM] * len(out_shap...  8.58 us
    reduce_sum x1, other arithmetic, update_of(): jnp.sum(norm_grad.astype(F32) * normed.astype(F32), axis=1).reshape(64, 128)  2.83 us
  transfers between devices with their start and end apart: 49, of which 21 were waited for; matrix products, arithmetic and copies ran while one was open for 2% of the time, Pallas kernels for 6%

profile of v8, /device:TPU:1, one launch (start us, length us, event | category | flops | bytes accessed | tf_op | source)
XLA Modules:
  0.0 132.4 jit_solution(5505854066528928584)
XLA Ops:
  1.8 6.5 %collective-permute-start.19 = (bf16[128,1024]{1,0:T(8,128)(2,1)S(1)}, bf16[128,1024]{1,0:T(8,128)(2,1)S(1)}, u32[]{:S(2)}, u32[]{:S(2)}) collective-permute-start(bf16[128,1024]{1,0:T(8,128)(2,1)S(1)} %shard_map.98.refs_0_), channel_id=1, source_target_pairs={{0,14},{2,0},{4,2},{6,4},{8,6},{10,8},{12,10},{14,12},{1,15},{3,1}... | collective-permute-start | bytes 786440 | tf_op jit(solution)/shard_map/ppermute | solution.py:44
  9.2 2.8 %multiply_reduce_fusion = f32[8192]{0:T(1024)S(1)} fusion(bf16[1,128,8192]{2,1,0:T(8,128)(2,1)} %param.8, bf16[1,128,8192]{2,1,0:T(8,128)(2,1)} %param.9), kind=kLoop, calls=%fused_computation | loop fusion | flops 4186112 | bytes 4227072 | tf_op jit(solution)/shard_map/reduce_sum | solution.py:258
  13.2 3.4 %collective-permute-start.8 = (bf16[144,1024]{1,0:T(8,128)(2,1)S(1)}, bf16[144,1024]{1,0:T(8,128)(2,1)S(1)}, u32[]{:S(2)}, u32[]{:S(2)}) collective-permute-start(bf16[144,1024]{1,0:T(8,128)(2,1)S(1)} %shard_map.95.refs_0_), channel_id=1, source_target_pairs={{0,14},{2,0},{4,2},{6,4},{8,6},{10,8},{12,10},{14,12},{1,15},{3,1}... | collective-permute-start | bytes 884744 | tf_op jit(solution)/shard_map/ppermute | solution.py:44
  19.6 5.0 %collective-permute-done.1.refs_2_ = bf16[144,1024]{1,0:T(8,128)(2,1)S(1)} collective-permute-done((bf16[144,1024]{1,0:T(8,128)(2,1)S(1)}, bf16[144,1024]{1,0:T(8,128)(2,1)S(1)}, u32[]{:S(2)}, u32[]{:S(2)}) %collective-permute-start.1) | collective-permute-done | bytes 294944 | tf_op jit(solution)/shard_map/ppermute | solution.py:44
  27.1 2.4 %collective-permute-start.7 = (bf16[144,1024]{1,0:T(8,128)(2,1)S(1)}, bf16[144,1024]{1,0:T(8,128)(2,1)S(1)}, u32[]{:S(2)}, u32[]{:S(2)}) collective-permute-start(bf16[144,1024]{1,0:T(8,128)(2,1)S(1)} %collective-permute-done.1.refs_2_), channel_id=1, source_target_pairs={{0,1},{1,0},{2,3},{3,2},{4,5},{5,4},{6,7},{7,6},{8,9},{9,8},{10,11... | collective-permute-start | bytes 884744 | tf_op jit(solution)/shard_map/ppermute | solution.py:39
  29.9 3.0 %collective-permute-start = (bf16[256,2048]{1,0:T(8,128)(2,1)S(1)}, bf16[256,2048]{1,0:T(8,128)(2,1)S(1)}, u32[]{:S(2)}, u32[]{:S(2)}) collective-permute-start(bf16[256,2048]{1,0:T(8,128)(2,1)S(1)} %shard_map.94), channel_id=1, source_target_pairs={{0,16},{16,0},{1,17},{17,1},{2,18},{18,2},{3,19},{19,3},{4,20},{20... | collective-permute-start | bytes 3145736 | tf_op jit(solution)/shard_map/ppermute | solution.py:39
  36.6 4.3 %collective-permute-done.2.refs_6_ = bf16[144,1024]{1,0:T(8,128)(2,1)S(1)} collective-permute-done((bf16[144,1024]{1,0:T(8,128)(2,1)S(1)}, bf16[144,1024]{1,0:T(8,128)(2,1)S(1)}, u32[]{:S(2)}, u32[]{:S(2)}) %collective-permute-start.2) | collective-permute-done | bytes 294944 | tf_op jit(solution)/shard_map/ppermute | solution.py:44
  43.6 4.8 %collective-permute-done.21.refs_12_ = bf16[128,1024]{1,0:T(8,128)(2,1)S(1)} collective-permute-done((bf16[128,1024]{1,0:T(8,128)(2,1)S(1)}, bf16[128,1024]{1,0:T(8,128)(2,1)S(1)}, u32[]{:S(2)}, u32[]{:S(2)}) %collective-permute-start.21) | collective-permute-done | bytes 262176 | tf_op jit(solution)/shard_map/ppermute | solution.py:44
  48.3 3.4 %collective-permute-start.14 = (bf16[144,1024]{1,0:T(8,128)(2,1)S(1)}, bf16[144,1024]{1,0:T(8,128)(2,1)S(1)}, u32[]{:S(2)}, u32[]{:S(2)}) collective-permute-start(bf16[144,1024]{1,0:T(8,128)(2,1)S(1)} %collective-permute-done.11.refs_8_), channel_id=1, source_target_pairs={{0,14},{2,0},{4,2},{6,4},{8,6},{10,8},{12,10},{14,12},{1,15},{3,1}... | collective-permute-start | bytes 884744 | tf_op jit(solution)/shard_map/ppermute | solution.py:44
  51.7 2.7 %collective-permute-start.22 = (bf16[128,1024]{1,0:T(8,128)(2,1)S(1)}, bf16[128,1024]{1,0:T(8,128)(2,1)S(1)}, u32[]{:S(2)}, u32[]{:S(2)}) collective-permute-start(bf16[128,1024]{1,0:T(8,128)(2,1)S(1)} %collective-permute-done.21.refs_12_), channel_id=1, source_target_pairs={{0,14},{2,0},{4,2},{6,4},{8,6},{10,8},{12,10},{14,12},{1,15},{3,1}... | collective-permute-start | bytes 786440 | tf_op jit(solution)/shard_map/ppermute | solution.py:44
  54.4 5.0 %collective-permute-done.31.refs_10_ = bf16[128,1024]{1,0:T(8,128)(2,1)S(1)} collective-permute-done((bf16[128,1024]{1,0:T(8,128)(2,1)S(1)}, bf16[128,1024]{1,0:T(8,128)(2,1)S(1)}, u32[]{:S(2)}, u32[]{:S(2)}) %collective-permute-start.31) | collective-permute-done | bytes 262176 | tf_op jit(solution)/shard_map/ppermute | solution.py:44
  59.4 4.0 %collective-permute-start.32 = (bf16[128,1024]{1,0:T(8,128)(2,1)S(1)}, bf16[128,1024]{1,0:T(8,128)(2,1)S(1)}, u32[]{:S(2)}, u32[]{:S(2)}) collective-permute-start(bf16[128,1024]{1,0:T(8,128)(2,1)S(1)} %collective-permute-done.31.refs_10_), channel_id=1, source_target_pairs={{0,1},{1,0},{2,3},{3,2},{4,5},{5,4},{6,7},{7,6},{8,9},{9,8},{10,11... | collective-permute-start | bytes 786440 | tf_op jit(solution)/shard_map/ppermute | solution.py:39
  65.8 2.2 %collective-permute-start.15 = (bf16[144,1024]{1,0:T(8,128)(2,1)S(1)}, bf16[144,1024]{1,0:T(8,128)(2,1)S(1)}, u32[]{:S(2)}, u32[]{:S(2)}) collective-permute-start(bf16[144,1024]{1,0:T(8,128)(2,1)S(1)} %collective-permute-done.14.refs_12_), channel_id=1, source_target_pairs={{0,1},{1,0},{2,3},{3,2},{4,5},{5,4},{6,7},{7,6},{8,9},{9,8},{10,11... | collective-permute-start | bytes 884744 | tf_op jit(solution)/shard_map/ppermute | solution.py:39
  68.5 2.6 %shard_map.99 = (f32[4,224,256]{2,1,0:T(8,128)S(1)}, f32[4,144,512]{2,1,0:T(8,128)S(1)}) custom-call(bf16[256,2048]{1,0:T(8,128)(2,1)S(1)} %shard_map.93.mine_ref, bf16[256,2048]{1,0:T(8,128)(2,1)S(1)} %collective-permute-done.other_ref, bf16[128,1024]{1,0:T(8,128)(2,1)S(1)} %shard_map.98.refs_0_, bf16[128,1024]{1,0:T(8,128)(2,1)S(1)} %collective-permute-done.24.refs_1_, ...), custom_call_target="tpu_custom_call" | custom-call | flops 1879048192 | bytes 8388608 | tf_op jit(solution)/shard_map/pallas_call | solution.py:56
  72.9 2.5 %collective-permute-start.35 = (f32[224,256]{1,0:T(8,128)S(1)}, f32[224,256]{1,0:T(8,128)S(1)}, u32[]{:S(2)}, u32[]{:S(2)}) collective-permute-start(f32[224,256]{1,0:T(8,128)S(1)} %get-tuple-element.48), channel_id=1, source_target_pairs={{0,128},{64,192},{128,0},{192,64},{1,129},{65,193},{129,1},{193,65... | collective-permute-start | bytes 688136 | tf_op jit(solution)/shard_map/ppermute | solution.py:39
  76.1 2.6 %shard_map.96 = (f32[4,224,256]{2,1,0:T(8,128)S(1)}, f32[4,144,512]{2,1,0:T(8,128)S(1)}, bf16[16,16,1024]{2,1,0:T(8,128)(2,1)S(1)}) custom-call(bf16[256,2048]{1,0:T(8,128)(2,1)S(1)} %shard_map.93.mine_ref, bf16[256,2048]{1,0:T(8,128)(2,1)S(1)} %collective-permute-done.other_ref, bf16[144,1024]{1,0:T(8,128)(2,1)S(1)} %shard_map.95.refs_0_, ...), custom_call_target="tpu_custom_call" | custom-call | flops 1879048192 | bytes 8388608 | tf_op jit(solution)/shard_map/pallas_call | solution.py:56
  79.5 3.5 %collective-permute-start.17 = (f32[256,256]{1,0:T(8,128)S(1)}, f32[256,256]{1,0:T(8,128)S(1)}, u32[]{:S(2)}, u32[]{:S(2)}) collective-permute-start(f32[256,256]{1,0:T(8,128)S(1)} %get-tuple-element.42), channel_id=1, source_target_pairs={{0,128},{64,192},{128,0},{192,64},{1,129},{65,193},{129,1},{193,65... | collective-permute-start | bytes 786440 | tf_op jit(solution)/shard_map/ppermute | solution.py:39
  83.1 2.5 %collective-permute-done.35.refs_6_ = f32[224,256]{1,0:T(8,128)S(1)} collective-permute-done((f32[224,256]{1,0:T(8,128)S(1)}, f32[224,256]{1,0:T(8,128)S(1)}, u32[]{:S(2)}, u32[]{:S(2)}) %collective-permute-start.35) | collective-permute-done | bytes 229408 | tf_op jit(solution)/shard_map/ppermute | solution.py:39
  88.3 2.3 %collective-permute-start.45 = (f32[144,512]{1,0:T(8,128)S(1)}, f32[144,512]{1,0:T(8,128)S(1)}, u32[]{:S(2)}, u32[]{:S(2)}) collective-permute-start(f32[144,512]{1,0:T(8,128)S(1)} %get-tuple-element.61), channel_id=1, source_target_pairs={{0,48},{16,32},{32,16},{48,0},{1,49},{17,33},{33,17},{49,1},{2,50}... | collective-permute-start | bytes 884744 | tf_op jit(solution)/shard_map/ppermute | solution.py:39
  90.5 6.3 %collective-permute-done.17.refs_2_ = f32[256,256]{1,0:T(8,128)S(1)} collective-permute-done((f32[256,256]{1,0:T(8,128)S(1)}, f32[256,256]{1,0:T(8,128)S(1)}, u32[]{:S(2)}, u32[]{:S(2)}) %collective-permute-start.17) | collective-permute-done | bytes 262176 | tf_op jit(solution)/shard_map/ppermute | solution.py:39
  99.8 6.7 %collective-permute-done.45.refs_7_ = f32[144,512]{1,0:T(8,128)S(1)} collective-permute-done((f32[144,512]{1,0:T(8,128)S(1)}, f32[144,512]{1,0:T(8,128)S(1)}, u32[]{:S(2)}, u32[]{:S(2)}) %collective-permute-start.45) | collective-permute-done | bytes 294944 | tf_op jit(solution)/shard_map/ppermute | solution.py:39
  108.8 11.5 %collective-permute-done.42.refs_3_ = f32[144,512]{1,0:T(8,128)S(1)} collective-permute-done((f32[144,512]{1,0:T(8,128)S(1)}, f32[144,512]{1,0:T(8,128)S(1)}, u32[]{:S(2)}, u32[]{:S(2)}) %collective-permute-start.42) | collective-permute-done | bytes 294944 | tf_op jit(solution)/shard_map/ppermute | solution.py:39
  125.4 3.4 %collective-permute-done.47.refs_6_ = f32[144,256]{1,0:T(8,128)S(1)} collective-permute-done((f32[144,256]{1,0:T(8,128)S(1)}, f32[144,256]{1,0:T(8,128)S(1)}, u32[]{:S(2)}, u32[]{:S(2)}) %collective-permute-start.47) | collective-permute-done | bytes 147488 | tf_op jit(solution)/shard_map/ppermute | solution.py:39
  128.8 2.6 %collective-permute-done.48.refs_7_ = f32[144,256]{1,0:T(8,128)S(1)} collective-permute-done((f32[144,256]{1,0:T(8,128)S(1)}, f32[144,256]{1,0:T(8,128)S(1)}, u32[]{:S(2)}, u32[]{:S(2)}) %collective-permute-start.48) | collective-permute-done | bytes 147488 | tf_op jit(solution)/shard_map/ppermute | solution.py:39
  (96 shorter events, 35.4 us)
Async XLA Ops:
  1.8 11.5 %collective-permute-start.19 = (bf16[128,1024]{1,0:T(8,128)(2,1)S(1)}, bf16[128,1024]{1,0:T(8,128)(2,1)S(1)}, u32[]{:S(2)}, u32[]{:S(2)}) collective-permute-start(bf16[128,1024]{1,0:T(8,128)(2,1)S(1)} %shard_map.98.refs_0_), channel_id=1, source_target_pairs={{0,14},{2,0},{4,2},{6,4},{8,6},{10,8},{12,10},{14,12},{1,15},{3,1}... | collective-permute-start | bytes 786440 | tf_op jit(solution)/shard_map/ppermute | solution.py:44
  12.1 12.5 %collective-permute-start.1 = (bf16[144,1024]{1,0:T(8,128)(2,1)S(1)}, bf16[144,1024]{1,0:T(8,128)(2,1)S(1)}, u32[]{:S(2)}, u32[]{:S(2)}) collective-permute-start(bf16[144,1024]{1,0:T(8,128)(2,1)S(1)} %shard_map.95.refs_0_), channel_id=1, source_target_pairs={{0,2},{2,4},{4,6},{6,8},{8,10},{10,12},{12,14},{14,0},{1,3},{3,5},... | collective-permute-start | bytes 884744 | tf_op jit(solution)/shard_map/ppermute | solution.py:44
  12.2 13.2 %collective-permute-start.6 = (bf16[144,1024]{1,0:T(8,128)(2,1)S(1)}, bf16[144,1024]{1,0:T(8,128)(2,1)S(1)}, u32[]{:S(2)}, u32[]{:S(2)}) collective-permute-start(bf16[144,1024]{1,0:T(8,128)(2,1)S(1)} %shard_map.95.refs_0_), channel_id=1, source_target_pairs={{0,1},{1,0},{2,3},{3,2},{4,5},{5,4},{6,7},{7,6},{8,9},{9,8},{10,11... | collective-permute-start | bytes 884744 | tf_op jit(solution)/shard_map/ppermute | solution.py:39
  13.2 12.2 %collective-permute-start.8 = (bf16[144,1024]{1,0:T(8,128)(2,1)S(1)}, bf16[144,1024]{1,0:T(8,128)(2,1)S(1)}, u32[]{:S(2)}, u32[]{:S(2)}) collective-permute-start(bf16[144,1024]{1,0:T(8,128)(2,1)S(1)} %shard_map.95.refs_0_), channel_id=1, source_target_pairs={{0,14},{2,0},{4,2},{6,4},{8,6},{10,8},{12,10},{14,12},{1,15},{3,1}... | collective-permute-start | bytes 884744 | tf_op jit(solution)/shard_map/ppermute | solution.py:44
  18.3 11.6 %collective-permute-start.26 = (bf16[128,1024]{1,0:T(8,128)(2,1)S(1)}, bf16[128,1024]{1,0:T(8,128)(2,1)S(1)}, u32[]{:S(2)}, u32[]{:S(2)}) collective-permute-start(bf16[128,1024]{1,0:T(8,128)(2,1)S(1)} %collective-permute-done.25.refs_2_), channel_id=1, source_target_pairs={{0,1},{1,0},{2,3},{3,2},{4,5},{5,4},{6,7},{7,6},{8,9},{9,8},{10,11... | collective-permute-start | bytes 786440 | tf_op jit(solution)/shard_map/ppermute | solution.py:39
  25.5 15.4 %collective-permute-start.2 = (bf16[144,1024]{1,0:T(8,128)(2,1)S(1)}, bf16[144,1024]{1,0:T(8,128)(2,1)S(1)}, u32[]{:S(2)}, u32[]{:S(2)}) collective-permute-start(bf16[144,1024]{1,0:T(8,128)(2,1)S(1)} %collective-permute-done.1.refs_2_), channel_id=1, source_target_pairs={{0,2},{2,4},{4,6},{6,8},{8,10},{10,12},{12,14},{14,0},{1,3},{3,5},... | collective-permute-start | bytes 884744 | tf_op jit(solution)/shard_map/ppermute | solution.py:44
  27.1 13.8 %collective-permute-start.7 = (bf16[144,1024]{1,0:T(8,128)(2,1)S(1)}, bf16[144,1024]{1,0:T(8,128)(2,1)S(1)}, u32[]{:S(2)}, u32[]{:S(2)}) collective-permute-start(bf16[144,1024]{1,0:T(8,128)(2,1)S(1)} %collective-permute-done.1.refs_2_), channel_id=1, source_target_pairs={{0,1},{1,0},{2,3},{3,2},{4,5},{5,4},{6,7},{7,6},{8,9},{9,8},{10,11... | collective-permute-start | bytes 884744 | tf_op jit(solution)/shard_map/ppermute | solution.py:39
  29.9 34.7 %collective-permute-start = (bf16[256,2048]{1,0:T(8,128)(2,1)S(1)}, bf16[256,2048]{1,0:T(8,128)(2,1)S(1)}, u32[]{:S(2)}, u32[]{:S(2)}) collective-permute-start(bf16[256,2048]{1,0:T(8,128)(2,1)S(1)} %shard_map.94), channel_id=1, source_target_pairs={{0,16},{16,0},{1,17},{17,1},{2,18},{18,2},{3,19},{19,3},{4,20},{20... | collective-permute-start | bytes 3145736 | tf_op jit(solution)/shard_map/ppermute | solution.py:39
  42.7 11.7 %collective-permute-start.3 = (bf16[144,1024]{1,0:T(8,128)(2,1)S(1)}, bf16[144,1024]{1,0:T(8,128)(2,1)S(1)}, u32[]{:S(2)}, u32[]{:S(2)}) collective-permute-start(bf16[144,1024]{1,0:T(8,128)(2,1)S(1)} %collective-permute-done.2.refs_6_), channel_id=1, source_target_pairs={{0,2},{2,4},{4,6},{6,8},{8,10},{10,12},{12,14},{14,0},{1,3},{3,5},... | collective-permute-start | bytes 884744 | tf_op jit(solution)/shard_map/ppermute | solution.py:44
  48.3 15.2 %collective-permute-start.14 = (bf16[144,1024]{1,0:T(8,128)(2,1)S(1)}, bf16[144,1024]{1,0:T(8,128)(2,1)S(1)}, u32[]{:S(2)}, u32[]{:S(2)}) collective-permute-start(bf16[144,1024]{1,0:T(8,128)(2,1)S(1)} %collective-permute-done.11.refs_8_), channel_id=1, source_target_pairs={{0,14},{2,0},{4,2},{6,4},{8,6},{10,8},{12,10},{14,12},{1,15},{3,1}... | collective-permute-start | bytes 884744 | tf_op jit(solution)/shard_map/ppermute | solution.py:44
  51.7 11.8 %collective-permute-start.22 = (bf16[128,1024]{1,0:T(8,128)(2,1)S(1)}, bf16[128,1024]{1,0:T(8,128)(2,1)S(1)}, u32[]{:S(2)}, u32[]{:S(2)}) collective-permute-start(bf16[128,1024]{1,0:T(8,128)(2,1)S(1)} %collective-permute-done.21.refs_12_), channel_id=1, source_target_pairs={{0,14},{2,0},{4,2},{6,4},{8,6},{10,8},{12,10},{14,12},{1,15},{3,1}... | collective-permute-start | bytes 786440 | tf_op jit(solution)/shard_map/ppermute | solution.py:44
  72.9 12.7 %collective-permute-start.35 = (f32[224,256]{1,0:T(8,128)S(1)}, f32[224,256]{1,0:T(8,128)S(1)}, u32[]{:S(2)}, u32[]{:S(2)}) collective-permute-start(f32[224,256]{1,0:T(8,128)S(1)} %get-tuple-element.48), channel_id=1, source_target_pairs={{0,128},{64,192},{128,0},{192,64},{1,129},{65,193},{129,1},{193,65... | collective-permute-start | bytes 688136 | tf_op jit(solution)/shard_map/ppermute | solution.py:39
  75.4 12.4 %collective-permute-start.36 = (f32[224,256]{1,0:T(8,128)S(1)}, f32[224,256]{1,0:T(8,128)S(1)}, u32[]{:S(2)}, u32[]{:S(2)}) collective-permute-start(f32[224,256]{1,0:T(8,128)S(1)} %get-tuple-element.49), channel_id=1, source_target_pairs={{0,192},{64,128},{128,64},{192,0},{1,193},{65,129},{129,65},{193,1... | collective-permute-start | bytes 688136 | tf_op jit(solution)/shard_map/ppermute | solution.py:39
  75.6 12.7 %collective-permute-start.43 = (f32[144,512]{1,0:T(8,128)S(1)}, f32[144,512]{1,0:T(8,128)S(1)}, u32[]{:S(2)}, u32[]{:S(2)}) collective-permute-start(f32[144,512]{1,0:T(8,128)S(1)} %get-tuple-element.59), channel_id=1, source_target_pairs={{0,32},{32,0},{1,33},{33,1},{2,34},{34,2},{3,35},{35,3},{4,36},{36... | collective-permute-start | bytes 884744 | tf_op jit(solution)/shard_map/ppermute | solution.py:39
  79.5 17.3 %collective-permute-start.17 = (f32[256,256]{1,0:T(8,128)S(1)}, f32[256,256]{1,0:T(8,128)S(1)}, u32[]{:S(2)}, u32[]{:S(2)}) collective-permute-start(f32[256,256]{1,0:T(8,128)S(1)} %get-tuple-element.42), channel_id=1, source_target_pairs={{0,128},{64,192},{128,0},{192,64},{1,129},{65,193},{129,1},{193,65... | collective-permute-start | bytes 786440 | tf_op jit(solution)/shard_map/ppermute | solution.py:39
  85.6 12.9 %collective-permute-start.18 = (f32[256,256]{1,0:T(8,128)S(1)}, f32[256,256]{1,0:T(8,128)S(1)}, u32[]{:S(2)}, u32[]{:S(2)}) collective-permute-start(f32[256,256]{1,0:T(8,128)S(1)} %get-tuple-element.43), channel_id=1, source_target_pairs={{0,192},{64,128},{128,64},{192,0},{1,193},{65,129},{129,65},{193,1... | collective-permute-start | bytes 786440 | tf_op jit(solution)/shard_map/ppermute | solution.py:39
  87.7 12.0 %collective-permute-start.44 = (f32[144,512]{1,0:T(8,128)S(1)}, f32[144,512]{1,0:T(8,128)S(1)}, u32[]{:S(2)}, u32[]{:S(2)}) collective-permute-start(f32[144,512]{1,0:T(8,128)S(1)} %get-tuple-element.60), channel_id=1, source_target_pairs={{0,16},{16,0},{1,17},{17,1},{2,18},{18,2},{3,19},{19,3},{4,20},{20... | collective-permute-start | bytes 884744 | tf_op jit(solution)/shard_map/ppermute | solution.py:39
  88.3 18.3 %collective-permute-start.45 = (f32[144,512]{1,0:T(8,128)S(1)}, f32[144,512]{1,0:T(8,128)S(1)}, u32[]{:S(2)}, u32[]{:S(2)}) collective-permute-start(f32[144,512]{1,0:T(8,128)S(1)} %get-tuple-element.61), channel_id=1, source_target_pairs={{0,48},{16,32},{32,16},{48,0},{1,49},{17,33},{33,17},{49,1},{2,50}... | collective-permute-start | bytes 884744 | tf_op jit(solution)/shard_map/ppermute | solution.py:39
  90.5 16.6 %collective-permute-start.40 = (f32[144,512]{1,0:T(8,128)S(1)}, f32[144,512]{1,0:T(8,128)S(1)}, u32[]{:S(2)}, u32[]{:S(2)}) collective-permute-start(f32[144,512]{1,0:T(8,128)S(1)} %get-tuple-element.55), channel_id=1, source_target_pairs={{0,32},{32,0},{1,33},{33,1},{2,34},{34,2},{3,35},{35,3},{4,36},{36... | collective-permute-start | bytes 884744 | tf_op jit(solution)/shard_map/ppermute | solution.py:39
  96.9 11.9 %collective-permute-start.41 = (f32[144,512]{1,0:T(8,128)S(1)}, f32[144,512]{1,0:T(8,128)S(1)}, u32[]{:S(2)}, u32[]{:S(2)}) collective-permute-start(f32[144,512]{1,0:T(8,128)S(1)} %get-tuple-element.56), channel_id=1, source_target_pairs={{0,16},{16,0},{1,17},{17,1},{2,18},{18,2},{3,19},{19,3},{4,20},{20... | collective-permute-start | bytes 884744 | tf_op jit(solution)/shard_map/ppermute | solution.py:39
  98.5 21.8 %collective-permute-start.42 = (f32[144,512]{1,0:T(8,128)S(1)}, f32[144,512]{1,0:T(8,128)S(1)}, u32[]{:S(2)}, u32[]{:S(2)}) collective-permute-start(f32[144,512]{1,0:T(8,128)S(1)} %get-tuple-element.57), channel_id=1, source_target_pairs={{0,48},{16,32},{32,16},{48,0},{1,49},{17,33},{33,17},{49,1},{2,50}... | collective-permute-start | bytes 884744 | tf_op jit(solution)/shard_map/ppermute | solution.py:39
  99.7 22.5 %collective-permute-start.37 = (f32[144,256]{1,0:T(8,128)S(1)}, f32[144,256]{1,0:T(8,128)S(1)}, u32[]{:S(2)}, u32[]{:S(2)}) collective-permute-start(f32[144,256]{1,0:T(8,128)S(1)} %get-tuple-element.51), channel_id=1, source_target_pairs={{0,32},{32,0},{1,33},{33,1},{2,34},{34,2},{3,35},{35,3},{4,36},{36... | collective-permute-start | bytes 442376 | tf_op jit(solution)/shard_map/ppermute | solution.py:39
  106.6 17.9 %collective-permute-start.38 = (f32[144,256]{1,0:T(8,128)S(1)}, f32[144,256]{1,0:T(8,128)S(1)}, u32[]{:S(2)}, u32[]{:S(2)}) collective-permute-start(f32[144,256]{1,0:T(8,128)S(1)} %get-tuple-element.52), channel_id=1, source_target_pairs={{0,16},{16,0},{1,17},{17,1},{2,18},{18,2},{3,19},{19,3},{4,20},{20... | collective-permute-start | bytes 442376 | tf_op jit(solution)/shard_map/ppermute | solution.py:39
  107.1 17.3 %collective-permute-start.39 = (f32[144,256]{1,0:T(8,128)S(1)}, f32[144,256]{1,0:T(8,128)S(1)}, u32[]{:S(2)}, u32[]{:S(2)}) collective-permute-start(f32[144,256]{1,0:T(8,128)S(1)} %get-tuple-element.53), channel_id=1, source_target_pairs={{0,48},{16,32},{32,16},{48,0},{1,49},{17,33},{33,17},{49,1},{2,50}... | collective-permute-start | bytes 442376 | tf_op jit(solution)/shard_map/ppermute | solution.py:39
  (30 other events, 311.1 us)
